TPU v7x, 256 devices: a 4x2x16 block of a 4x16x16 slice. The times are simulated.
256 devices in a mesh: groups: 2 (over y), seq: 128 (over z, x, core).
Axes of the slice: x: 4, y: 2, z: 16, core: 2. Of those that a mesh axis runs over, the one named last changes fastest.
The devices are a block of a 4x16x16 slice.
Arguments:
- query_rows: bfloat16 [16384, 2048], P(('groups', 'seq')), parts along dimension 0, may hold values from -180 to 180
- key_rows: bfloat16 [16384, 512], P(('groups', 'seq')), parts along dimension 0, may hold values from -6 to 6
- value_rows: bfloat16 [16384, 512], P(('groups', 'seq')), parts along dimension 0, may hold values from -6 to 6
- positions: int32 [16384], P(('groups', 'seq')), parts along dimension 0, may hold values from 0 to 8191, as said below
- prompt_length: int32 [2], P('groups'), parts along dimension 0, may hold values from 4096 to 8192
- out_weight: bfloat16 [2048, 2048], replicated, may hold values from -0.125 to 0.125
- residual: bfloat16 [16384, 2048], P(('groups', 'seq')), parts along dimension 0, may hold values from -0.59765625 to 0.59765625
Outputs:
- layer_out: bfloat16 [16384, 2048], P(('groups', 'seq')), parts along dimension 0
There are 2 independent parts, one for each index of `groups`. A program takes and returns all parts, laid end to end along the dimension named above; an argument that names none is the same for every part. Nothing has to cross between parts.
Inputs may be any that keep to these rules, and one draw needn't show every extreme that they name: A permutation of 0 to 8191 in which each device's rows hold exactly one position of every run of 128 consecutive positions.
All inputs are finite; a program needn't handle non-finite values.
Results may differ from a plain program's by a relative error of at most 0.009.
Values may be sent and summed in bfloat16 or wider, within the bound.
No kernel may reach another device: no remote copies, remote signals or barrier semaphores. Data moves between devices by JAX's collectives and lax.ppermute only.
A program may use at most 128 MiB of HBM per device.

v0:
```python
import functools
import math
import jax
import jax.numpy as jnp
from jax import lax
from jax.experimental import pallas as pl
from jax.experimental.pallas import tpu as pltpu
from jax.sharding import PartitionSpec as P

HEADS = 16
KV_HEADS = 4
HEAD_DIM = 128
GROUP = HEADS // KV_HEADS
TOK = 64
RUN = 128
X_DEV = 4
CORES = 2
BLOCK = KV_HEADS
HALF = 32
KV_ROWS = 2 * TOK + 8
ROWS = 256
SCALE = HEAD_DIM ** -0.5 * math.log2(math.e)
NEVER = -1e30
LOWEST = -1e20
VMEM = pltpu.VMEM
F32 = jnp.float32
BF16 = jnp.bfloat16


def iota(shape, dim):
    return lax.broadcasted_iota(jnp.int32, shape, dim)


def prep_kernel(pos_ref, q_ref, k_ref, v_ref, qs_ref, kv_ref):
    pos = pos_ref[...]
    run = pos // RUN
    off = (pos - run * RUN).astype(F32)
    pick = (iota((TOK, TOK), 0) == jnp.broadcast_to(run, (TOK, TOK))).astype(F32)
    pick16 = pick.astype(BF16)
    off_col = jnp.dot(
        (pick * jnp.broadcast_to(off, (TOK, TOK))).astype(BF16),
        jnp.ones((TOK, HEAD_DIM), BF16),
        preferred_element_type=F32,
    )
    row = iota((TOK, HEAD_DIM), 0)
    lane = iota((TOK, HEAD_DIM), 1)
    lines = [
        jnp.sum(jnp.where(row == HALF * j + lane % HALF, off_col, 0.0), axis=0, keepdims=True)
        for j in range(TOK // HALF)
    ]
    table = jnp.concatenate(lines + [jnp.zeros((8 - len(lines), HEAD_DIM), F32)], axis=0).astype(BF16)
    sorted_q = jnp.dot(pick16, q_ref[...], preferred_element_type=F32).astype(BF16)
    sorted_k = jnp.dot(pick16, k_ref[...], preferred_element_type=F32).astype(BF16)
    sorted_v = jnp.dot(pick16, v_ref[...], preferred_element_type=F32).astype(BF16)
    off16 = off_col.astype(BF16)
    for h in range(KV_HEADS):
        cols = slice(h * HEAD_DIM, (h + 1) * HEAD_DIM)
        kv_ref[h, 0:TOK, :] = sorted_k[:, cols]
        kv_ref[h, TOK:2 * TOK, :] = sorted_v[:, cols]
        kv_ref[h, 2 * TOK:KV_ROWS, :] = table
        for g in range(GROUP):
            at = (h * GROUP + g) * HEAD_DIM
            qs_ref[h, g] = sorted_q[:, at:at + HEAD_DIM]
        qs_ref[h, GROUP] = off16


def prep(positions, query_rows, key_rows, value_rows):
    return pl.pallas_call(
        prep_kernel,
        out_shape=(
            jax.ShapeDtypeStruct((KV_HEADS, GROUP + 1, TOK, HEAD_DIM), BF16),
            jax.ShapeDtypeStruct((KV_HEADS, KV_ROWS, HEAD_DIM), BF16),
        ),
        in_specs=[pl.BlockSpec(memory_space=VMEM)] * 4,
        out_specs=(pl.BlockSpec(memory_space=VMEM),) * 2,
        compiler_params=pltpu.CompilerParams(vmem_limit_bytes=60 * 1024 * 1024),
        cost_estimate=pl.CostEstimate(flops=TOK * TOK * 3072 * 2, bytes_accessed=800_000, transcendentals=0),
        name="prep",
    )(positions.reshape(1, TOK), query_rows, key_rows, value_rows)


def attend_kernel(shards, first, last, *refs):
    limit_ref, qa_ref, qb_ref = refs[:3]
    kv_refs = refs[3:3 + shards]
    refs = refs[3 + shards:]
    if first:
        old_refs = None
    else:
        old_refs, refs = refs[:4], refs[4:]
    new_refs, (keys, vals) = refs[:-2], refs[-2:]
    limit = limit_ref[0]
    wide = shards * HEAD_DIM
    sources = KV_HEADS
    for j in range(2):
        for n, kv in enumerate(kv_refs):
            for s in range(sources):
                at = j * wide + (n * sources + s) * HALF
                keys[at:at + HALF, :] = kv[s, HALF * j:HALF * (j + 1), :]
                vals[at:at + HALF, 0:HEAD_DIM] = kv[s, TOK + HALF * j:TOK + HALF * (j + 1), :]
    vals[:, HEAD_DIM:] = jnp.ones((2 * wide, HEAD_DIM), BF16)
    lane8 = iota((8, HEAD_DIM), 1)
    tables = []
    for kv in kv_refs:
        table = kv[0, 2 * TOK:KV_ROWS, :].astype(F32)
        for s in range(1, sources):
            table = jnp.where(lane8 // HALF == s, kv[s, 2 * TOK:KV_ROWS, :].astype(F32), table)
        table = table + (lane8 % HALF * RUN).astype(F32)
        chunk = (iota((8, HEAD_DIM), 0) * (HALF * RUN)).astype(F32)
        tables.append(jnp.where(table + chunk >= limit.astype(F32), 1e9, table))
    ramp = (iota((HALF, HEAD_DIM), 0) * RUN).astype(F32)
    for half, q_ref in enumerate((qa_ref, qb_ref)):
        for i in range(2):
            for sp in range(2):
                b = i * 2 + sp
                rows_at = slice(HALF * i, HALF * (i + 1))
                q = q_ref[2 * sp:2 * sp + 2, 0:GROUP, rows_at, :].reshape(ROWS, HEAD_DIM)
                q_off = q_ref[2 * sp:2 * sp + 2, GROUP:GROUP + 1, rows_at, :].astype(F32)
                q_pos = jnp.broadcast_to(q_off + ramp[None, None], (2, GROUP, HALF, HEAD_DIM)).reshape(ROWS, HEAD_DIM)
                count = (i + 1) * wide
                s = lax.dot_general(
                    q, keys[0:count, :], (((1,), (1,)), ((), ())), preferred_element_type=F32
                ) * SCALE
                pieces = [s[:, c * HEAD_DIM:(c + 1) * HEAD_DIM] for c in range(count // HEAD_DIM)]
                for n in range(shards):
                    c = i * shards + n
                    pieces[c] = jnp.where(tables[n][i:i + 1, :] <= q_pos, pieces[c], NEVER)
                top = functools.reduce(jnp.maximum, pieces)
                top = jnp.max(top, axis=1, keepdims=True)
                if first:
                    new_max = jnp.broadcast_to(jnp.maximum(top, LOWEST), (ROWS, HEAD_DIM))
                else:
                    old_max = old_refs[2 * half][b]
                    new_max = jnp.maximum(old_max, top)
                weights = jnp.concatenate([jnp.exp2(piece - new_max).astype(BF16) for piece in pieces], axis=1)
                sums = jnp.dot(weights, vals[0:count, :], preferred_element_type=F32)
                if not first:
                    rescale = jnp.exp2(old_max - new_max)
                    sums = sums + old_refs[2 * half + 1][b] * jnp.concatenate([rescale, rescale], axis=1)
                if last and half == 1:
                    lane = iota((ROWS, HEAD_DIM), 1)
                    new_refs[2][b, :, 0:HEAD_DIM] = sums[:, 0:HEAD_DIM]
                    new_refs[2][b, :, HEAD_DIM:] = jnp.where(lane < HEAD_DIM // 2, new_max, sums[:, HEAD_DIM:])
                else:
                    new_refs[2 * half][b] = new_max
                    new_refs[2 * half + 1][b] = sums


def attend(limit, qa, qb, parts, state, last=False):
    shards = len(parts)
    wide = shards * HEAD_DIM
    stats = jax.ShapeDtypeStruct((4, ROWS, HEAD_DIM), F32)
    sums = jax.ShapeDtypeStruct((4, ROWS, 2 * HEAD_DIM), F32)
    shapes = (stats, sums, sums) if last else (stats, sums, stats, sums)
    first = state is None
    held = [] if first else list(state)
    score_count = 4 * 2 * ROWS * 3 * wide
    base = 3 + shards
    return pl.pallas_call(
        functools.partial(attend_kernel, shards, first, last),
        out_shape=shapes,
        in_specs=[pl.BlockSpec(memory_space=pltpu.SMEM)] + [pl.BlockSpec(memory_space=VMEM)] * (2 + shards + len(held)),
        out_specs=(pl.BlockSpec(memory_space=VMEM),) * len(shapes),
        scratch_shapes=[VMEM((2 * wide, HEAD_DIM), BF16), VMEM((2 * wide, 2 * HEAD_DIM), BF16)],
        input_output_aliases={} if first else ({base: 0, base + 1: 1, base + 3: 2} if last else {base + n: n for n in range(4)}),
        compiler_params=pltpu.CompilerParams(vmem_limit_bytes=16 * 1024 * 1024),
        cost_estimate=pl.CostEstimate(
            flops=score_count * HEAD_DIM * 6, bytes_accessed=4_000_000, transcendentals=score_count
        ),
        name="attend_last" if last else "attend",
    )(limit, qa, qb, *parts, *held)


def hold_kernel(weight_ref, held_ref, arrived):
    copy = pltpu.make_async_copy(weight_ref, held_ref, arrived)
    copy.start()
    copy.wait()


def hold(weight):
    return pl.pallas_call(
        hold_kernel,
        out_shape=jax.ShapeDtypeStruct(weight.shape, weight.dtype),
        in_specs=[pl.BlockSpec(memory_space=pl.ANY)],
        out_specs=pl.BlockSpec(memory_space=VMEM),
        scratch_shapes=[pltpu.SemaphoreType.DMA],
        compiler_params=pltpu.CompilerParams(vmem_limit_bytes=10 * 1024 * 1024),
        cost_estimate=pl.CostEstimate(flops=2_000_000_000, bytes_accessed=8_000_000, transcendentals=0),
        name="hold",
    )(weight)


def merge_kernel(max_ref, sum_ref, got_ref, out_ref):
    for i in range(2):
        for sp in range(2):
            b = i * 2 + sp
            max_a = max_ref[b]
            max_b = jnp.broadcast_to(got_ref[b, :, HEAD_DIM:HEAD_DIM + 1], (ROWS, HEAD_DIM))
            total_b = jnp.broadcast_to(got_ref[b, :, 2 * HEAD_DIM - 1:], (ROWS, HEAD_DIM))
            top = jnp.maximum(max_a, max_b)
            part_a = jnp.exp2(max_a - top)
            part_b = jnp.exp2(max_b - top)
            total = sum_ref[b, :, HEAD_DIM:] * part_a + total_b * part_b
            value = sum_ref[b, :, 0:HEAD_DIM] * part_a + got_ref[b, :, 0:HEAD_DIM] * part_b
            value = (value / total).astype(BF16).reshape(2, GROUP, HALF, HEAD_DIM)
            out_ref[2 * sp:2 * sp + 2, :, HALF * i:HALF * (i + 1), :] = value


def merge(maxima, sums, got):
    return pl.pallas_call(
        merge_kernel,
        out_shape=jax.ShapeDtypeStruct((KV_HEADS, GROUP, TOK, HEAD_DIM), BF16),
        in_specs=[pl.BlockSpec(memory_space=VMEM)] * 3,
        out_specs=pl.BlockSpec(memory_space=VMEM),
        compiler_params=pltpu.CompilerParams(vmem_limit_bytes=12 * 1024 * 1024),
        cost_estimate=pl.CostEstimate(flops=4_000_000, bytes_accessed=3_000_000, transcendentals=300_000),
        name="merge",
    )(maxima, sums, got)


def project_kernel(member_ref, pos_ref, *refs):
    parts = refs[:KV_HEADS]
    weight_ref, residual_ref, out_ref, heads = refs[KV_HEADS:]
    member = member_ref[0]
    for d, part in enumerate(parts):
        heads[lax.rem(member + d, KV_HEADS)] = part[...]
    run = pos_ref[...] // RUN
    put = (jnp.broadcast_to(run, (TOK, TOK)) == iota((TOK, TOK), 1)).astype(F32).astype(BF16)
    rows = jnp.concatenate([heads[h, g] for h in range(KV_HEADS) for g in range(GROUP)], axis=1)
    rows = jnp.dot(put, rows, preferred_element_type=F32).astype(BF16)
    wide = 512
    for n in range(weight_ref.shape[1] // wide):
        cols = slice(n * wide, (n + 1) * wide)
        total = jnp.dot(rows, weight_ref[:, cols], preferred_element_type=F32)
        out_ref[:, cols] = (total + residual_ref[:, cols].astype(F32)).astype(BF16)


def project(member, positions, parts, out_weight, residual):
    return pl.pallas_call(
        project_kernel,
        out_shape=jax.ShapeDtypeStruct(residual.shape, BF16),
        in_specs=[pl.BlockSpec(memory_space=pltpu.SMEM)] + [pl.BlockSpec(memory_space=VMEM)] * (len(parts) + 3),
        out_specs=pl.BlockSpec(memory_space=VMEM),
        scratch_shapes=[VMEM((KV_HEADS, GROUP, TOK, HEAD_DIM), BF16)],
        compiler_params=pltpu.CompilerParams(vmem_limit_bytes=12 * 1024 * 1024),
        cost_estimate=pl.CostEstimate(flops=TOK * 2048 * 4096, bytes_accessed=9_000_000, transcendentals=0),
        name="project",
    )(member, positions.reshape(TOK, 1), *parts, out_weight, residual)


def on_device(seq_size, query_rows, key_rows, value_rows, positions, prompt_length, out_weight, residual):
    z_dev = seq_size // (X_DEV * CORES)

    def at(z, x, c):
        return ((z % z_dev) * X_DEV + x % X_DEV) * CORES + c % CORES

    spots = [(z, x, c) for z in range(z_dev) for x in range(X_DEV) for c in range(CORES)]

    def move(a, dz=0, dx=0, dc=0):
        return lax.ppermute(a, "seq", [(at(z, x, c), at(z + dz, x + dx, c + dc)) for z, x, c in spots])

    def turn(a, d):
        return lax.ppermute(
            a, "seq", [(at(z, x, c), at(z // BLOCK * BLOCK + (z + d) % BLOCK, x, c)) for z, x, c in spots]
        )

    member = lax.rem(lax.axis_index("seq") // (X_DEV * CORES), BLOCK)

    def exchange(a):
        pick = [lax.dynamic_index_in_dim(a, lax.rem(member + d, BLOCK), 0, keepdims=False) for d in range(BLOCK)]
        return [pick[0]] + [turn(pick[d], d) for d in range(1, BLOCK)]

    qs, kvs = prep(positions, query_rows, key_rows, value_rows)
    own = jnp.stack(exchange(kvs))

    def spread(a):
        return [a, move(a, dx=1), move(a, dx=-1), move(a, dx=2)]

    ahead = move(own, dz=BLOCK)
    behind = move(own, dz=-BLOCK)
    across = move(own, dz=2 * BLOCK)
    group = spread(own)
    qs, own = lax.optimization_barrier((qs, own))
    qa = jnp.stack(exchange(qs))
    qb = move(qa, dc=1)
    state = attend(prompt_length, qa, qb, group, None)
    state, ahead, behind = lax.optimization_barrier((state, ahead, behind))
    next_group, group = spread(ahead), spread(behind)
    state = attend(prompt_length, qa, qb, next_group, state)
    state, across = lax.optimization_barrier((state, across))
    last_group = spread(across)
    state = attend(prompt_length, qa, qb, group, state)
    state = attend(prompt_length, qa, qb, last_group, state, last=True)
    got = move(state[2], dc=1)
    done = merge(state[0], state[1], got)
    parts = [done[0]] + [turn(done[d], -d) for d in range(1, BLOCK)]
    weight, done = lax.optimization_barrier((out_weight, done))
    weight = hold(weight)
    return project(member.reshape(1), positions, parts, weight, residual)


def solution(mesh):
    def step(*args):
        return on_device(mesh.shape["seq"], *args)

    return jax.shard_map(
        step,
        mesh=mesh,
        in_specs=(
            P(("groups", "seq"), None),
            P(("groups", "seq"), None),
            P(("groups", "seq"), None),
            P(("groups", "seq")),
            P("groups"),
            P(),
            P(("groups", "seq"), None),
        ),
        out_specs=P(("groups", "seq"), None),
        check_vma=False,
    )
```

profile of v0, /device:TPU:40, one launch (start us, length us, event | category | flops | bytes accessed | tf_op | source)
XLA Modules:
  0.0 120.8 jit_solution(16764833772599910859)
XLA Ops:
  0.0 2.0 %prep.1 = (bf16[4,5,64,128]{3,2,1,0:T(8,128)(2,1)}, bf16[4,136,128]{2,1,0:T(8,128)(2,1)}) custom-call(s32[1,64]{1,0:T(1,128)} %bitcast.35, bf16[64,2048]{1,0:T(8,128)(2,1)} %q_ref.1, bf16[64,512]{1,0:T(8,128)(2,1)} %k_ref.1, bf16[64,512]{1,0:T(8,128)(2,1)} %v_ref.1), custom_call_target="tpu_custom_call" | custom-call | flops 25165824 | bytes 800000 | tf_op jit(solution)/shard_map/prep/pallas_call | solution.py:68
  2.0 0.8 constant_dynamic-slice_fusion.1
  2.8 7.3 %collective-permute-start.2 = (bf16[136,128]{1,0:T(8,128)(2,1)S(1)}, bf16[136,128]{1,0:T(8,128)(2,1)S(1)}, u32[]{:S(2)}, u32[]{:S(2)}) collective-permute-start(bf16[136,128]{1,0:T(8,128)(2,1)S(1)} %get-tuple-element.74), channel_id=1, source_target_pairs={{0,24},{1,25},{2,26},{3,27},{4,28},{5,29},{6,30},{7,31},{8,0},{9,1... | collective-permute-start | bytes 104456 | tf_op jit(solution)/shard_map/ppermute | solution.py:262
  10.1 0.7 collective-permute-start
  10.8 0.9 collective-permute-done.2
  11.7 3.2 %collective-permute-done.1 = bf16[136,128]{1,0:T(8,128)(2,1)S(1)} collective-permute-done((bf16[136,128]{1,0:T(8,128)(2,1)S(1)}, bf16[136,128]{1,0:T(8,128)(2,1)S(1)}, u32[]{:S(2)}, u32[]{:S(2)}) %collective-permute-start.1) | collective-permute-done | bytes 34848 | tf_op jit(solution)/shard_map/ppermute | solution.py:262
  14.9 0.9 collective-permute-done
  15.9 1.0 constant_dynamic-slice_fusion
  16.9 0.7 collective-permute-start.5
  17.6 0.7 collective-permute-start.4
  18.3 1.9 %collective-permute-start.3 = (bf16[5,64,128]{2,1,0:T(8,128)(2,1)S(1)}, bf16[5,64,128]{2,1,0:T(8,128)(2,1)S(1)}, u32[]{:S(2)}, u32[]{:S(2)}) collective-permute-start(bf16[5,64,128]{2,1,0:T(8,128)(2,1)S(1)} %get-tuple-element.68), channel_id=1, source_target_pairs={{0,8},{1,9},{2,10},{3,11},{4,12},{5,13},{6,14},{7,15},{8,16},{9,17... | collective-permute-start | bytes 245768 | tf_op jit(solution)/shard_map/ppermute | solution.py:262
  20.2 2.4 %collective-permute-done.5 = bf16[5,64,128]{2,1,0:T(8,128)(2,1)S(1)} collective-permute-done((bf16[5,64,128]{2,1,0:T(8,128)(2,1)S(1)}, bf16[5,64,128]{2,1,0:T(8,128)(2,1)S(1)}, u32[]{:S(2)}, u32[]{:S(2)}) %collective-permute-start.5) | collective-permute-done | bytes 81952 | tf_op jit(solution)/shard_map/ppermute | solution.py:262
  22.5 3.3 %collective-permute-done.4 = bf16[5,64,128]{2,1,0:T(8,128)(2,1)S(1)} collective-permute-done((bf16[5,64,128]{2,1,0:T(8,128)(2,1)S(1)}, bf16[5,64,128]{2,1,0:T(8,128)(2,1)S(1)}, u32[]{:S(2)}, u32[]{:S(2)}) %collective-permute-start.4) | collective-permute-done | bytes 81952 | tf_op jit(solution)/shard_map/ppermute | solution.py:262
  25.8 0.0 collective-permute-done.3
  25.9 0.1 collective-permute-start.6
  26.0 3.4 %collective-permute-start.9 = (bf16[4,136,128]{2,1,0:T(8,128)(2,1)S(1)}, bf16[4,136,128]{2,1,0:T(8,128)(2,1)S(1)}, u32[]{:S(2)}, u32[]{:S(2)}) collective-permute-start(bf16[4,136,128]{2,1,0:T(8,128)(2,1)S(1)} %pad_maximum_fusion.1.refs_3_), channel_id=1, source_target_pairs={{0,4},{1,5},{2,6},{3,7},{4,0},{5,1},{6,2},{7,3},{8,12},{9,13},{10,... | collective-permute-start | bytes 417800 | tf_op jit(solution)/shard_map/ppermute | solution.py:259
  29.5 1.0 collective-permute-start.8
  30.5 1.0 collective-permute-start.7
  32.1 18.5 %collective-permute-start.11 = (bf16[4,136,128]{2,1,0:T(8,128)(2,1)S(1)}, bf16[4,136,128]{2,1,0:T(8,128)(2,1)S(1)}, u32[]{:S(2)}, u32[]{:S(2)}) collective-permute-start(bf16[4,136,128]{2,1,0:T(8,128)(2,1)S(1)} %pad_maximum_fusion.1.refs_3_), channel_id=1, source_target_pairs={{0,96},{1,97},{2,98},{3,99},{4,100},{5,101},{6,102},{7,103},{8,104... | collective-permute-start | bytes 417800 | tf_op jit(solution)/shard_map/ppermute | solution.py:259
  50.7 0.0 collective-permute-start.10
  50.7 0.0 collective-permute-done.8.refs_5_
  50.7 0.0 collective-permute-done.7.refs_4_
  50.7 4.0 %attend.3 = (f32[4,256,128]{2,1,0:T(8,128)S(1)}, f32[4,256,256]{2,1,0:T(8,128)S(1)}, f32[4,256,128]{2,1,0:T(8,128)S(1)}, f32[4,256,256]{2,1,0:T(8,128)}) custom-call(s32[1]{0:T(128)S(6)} %copy.31.refs_0_, bf16[4,5,64,128]{3,2,1,0:T(8,128)(2,1)S(1)} %pad_maximum_fusion.refs_1_, bf16[4,5,64,128]{3,2,1,0:T(8,128)(2,1)S(1)} %collective-permute-done.6.refs_2_, ...), custom_call_target="tpu_custom_call" | custom-call | flops 2415919104 | bytes 4000000 | tf_op jit(solution)/shard_map/attend/pallas_call | solution.py:158
  54.8 12.7 %collective-permute-done.10.refs_3_ = bf16[4,136,128]{2,1,0:T(8,128)(2,1)S(1)} collective-permute-done((bf16[4,136,128]{2,1,0:T(8,128)(2,1)S(1)}, bf16[4,136,128]{2,1,0:T(8,128)(2,1)S(1)}, u32[]{:S(2)}, u32[]{:S(2)}) %collective-permute-start.10) | collective-permute-done | bytes 139296 | tf_op jit(solution)/shard_map/ppermute | solution.py:259
  67.4 4.3 %collective-permute-start.13 = (bf16[4,136,128]{2,1,0:T(8,128)(2,1)S(1)}, bf16[4,136,128]{2,1,0:T(8,128)(2,1)S(1)}, u32[]{:S(2)}, u32[]{:S(2)}) collective-permute-start(bf16[4,136,128]{2,1,0:T(8,128)(2,1)S(1)} %collective-permute-done.10.refs_3_), channel_id=1, source_target_pairs={{0,6},{1,7},{2,0},{3,1},{4,2},{5,3},{6,4},{7,5},{8,14},{9,15},{10,... | collective-permute-start | bytes 417800 | tf_op jit(solution)/shard_map/ppermute | solution.py:259
  71.7 1.8 %collective-permute-start.21 = (bf16[4,136,128]{2,1,0:T(8,128)(2,1)S(1)}, bf16[4,136,128]{2,1,0:T(8,128)(2,1)S(1)}, u32[]{:S(2)}, u32[]{:S(2)}) collective-permute-start(bf16[4,136,128]{2,1,0:T(8,128)(2,1)S(1)} %collective-permute-done.11.refs_3_), channel_id=1, source_target_pairs={{0,4},{1,5},{2,6},{3,7},{4,0},{5,1},{6,2},{7,3},{8,12},{9,13},{10,... | collective-permute-start | bytes 417800 | tf_op jit(solution)/shard_map/ppermute | solution.py:259
  73.5 0.7 collective-permute-done.14.refs_6_
  74.2 4.4 %collective-permute-start.20 = (bf16[4,136,128]{2,1,0:T(8,128)(2,1)S(1)}, bf16[4,136,128]{2,1,0:T(8,128)(2,1)S(1)}, u32[]{:S(2)}, u32[]{:S(2)}) collective-permute-start(bf16[4,136,128]{2,1,0:T(8,128)(2,1)S(1)} %collective-permute-done.11.refs_3_), channel_id=1, source_target_pairs={{0,6},{1,7},{2,0},{3,1},{4,2},{5,3},{6,4},{7,5},{8,14},{9,15},{10,... | collective-permute-start | bytes 417800 | tf_op jit(solution)/shard_map/ppermute | solution.py:259
  78.6 0.3 collective-permute-done.13.refs_5_
  78.9 1.2 %collective-permute-start.19 = (bf16[4,136,128]{2,1,0:T(8,128)(2,1)S(1)}, bf16[4,136,128]{2,1,0:T(8,128)(2,1)S(1)}, u32[]{:S(2)}, u32[]{:S(2)}) collective-permute-start(bf16[4,136,128]{2,1,0:T(8,128)(2,1)S(1)} %collective-permute-done.11.refs_3_), channel_id=1, source_target_pairs={{0,2},{1,3},{2,4},{3,5},{4,6},{5,7},{6,0},{7,1},{8,10},{9,11},{10,... | collective-permute-start | bytes 417800 | tf_op jit(solution)/shard_map/ppermute | solution.py:259
  80.2 0.7 collective-permute-done.12.refs_4_
  80.9 5.8 %attend.4 = (f32[4,256,128]{2,1,0:T(8,128)S(1)}, f32[4,256,256]{2,1,0:T(8,128)S(1)}, f32[4,256,128]{2,1,0:T(8,128)S(1)}, f32[4,256,256]{2,1,0:T(8,128)}) custom-call(s32[1]{0:T(128)S(6)} %copy.31.refs_0_, bf16[4,5,64,128]{3,2,1,0:T(8,128)(2,1)S(1)} %pad_maximum_fusion.refs_1_, ...), custom_call_target="tpu_custom_call", output_to_operand_aliasing={{0}: (7, {}), {1}: (8, {}), {2}: (9, {}), {3}: (10, {})} | custom-call | flops 2415919104 | bytes 4000000 | tf_op jit(solution)/shard_map/attend/pallas_call | solution.py:158
  86.7 1.9 %collective-permute-done.15.refs_3_ = bf16[4,136,128]{2,1,0:T(8,128)(2,1)S(1)} collective-permute-done((bf16[4,136,128]{2,1,0:T(8,128)(2,1)S(1)}, bf16[4,136,128]{2,1,0:T(8,128)(2,1)S(1)}, u32[]{:S(2)}, u32[]{:S(2)}) %collective-permute-start.15) | collective-permute-done | bytes 139296 | tf_op jit(solution)/shard_map/ppermute | solution.py:259
  88.5 1.7 %collective-permute-start.18 = (bf16[4,136,128]{2,1,0:T(8,128)(2,1)S(1)}, bf16[4,136,128]{2,1,0:T(8,128)(2,1)S(1)}, u32[]{:S(2)}, u32[]{:S(2)}) collective-permute-start(bf16[4,136,128]{2,1,0:T(8,128)(2,1)S(1)} %collective-permute-done.15.refs_3_), channel_id=1, source_target_pairs={{0,4},{1,5},{2,6},{3,7},{4,0},{5,1},{6,2},{7,3},{8,12},{9,13},{10,... | collective-permute-start | bytes 417800 | tf_op jit(solution)/shard_map/ppermute | solution.py:259
  90.2 2.3 %collective-permute-start.17 = (bf16[4,136,128]{2,1,0:T(8,128)(2,1)S(1)}, bf16[4,136,128]{2,1,0:T(8,128)(2,1)S(1)}, u32[]{:S(2)}, u32[]{:S(2)}) collective-permute-start(bf16[4,136,128]{2,1,0:T(8,128)(2,1)S(1)} %collective-permute-done.15.refs_3_), channel_id=1, source_target_pairs={{0,6},{1,7},{2,0},{3,1},{4,2},{5,3},{6,4},{7,5},{8,14},{9,15},{10,... | collective-permute-start | bytes 417800 | tf_op jit(solution)/shard_map/ppermute | solution.py:259
  92.5 5.8 %attend.5 = (f32[4,256,128]{2,1,0:T(8,128)S(1)}, f32[4,256,256]{2,1,0:T(8,128)S(1)}, f32[4,256,128]{2,1,0:T(8,128)S(1)}, f32[4,256,256]{2,1,0:T(8,128)}) custom-call(s32[1]{0:T(128)S(6)} %copy.31.refs_0_, bf16[4,5,64,128]{3,2,1,0:T(8,128)(2,1)S(1)} %pad_maximum_fusion.refs_1_, ...), custom_call_target="tpu_custom_call", output_to_operand_aliasing={{0}: (7, {}), {1}: (8, {}), {2}: (9, {}), {3}: (10, {})} | custom-call | flops 2415919104 | bytes 4000000 | tf_op jit(solution)/shard_map/attend/pallas_call | solution.py:158
  98.3 0.5 collective-permute-done.16.refs_4_
  98.7 5.6 %attend_last.1 = (f32[4,256,128]{2,1,0:T(8,128)S(1)}, f32[4,256,256]{2,1,0:T(8,128)S(1)}, f32[4,256,256]{2,1,0:T(8,128)}) custom-call(s32[1]{0:T(128)S(6)} %copy.31.refs_0_, bf16[4,5,64,128]{3,2,1,0:T(8,128)(2,1)S(1)} %pad_maximum_fusion.refs_1_, ...), custom_call_target="tpu_custom_call", output_to_operand_aliasing={{0}: (7, {}), {1}: (8, {}), {2}: (10, {})} | custom-call | flops 2415919104 | bytes 4000000 | tf_op jit(solution)/shard_map/attend_last/pallas_call | solution.py:158
  104.4 0.1 copy.19.pos_ref
  104.5 2.8 %collective-permute-done.22.got_ref = f32[4,256,256]{2,1,0:T(8,128)S(1)} collective-permute-done((f32[4,256,256]{2,1,0:T(8,128)}, f32[4,256,256]{2,1,0:T(8,128)S(1)}, u32[]{:S(2)}, u32[]{:S(2)}) %collective-permute-start.22) | collective-permute-done | bytes 1048608 | tf_op jit(solution)/shard_map/ppermute | solution.py:259
  107.3 0.4 merge.1
  107.7 0.1 collective-permute-start.25
  107.8 3.4 %collective-permute-start.24 = (bf16[4,64,128]{2,1,0:T(8,128)(2,1)S(1)}, bf16[4,64,128]{2,1,0:T(8,128)(2,1)S(1)}, u32[]{:S(2)}, u32[]{:S(2)}) collective-permute-start(bf16[4,64,128]{2,1,0:T(8,128)(2,1)S(1)} %get-tuple-element.70), channel_id=1, source_target_pairs={{0,16},{1,17},{2,18},{3,19},{4,20},{5,21},{6,22},{7,23},{8,24},{9,... | collective-permute-start | bytes 196616 | tf_op jit(solution)/shard_map/ppermute | solution.py:262
  111.2 2.8 %collective-permute-start.23 = (bf16[4,64,128]{2,1,0:T(8,128)(2,1)S(1)}, bf16[4,64,128]{2,1,0:T(8,128)(2,1)S(1)}, u32[]{:S(2)}, u32[]{:S(2)}) collective-permute-start(bf16[4,64,128]{2,1,0:T(8,128)(2,1)S(1)} %get-tuple-element.71), channel_id=1, source_target_pairs={{0,24},{1,25},{2,26},{3,27},{4,28},{5,29},{6,30},{7,31},{8,0},{9,1... | collective-permute-start | bytes 196616 | tf_op jit(solution)/shard_map/ppermute | solution.py:262
  114.0 3.4 %copy-done = bf16[2048,2048]{1,0:T(8,128)(2,1)S(1)} copy-done((bf16[2048,2048]{1,0:T(8,128)(2,1)S(1)}, bf16[2048,2048]{1,0:T(8,128)(2,1)}, u32[]{:S(2)}) %copy-start) | copy-done | bytes 8388632
  117.4 0.6 hold.1.refs_4_
  118.0 0.3 copy-done.1
  118.3 2.5 %project.1 = bf16[64,2048]{1,0:T(8,128)(2,1)} custom-call(s32[1]{0:T(128)} %bitcast.member_ref, s32[64,1]{1,0:T(8,128)S(1)} %copy.19.pos_ref, bf16[4,64,128]{2,1,0:T(8,128)(2,1)S(1)} %get-tuple-element.72.refs_0_, bf16[4,64,128]{2,1,0:T(8,128)(2,1)S(1)} %collective-permute-done.23.refs_1_, bf16[4,64,128]{2,1,0:T(8,128)(2,1)S(1)} %collective-permute-done.24.refs_2_, ...), custom_call_target="tpu_custom_call" | custom-call | flops 536870912 | bytes 9000000 | tf_op jit(solution)/shard_map/project/pallas_call | solution.py:238
  (24 shorter events, 0.1 us)
Async XLA Ops:
  2.8 8.9 %collective-permute-start.2 = (bf16[136,128]{1,0:T(8,128)(2,1)S(1)}, bf16[136,128]{1,0:T(8,128)(2,1)S(1)}, u32[]{:S(2)}, u32[]{:S(2)}) collective-permute-start(bf16[136,128]{1,0:T(8,128)(2,1)S(1)} %get-tuple-element.74), channel_id=1, source_target_pairs={{0,24},{1,25},{2,26},{3,27},{4,28},{5,29},{6,30},{7,31},{8,0},{9,1... | collective-permute-start | bytes 104456 | tf_op jit(solution)/shard_map/ppermute | solution.py:262
  10.1 4.8 %collective-permute-start.1 = (bf16[136,128]{1,0:T(8,128)(2,1)S(1)}, bf16[136,128]{1,0:T(8,128)(2,1)S(1)}, u32[]{:S(2)}, u32[]{:S(2)}) collective-permute-start(bf16[136,128]{1,0:T(8,128)(2,1)S(1)} %get-tuple-element.75), channel_id=1, source_target_pairs={{0,16},{1,17},{2,18},{3,19},{4,20},{5,21},{6,22},{7,23},{8,24},{9,... | collective-permute-start | bytes 104456 | tf_op jit(solution)/shard_map/ppermute | solution.py:262
  10.1 5.7 %collective-permute-start = (bf16[136,128]{1,0:T(8,128)(2,1)S(1)}, bf16[136,128]{1,0:T(8,128)(2,1)S(1)}, u32[]{:S(2)}, u32[]{:S(2)}) collective-permute-start(bf16[136,128]{1,0:T(8,128)(2,1)S(1)} %get-tuple-element.76), channel_id=1, source_target_pairs={{0,8},{1,9},{2,10},{3,11},{4,12},{5,13},{6,14},{7,15},{8,16},{9,17... | collective-permute-start | bytes 104456 | tf_op jit(solution)/shard_map/ppermute | solution.py:262
  16.9 5.6 %collective-permute-start.5 = (bf16[5,64,128]{2,1,0:T(8,128)(2,1)S(1)}, bf16[5,64,128]{2,1,0:T(8,128)(2,1)S(1)}, u32[]{:S(2)}, u32[]{:S(2)}) collective-permute-start(bf16[5,64,128]{2,1,0:T(8,128)(2,1)S(1)} %get-tuple-element.66), channel_id=1, source_target_pairs={{0,24},{1,25},{2,26},{3,27},{4,28},{5,29},{6,30},{7,31},{8,0},{9,1... | collective-permute-start | bytes 245768 | tf_op jit(solution)/shard_map/ppermute | solution.py:262
  17.6 8.3 %collective-permute-start.4 = (bf16[5,64,128]{2,1,0:T(8,128)(2,1)S(1)}, bf16[5,64,128]{2,1,0:T(8,128)(2,1)S(1)}, u32[]{:S(2)}, u32[]{:S(2)}) collective-permute-start(bf16[5,64,128]{2,1,0:T(8,128)(2,1)S(1)} %get-tuple-element.67), channel_id=1, source_target_pairs={{0,16},{1,17},{2,18},{3,19},{4,20},{5,21},{6,22},{7,23},{8,24},{9,... | collective-permute-start | bytes 245768 | tf_op jit(solution)/shard_map/ppermute | solution.py:262
  18.3 7.5 %collective-permute-start.3 = (bf16[5,64,128]{2,1,0:T(8,128)(2,1)S(1)}, bf16[5,64,128]{2,1,0:T(8,128)(2,1)S(1)}, u32[]{:S(2)}, u32[]{:S(2)}) collective-permute-start(bf16[5,64,128]{2,1,0:T(8,128)(2,1)S(1)} %get-tuple-element.68), channel_id=1, source_target_pairs={{0,8},{1,9},{2,10},{3,11},{4,12},{5,13},{6,14},{7,15},{8,16},{9,17... | collective-permute-start | bytes 245768 | tf_op jit(solution)/shard_map/ppermute | solution.py:262
  25.9 24.8 %collective-permute-start.6 = (bf16[4,5,64,128]{3,2,1,0:T(8,128)(2,1)S(1)}, bf16[4,5,64,128]{3,2,1,0:T(8,128)(2,1)S(1)}, u32[]{:S(2)}, u32[]{:S(2)}) collective-permute-start(bf16[4,5,64,128]{3,2,1,0:T(8,128)(2,1)S(1)} %pad_maximum_fusion.refs_1_), channel_id=1, source_target_pairs={{0,1},{1,0},{2,3},{3,2},{4,5},{5,4},{6,7},{7,6},{8,9},{9,8},{10,11... | collective-permute-start | bytes 983048 | tf_op jit(solution)/shard_map/ppermute | solution.py:259
  26.0 24.6 %collective-permute-start.9 = (bf16[4,136,128]{2,1,0:T(8,128)(2,1)S(1)}, bf16[4,136,128]{2,1,0:T(8,128)(2,1)S(1)}, u32[]{:S(2)}, u32[]{:S(2)}) collective-permute-start(bf16[4,136,128]{2,1,0:T(8,128)(2,1)S(1)} %pad_maximum_fusion.1.refs_3_), channel_id=1, source_target_pairs={{0,4},{1,5},{2,6},{3,7},{4,0},{5,1},{6,2},{7,3},{8,12},{9,13},{10,... | collective-permute-start | bytes 417800 | tf_op jit(solution)/shard_map/ppermute | solution.py:259
  29.5 21.2 %collective-permute-start.8 = (bf16[4,136,128]{2,1,0:T(8,128)(2,1)S(1)}, bf16[4,136,128]{2,1,0:T(8,128)(2,1)S(1)}, u32[]{:S(2)}, u32[]{:S(2)}) collective-permute-start(bf16[4,136,128]{2,1,0:T(8,128)(2,1)S(1)} %pad_maximum_fusion.1.refs_3_), channel_id=1, source_target_pairs={{0,6},{1,7},{2,0},{3,1},{4,2},{5,3},{6,4},{7,5},{8,14},{9,15},{10,... | collective-permute-start | bytes 417800 | tf_op jit(solution)/shard_map/ppermute | solution.py:259
  30.5 20.2 %collective-permute-start.7 = (bf16[4,136,128]{2,1,0:T(8,128)(2,1)S(1)}, bf16[4,136,128]{2,1,0:T(8,128)(2,1)S(1)}, u32[]{:S(2)}, u32[]{:S(2)}) collective-permute-start(bf16[4,136,128]{2,1,0:T(8,128)(2,1)S(1)} %pad_maximum_fusion.1.refs_3_), channel_id=1, source_target_pairs={{0,2},{1,3},{2,4},{3,5},{4,6},{5,7},{6,0},{7,1},{8,10},{9,11},{10,... | collective-permute-start | bytes 417800 | tf_op jit(solution)/shard_map/ppermute | solution.py:259
  32.1 22.6 %collective-permute-start.11 = (bf16[4,136,128]{2,1,0:T(8,128)(2,1)S(1)}, bf16[4,136,128]{2,1,0:T(8,128)(2,1)S(1)}, u32[]{:S(2)}, u32[]{:S(2)}) collective-permute-start(bf16[4,136,128]{2,1,0:T(8,128)(2,1)S(1)} %pad_maximum_fusion.1.refs_3_), channel_id=1, source_target_pairs={{0,96},{1,97},{2,98},{3,99},{4,100},{5,101},{6,102},{7,103},{8,104... | collective-permute-start | bytes 417800 | tf_op jit(solution)/shard_map/ppermute | solution.py:259
  50.7 16.7 %collective-permute-start.10 = (bf16[4,136,128]{2,1,0:T(8,128)(2,1)S(1)}, bf16[4,136,128]{2,1,0:T(8,128)(2,1)S(1)}, u32[]{:S(2)}, u32[]{:S(2)}) collective-permute-start(bf16[4,136,128]{2,1,0:T(8,128)(2,1)S(1)} %pad_maximum_fusion.1.refs_3_), channel_id=1, source_target_pairs={{0,32},{1,33},{2,34},{3,35},{4,36},{5,37},{6,38},{7,39},{8,40},{9,... | collective-permute-start | bytes 417800 | tf_op jit(solution)/shard_map/ppermute | solution.py:259
  67.4 6.8 %collective-permute-start.14 = (bf16[4,136,128]{2,1,0:T(8,128)(2,1)S(1)}, bf16[4,136,128]{2,1,0:T(8,128)(2,1)S(1)}, u32[]{:S(2)}, u32[]{:S(2)}) collective-permute-start(bf16[4,136,128]{2,1,0:T(8,128)(2,1)S(1)} %collective-permute-done.10.refs_3_), channel_id=1, source_target_pairs={{0,4},{1,5},{2,6},{3,7},{4,0},{5,1},{6,2},{7,3},{8,12},{9,13},{10,... | collective-permute-start | bytes 417800 | tf_op jit(solution)/shard_map/ppermute | solution.py:259
  67.4 11.5 %collective-permute-start.13 = (bf16[4,136,128]{2,1,0:T(8,128)(2,1)S(1)}, bf16[4,136,128]{2,1,0:T(8,128)(2,1)S(1)}, u32[]{:S(2)}, u32[]{:S(2)}) collective-permute-start(bf16[4,136,128]{2,1,0:T(8,128)(2,1)S(1)} %collective-permute-done.10.refs_3_), channel_id=1, source_target_pairs={{0,6},{1,7},{2,0},{3,1},{4,2},{5,3},{6,4},{7,5},{8,14},{9,15},{10,... | collective-permute-start | bytes 417800 | tf_op jit(solution)/shard_map/ppermute | solution.py:259
  71.7 9.2 %collective-permute-start.12 = (bf16[4,136,128]{2,1,0:T(8,128)(2,1)S(1)}, bf16[4,136,128]{2,1,0:T(8,128)(2,1)S(1)}, u32[]{:S(2)}, u32[]{:S(2)}) collective-permute-start(bf16[4,136,128]{2,1,0:T(8,128)(2,1)S(1)} %collective-permute-done.10.refs_3_), channel_id=1, source_target_pairs={{0,2},{1,3},{2,4},{3,5},{4,6},{5,7},{6,0},{7,1},{8,10},{9,11},{10,... | collective-permute-start | bytes 417800 | tf_op jit(solution)/shard_map/ppermute | solution.py:259
  71.7 16.8 %collective-permute-start.15 = (bf16[4,136,128]{2,1,0:T(8,128)(2,1)S(1)}, bf16[4,136,128]{2,1,0:T(8,128)(2,1)S(1)}, u32[]{:S(2)}, u32[]{:S(2)}) collective-permute-start(bf16[4,136,128]{2,1,0:T(8,128)(2,1)S(1)} %pad_maximum_fusion.1.refs_3_), channel_id=1, source_target_pairs={{0,64},{1,65},{2,66},{3,67},{4,68},{5,69},{6,70},{7,71},{8,72},{9,... | collective-permute-start | bytes 417800 | tf_op jit(solution)/shard_map/ppermute | solution.py:259
  71.7 20.7 %collective-permute-start.21 = (bf16[4,136,128]{2,1,0:T(8,128)(2,1)S(1)}, bf16[4,136,128]{2,1,0:T(8,128)(2,1)S(1)}, u32[]{:S(2)}, u32[]{:S(2)}) collective-permute-start(bf16[4,136,128]{2,1,0:T(8,128)(2,1)S(1)} %collective-permute-done.11.refs_3_), channel_id=1, source_target_pairs={{0,4},{1,5},{2,6},{3,7},{4,0},{5,1},{6,2},{7,3},{8,12},{9,13},{10,... | collective-permute-start | bytes 417800 | tf_op jit(solution)/shard_map/ppermute | solution.py:259
  74.2 18.3 %collective-permute-start.20 = (bf16[4,136,128]{2,1,0:T(8,128)(2,1)S(1)}, bf16[4,136,128]{2,1,0:T(8,128)(2,1)S(1)}, u32[]{:S(2)}, u32[]{:S(2)}) collective-permute-start(bf16[4,136,128]{2,1,0:T(8,128)(2,1)S(1)} %collective-permute-done.11.refs_3_), channel_id=1, source_target_pairs={{0,6},{1,7},{2,0},{3,1},{4,2},{5,3},{6,4},{7,5},{8,14},{9,15},{10,... | collective-permute-start | bytes 417800 | tf_op jit(solution)/shard_map/ppermute | solution.py:259
  78.9 13.5 %collective-permute-start.19 = (bf16[4,136,128]{2,1,0:T(8,128)(2,1)S(1)}, bf16[4,136,128]{2,1,0:T(8,128)(2,1)S(1)}, u32[]{:S(2)}, u32[]{:S(2)}) collective-permute-start(bf16[4,136,128]{2,1,0:T(8,128)(2,1)S(1)} %collective-permute-done.11.refs_3_), channel_id=1, source_target_pairs={{0,2},{1,3},{2,4},{3,5},{4,6},{5,7},{6,0},{7,1},{8,10},{9,11},{10,... | collective-permute-start | bytes 417800 | tf_op jit(solution)/shard_map/ppermute | solution.py:259
  88.5 15.8 %copy-start.2 = (s32[64]{0:T(128)S(1)}, s32[64]{0:T(128)}, u32[]{:S(2)}) copy-start(s32[64]{0:T(128)} %param.10) | copy-start | bytes 772
  88.5 9.7 %collective-permute-start.18 = (bf16[4,136,128]{2,1,0:T(8,128)(2,1)S(1)}, bf16[4,136,128]{2,1,0:T(8,128)(2,1)S(1)}, u32[]{:S(2)}, u32[]{:S(2)}) collective-permute-start(bf16[4,136,128]{2,1,0:T(8,128)(2,1)S(1)} %collective-permute-done.15.refs_3_), channel_id=1, source_target_pairs={{0,4},{1,5},{2,6},{3,7},{4,0},{5,1},{6,2},{7,3},{8,12},{9,13},{10,... | collective-permute-start | bytes 417800 | tf_op jit(solution)/shard_map/ppermute | solution.py:259
  90.2 8.1 %collective-permute-start.17 = (bf16[4,136,128]{2,1,0:T(8,128)(2,1)S(1)}, bf16[4,136,128]{2,1,0:T(8,128)(2,1)S(1)}, u32[]{:S(2)}, u32[]{:S(2)}) collective-permute-start(bf16[4,136,128]{2,1,0:T(8,128)(2,1)S(1)} %collective-permute-done.15.refs_3_), channel_id=1, source_target_pairs={{0,6},{1,7},{2,0},{3,1},{4,2},{5,3},{6,4},{7,5},{8,14},{9,15},{10,... | collective-permute-start | bytes 417800 | tf_op jit(solution)/shard_map/ppermute | solution.py:259
  92.5 6.3 %collective-permute-start.16 = (bf16[4,136,128]{2,1,0:T(8,128)(2,1)S(1)}, bf16[4,136,128]{2,1,0:T(8,128)(2,1)S(1)}, u32[]{:S(2)}, u32[]{:S(2)}) collective-permute-start(bf16[4,136,128]{2,1,0:T(8,128)(2,1)S(1)} %collective-permute-done.15.refs_3_), channel_id=1, source_target_pairs={{0,2},{1,3},{2,4},{3,5},{4,6},{5,7},{6,0},{7,1},{8,10},{9,11},{10,... | collective-permute-start | bytes 417800 | tf_op jit(solution)/shard_map/ppermute | solution.py:259
  104.4 2.9 %collective-permute-start.22 = (f32[4,256,256]{2,1,0:T(8,128)}, f32[4,256,256]{2,1,0:T(8,128)S(1)}, u32[]{:S(2)}, u32[]{:S(2)}) collective-permute-start(f32[4,256,256]{2,1,0:T(8,128)} %get-tuple-element.63), channel_id=1, source_target_pairs={{0,1},{1,0},{2,3},{3,2},{4,5},{5,4},{6,7},{7,6},{8,9},{9,8},{10,11... | collective-permute-start | bytes 3145736 | tf_op jit(solution)/shard_map/ppermute | solution.py:259
  107.7 10.3 %collective-permute-start.25 = (bf16[4,64,128]{2,1,0:T(8,128)(2,1)S(1)}, bf16[4,64,128]{2,1,0:T(8,128)(2,1)S(1)}, u32[]{:S(2)}, u32[]{:S(2)}) collective-permute-start(bf16[4,64,128]{2,1,0:T(8,128)(2,1)S(1)} %get-tuple-element.69), channel_id=1, source_target_pairs={{0,8},{1,9},{2,10},{3,11},{4,12},{5,13},{6,14},{7,15},{8,16},{9,17... | collective-permute-start | bytes 196616 | tf_op jit(solution)/shard_map/ppermute | solution.py:262
  107.8 10.2 %collective-permute-start.24 = (bf16[4,64,128]{2,1,0:T(8,128)(2,1)S(1)}, bf16[4,64,128]{2,1,0:T(8,128)(2,1)S(1)}, u32[]{:S(2)}, u32[]{:S(2)}) collective-permute-start(bf16[4,64,128]{2,1,0:T(8,128)(2,1)S(1)} %get-tuple-element.70), channel_id=1, source_target_pairs={{0,16},{1,17},{2,18},{3,19},{4,20},{5,21},{6,22},{7,23},{8,24},{9,... | collective-permute-start | bytes 196616 | tf_op jit(solution)/shard_map/ppermute | solution.py:262
  111.2 6.8 %collective-permute-start.23 = (bf16[4,64,128]{2,1,0:T(8,128)(2,1)S(1)}, bf16[4,64,128]{2,1,0:T(8,128)(2,1)S(1)}, u32[]{:S(2)}, u32[]{:S(2)}) collective-permute-start(bf16[4,64,128]{2,1,0:T(8,128)(2,1)S(1)} %get-tuple-element.71), channel_id=1, source_target_pairs={{0,24},{1,25},{2,26},{3,27},{4,28},{5,29},{6,30},{7,31},{8,0},{9,1... | collective-permute-start | bytes 196616 | tf_op jit(solution)/shard_map/ppermute | solution.py:262
  114.0 3.4 %copy-start = (bf16[2048,2048]{1,0:T(8,128)(2,1)S(1)}, bf16[2048,2048]{1,0:T(8,128)(2,1)}, u32[]{:S(2)}) copy-start(bf16[2048,2048]{1,0:T(8,128)(2,1)} %weight_ref) | copy-start | bytes 25165828
  117.4 0.9 copy-start.1
where the time goes:
time: 122 us; the launch traced here: 121 us
  starting transfers between devices  57.4 us (47%)
  waiting for transfers between devices  30.2 us (25%)
  Pallas kernels  26.6 us (22%)
  local copies, waits for them, and re-layouts  5.71 us (5%)
    ppermute x17, starting transfers between devices, move(): lax.ppermute(a, 'seq', [(at(z, x, c), at(z + dz, x + dx, c + dc)) for z,...  39.8 us
    pallas_call x4, Pallas kernels, attend(): pl.pallas_call(functools.partial(attend_kernel, shards, first, last), out...  21.2 us
    ppermute x17, waiting for transfers between devices, move(): lax.ppermute(a, 'seq', [(at(z, x, c), at(z + dz, x + dx, c + dc)) for z,...  19.5 us
    ppermute x9, starting transfers between devices, turn(): lax.ppermute(a, 'seq', [(at(z, x, c), at(z // BLOCK * BLOCK + (z + d) % B...  17.6 us
    ppermute x9, waiting for transfers between devices, turn(): lax.ppermute(a, 'seq', [(at(z, x, c), at(z // BLOCK * BLOCK + (z + d) % B...  10.7 us
    unnamed x6, local copies, waits for them, and re-layouts  3.73 us
    pallas_call x1, Pallas kernels, project(): pl.pallas_call(project_kernel, out_shape=jax.ShapeDtypeStruct(residual.sh...  2.47 us
  transfers between devices with their start and end apart: 26, of which 12 were waited for; matrix products, arithmetic and copies ran while one was open for 0% of the time, Pallas kernels for 13%

commit v1 on v0

--- a/solution.py
+++ b/solution.py
@@ -18,6 +18,7 @@
 BLOCK = KV_HEADS
 HALF = 32
 KV_ROWS = 2 * TOK + 8
+ALL_ROWS = (2 + GROUP) * TOK + 8
 ROWS = 256
 SCALE = HEAD_DIM ** -0.5 * math.log2(math.e)
 NEVER = -1e30
@@ -31,7 +32,16 @@
     return lax.broadcasted_iota(jnp.int32, shape, dim)
 
 
-def prep_kernel(pos_ref, q_ref, k_ref, v_ref, qs_ref, kv_ref):
+def prep_kernel(pos_hbm, q_hbm, k_hbm, v_hbm, out_ref, pos_ref, q_ref, k_ref, v_ref, arrived):
+    copies = [
+        pltpu.make_async_copy(source, target, arrived.at[n])
+        for n, (source, target) in enumerate(
+            ((pos_hbm, pos_ref), (k_hbm, k_ref), (v_hbm, v_ref), (q_hbm, q_ref))
+        )
+    ]
+    for copy in copies:
+        copy.start()
+    copies[0].wait()
     pos = pos_ref[...]
     run = pos // RUN
     off = (pos - run * RUN).astype(F32)
@@ -49,73 +59,96 @@
         for j in range(TOK // HALF)
     ]
     table = jnp.concatenate(lines + [jnp.zeros((8 - len(lines), HEAD_DIM), F32)], axis=0).astype(BF16)
+    copies[1].wait()
+    sorted_k = jnp.dot(pick16, k_ref[...], preferred_element_type=F32).astype(BF16)
+    copies[2].wait()
+    sorted_v = jnp.dot(pick16, v_ref[...], preferred_element_type=F32).astype(BF16)
+    copies[3].wait()
     sorted_q = jnp.dot(pick16, q_ref[...], preferred_element_type=F32).astype(BF16)
-    sorted_k = jnp.dot(pick16, k_ref[...], preferred_element_type=F32).astype(BF16)
-    sorted_v = jnp.dot(pick16, v_ref[...], preferred_element_type=F32).astype(BF16)
-    off16 = off_col.astype(BF16)
     for h in range(KV_HEADS):
         cols = slice(h * HEAD_DIM, (h + 1) * HEAD_DIM)
-        kv_ref[h, 0:TOK, :] = sorted_k[:, cols]
-        kv_ref[h, TOK:2 * TOK, :] = sorted_v[:, cols]
-        kv_ref[h, 2 * TOK:KV_ROWS, :] = table
+        out_ref[h, 0:TOK, :] = sorted_k[:, cols]
+        out_ref[h, TOK:2 * TOK, :] = sorted_v[:, cols]
         for g in range(GROUP):
             at = (h * GROUP + g) * HEAD_DIM
-            qs_ref[h, g] = sorted_q[:, at:at + HEAD_DIM]
-        qs_ref[h, GROUP] = off16
+            out_ref[h, (2 + g) * TOK:(3 + g) * TOK, :] = sorted_q[:, at:at + HEAD_DIM]
+        out_ref[h, (2 + GROUP) * TOK:ALL_ROWS, :] = table
 
 
 def prep(positions, query_rows, key_rows, value_rows):
     return pl.pallas_call(
         prep_kernel,
-        out_shape=(
-            jax.ShapeDtypeStruct((KV_HEADS, GROUP + 1, TOK, HEAD_DIM), BF16),
-            jax.ShapeDtypeStruct((KV_HEADS, KV_ROWS, HEAD_DIM), BF16),
-        ),
-        in_specs=[pl.BlockSpec(memory_space=VMEM)] * 4,
-        out_specs=(pl.BlockSpec(memory_space=VMEM),) * 2,
+        out_shape=jax.ShapeDtypeStruct((KV_HEADS, ALL_ROWS, HEAD_DIM), BF16),
+        in_specs=[pl.BlockSpec(memory_space=pltpu.HBM)] * 4,
+        out_specs=pl.BlockSpec(memory_space=VMEM),
+        scratch_shapes=[
+            VMEM((1, TOK), jnp.int32),
+            VMEM(query_rows.shape, BF16),
+            VMEM(key_rows.shape, BF16),
+            VMEM(value_rows.shape, BF16),
+            pltpu.SemaphoreType.DMA((4,)),
+        ],
         compiler_params=pltpu.CompilerParams(vmem_limit_bytes=60 * 1024 * 1024),
         cost_estimate=pl.CostEstimate(flops=TOK * TOK * 3072 * 2, bytes_accessed=800_000, transcendentals=0),
         name="prep",
     )(positions.reshape(1, TOK), query_rows, key_rows, value_rows)
 
 
-def attend_kernel(shards, first, last, *refs):
+def attend_kernel(parts, first, last, *refs):
     limit_ref, qa_ref, qb_ref = refs[:3]
-    kv_refs = refs[3:3 + shards]
-    refs = refs[3 + shards:]
+    kv_refs = refs[3:3 + parts]
+    refs = refs[3 + parts:]
     if first:
         old_refs = None
     else:
         old_refs, refs = refs[:4], refs[4:]
     new_refs, (keys, vals) = refs[:-2], refs[-2:]
     limit = limit_ref[0]
+    sources = KV_HEADS
+    units = [(kv, at) for kv in kv_refs for at in range(0, kv.shape[0], sources)]
+    shards = len(units)
     wide = shards * HEAD_DIM
-    sources = KV_HEADS
     for j in range(2):
-        for n, kv in enumerate(kv_refs):
+        for n, (kv, base) in enumerate(units):
             for s in range(sources):
                 at = j * wide + (n * sources + s) * HALF
-                keys[at:at + HALF, :] = kv[s, HALF * j:HALF * (j + 1), :]
-                vals[at:at + HALF, 0:HEAD_DIM] = kv[s, TOK + HALF * j:TOK + HALF * (j + 1), :]
+                keys[at:at + HALF, :] = kv[base + s, HALF * j:HALF * (j + 1), :]
+                vals[at:at + HALF, 0:HEAD_DIM] = kv[base + s, TOK + HALF * j:TOK + HALF * (j + 1), :]
     vals[:, HEAD_DIM:] = jnp.ones((2 * wide, HEAD_DIM), BF16)
     lane8 = iota((8, HEAD_DIM), 1)
     tables = []
-    for kv in kv_refs:
-        table = kv[0, 2 * TOK:KV_ROWS, :].astype(F32)
+    for kv, base in units:
+        table = kv[base, 2 * TOK:KV_ROWS, :].astype(F32)
         for s in range(1, sources):
-            table = jnp.where(lane8 // HALF == s, kv[s, 2 * TOK:KV_ROWS, :].astype(F32), table)
+            table = jnp.where(lane8 // HALF == s, kv[base + s, 2 * TOK:KV_ROWS, :].astype(F32), table)
         table = table + (lane8 % HALF * RUN).astype(F32)
         chunk = (iota((8, HEAD_DIM), 0) * (HALF * RUN)).astype(F32)
         tables.append(jnp.where(table + chunk >= limit.astype(F32), 1e9, table))
     ramp = (iota((HALF, HEAD_DIM), 0) * RUN).astype(F32)
+    diagonal = iota((HALF, HEAD_DIM), 0) == iota((HALF, HEAD_DIM), 1)
+    spread = [
+        jnp.where(diagonal, q_ref[src, ALL_ROWS - 8 + i:ALL_ROWS - 7 + i, :].astype(F32), 0.0).astype(BF16)
+        for q_ref in (qa_ref, qb_ref)
+        for i in range(2)
+        for src in range(sources)
+    ]
+    offsets = jnp.dot(
+        jnp.concatenate(spread, axis=0), jnp.ones((HEAD_DIM, HEAD_DIM), BF16), preferred_element_type=F32
+    )
     for half, q_ref in enumerate((qa_ref, qb_ref)):
         for i in range(2):
             for sp in range(2):
                 b = i * 2 + sp
-                rows_at = slice(HALF * i, HALF * (i + 1))
-                q = q_ref[2 * sp:2 * sp + 2, 0:GROUP, rows_at, :].reshape(ROWS, HEAD_DIM)
-                q_off = q_ref[2 * sp:2 * sp + 2, GROUP:GROUP + 1, rows_at, :].astype(F32)
-                q_pos = jnp.broadcast_to(q_off + ramp[None, None], (2, GROUP, HALF, HEAD_DIM)).reshape(ROWS, HEAD_DIM)
+                q_rows = []
+                q_poss = []
+                for src in (2 * sp, 2 * sp + 1):
+                    for g in range(GROUP):
+                        at = (2 + g) * TOK + HALF * i
+                        q_rows.append(q_ref[src, at:at + HALF, :])
+                    at = ((half * 2 + i) * sources + src) * HALF
+                    q_poss += [offsets[at:at + HALF, :] + ramp] * GROUP
+                q = jnp.concatenate(q_rows, axis=0)
+                q_pos = jnp.concatenate(q_poss, axis=0)
                 count = (i + 1) * wide
                 s = lax.dot_general(
                     q, keys[0:count, :], (((1,), (1,)), ((), ())), preferred_element_type=F32
@@ -146,7 +179,7 @@
 
 
 def attend(limit, qa, qb, parts, state, last=False):
-    shards = len(parts)
+    shards = sum(part.shape[0] for part in parts) // KV_HEADS
     wide = shards * HEAD_DIM
     stats = jax.ShapeDtypeStruct((4, ROWS, HEAD_DIM), F32)
     sums = jax.ShapeDtypeStruct((4, ROWS, 2 * HEAD_DIM), F32)
@@ -154,15 +187,15 @@
     first = state is None
     held = [] if first else list(state)
     score_count = 4 * 2 * ROWS * 3 * wide
-    base = 3 + shards
-    return pl.pallas_call(
-        functools.partial(attend_kernel, shards, first, last),
+    base = 3 + len(parts)
+    return pl.pallas_call(
+        functools.partial(attend_kernel, len(parts), first, last),
         out_shape=shapes,
-        in_specs=[pl.BlockSpec(memory_space=pltpu.SMEM)] + [pl.BlockSpec(memory_space=VMEM)] * (2 + shards + len(held)),
+        in_specs=[pl.BlockSpec(memory_space=pltpu.SMEM)] + [pl.BlockSpec(memory_space=VMEM)] * (2 + len(parts) + len(held)),
         out_specs=(pl.BlockSpec(memory_space=VMEM),) * len(shapes),
         scratch_shapes=[VMEM((2 * wide, HEAD_DIM), BF16), VMEM((2 * wide, 2 * HEAD_DIM), BF16)],
-        input_output_aliases={} if first else ({base: 0, base + 1: 1, base + 3: 2} if last else {base + n: n for n in range(4)}),
-        compiler_params=pltpu.CompilerParams(vmem_limit_bytes=16 * 1024 * 1024),
+        input_output_aliases={} if first else ({base: 0, base + 1: 1} if last else {base + n: n for n in range(4)}),
+        compiler_params=pltpu.CompilerParams(vmem_limit_bytes=12 * 1024 * 1024),
         cost_estimate=pl.CostEstimate(
             flops=score_count * HEAD_DIM * 6, bytes_accessed=4_000_000, transcendentals=score_count
         ),
@@ -258,38 +291,42 @@
     def move(a, dz=0, dx=0, dc=0):
         return lax.ppermute(a, "seq", [(at(z, x, c), at(z + dz, x + dx, c + dc)) for z, x, c in spots])
 
+    def far(a):
+        return lax.ppermute(
+            a, "seq", [(at(z, x, c), at(z + (BLOCK if c == 0 else -BLOCK), x, c)) for z, x, c in spots]
+        )
+
     def turn(a, d):
         return lax.ppermute(
             a, "seq", [(at(z, x, c), at(z // BLOCK * BLOCK + (z + d) % BLOCK, x, c)) for z, x, c in spots]
         )
 
+    def spread(a):
+        return [move(a, dx=2), move(a, dx=1), move(a, dx=-1)]
+
     member = lax.rem(lax.axis_index("seq") // (X_DEV * CORES), BLOCK)
-
-    def exchange(a):
-        pick = [lax.dynamic_index_in_dim(a, lax.rem(member + d, BLOCK), 0, keepdims=False) for d in range(BLOCK)]
-        return [pick[0]] + [turn(pick[d], d) for d in range(1, BLOCK)]
-
-    qs, kvs = prep(positions, query_rows, key_rows, value_rows)
-    own = jnp.stack(exchange(kvs))
-
-    def spread(a):
-        return [a, move(a, dx=1), move(a, dx=-1), move(a, dx=2)]
-
-    ahead = move(own, dz=BLOCK)
-    behind = move(own, dz=-BLOCK)
-    across = move(own, dz=2 * BLOCK)
-    group = spread(own)
-    qs, own = lax.optimization_barrier((qs, own))
-    qa = jnp.stack(exchange(qs))
-    qb = move(qa, dc=1)
-    state = attend(prompt_length, qa, qb, group, None)
-    state, ahead, behind = lax.optimization_barrier((state, ahead, behind))
-    next_group, group = spread(ahead), spread(behind)
-    state = attend(prompt_length, qa, qb, next_group, state)
-    state, across = lax.optimization_barrier((state, across))
-    last_group = spread(across)
-    state = attend(prompt_length, qa, qb, group, state)
-    state = attend(prompt_length, qa, qb, last_group, state, last=True)
+    message = prep(positions, query_rows, key_rows, value_rows)
+    pick = [lax.dynamic_index_in_dim(message, lax.rem(member + d, BLOCK), 0, keepdims=False) for d in range(BLOCK)]
+    own = jnp.stack([pick[0]] + [turn(pick[d], d) for d in range(1, BLOCK)])
+    twin = move(own, dc=1)
+
+    def kv_of(a):
+        return jnp.concatenate([a[:, 0:2 * TOK], a[:, ALL_ROWS - 8:]], axis=1)
+
+    mine = kv_of(own)
+    one = far(mine)
+    other = far(kv_of(twin))
+    group = [mine] + spread(mine)
+    two = far(one)
+    state = attend(prompt_length, own, twin, group, None)
+    state, other = lax.optimization_barrier((state, other))
+    one = jnp.concatenate([one, other], axis=0)
+    group = [one] + spread(one)
+    state = attend(prompt_length, own, twin, group[:2], state)
+    state, two = lax.optimization_barrier((state, two))
+    last_group = spread(two)
+    state = attend(prompt_length, own, twin, group[2:] + [two], state)
+    state = attend(prompt_length, own, twin, last_group, state, last=True)
     got = move(state[2], dc=1)
     done = merge(state[0], state[1], got)
     parts = [done[0]] + [turn(done[d], -d) for d in range(1, BLOCK)]

time: 122 us -> 104 us (0.85)
  starting transfers between devices: 57.4 us -> 49.7 us
  Pallas kernels: 26.6 us -> 20.6 us
  waiting for transfers between devices: 30.2 us -> 27.8 us
    ppermute x17 -> x11, starting transfers between devices: 39.8 us -> 15.1 us  [move(): lax.ppermute(a, 'seq', [(at(z, x, c), at(z + dz, x + dx, c + dc)) for z,...]
    ppermute x0 -> x3, starting transfers between devices: none -> 18.4 us  [far(): lax.ppermute(a, 'seq', [(at(z, x, c), at(z + (BLOCK if c == 0 else -BLOCK...]
    ppermute x17 -> x11, waiting for transfers between devices: 19.5 us -> 4.82 us  [move(): lax.ppermute(a, 'seq', [(at(z, x, c), at(z + dz, x + dx, c + dc)) for z,...]
    ppermute x0 -> x3, waiting for transfers between devices: none -> 14.6 us  [far(): lax.ppermute(a, 'seq', [(at(z, x, c), at(z + (BLOCK if c == 0 else -BLOCK...]
    pallas_call x5, Pallas kernels: 23.2 us -> 17.2 us  [the longest x4 15.1 us: attend(): pl.pallas_call(functools.partial(attend_kernel, len(parts), first, last),...]
    ppermute x9 -> x6, waiting for transfers between devices: 10.7 us -> 8.37 us  [turn(): lax.ppermute(a, 'seq', [(at(z, x, c), at(z // BLOCK * BLOCK + (z + d) % B...]
    ppermute x9 -> x6, starting transfers between devices: 17.6 us -> 16.2 us  [turn(): lax.ppermute(a, 'seq', [(at(z, x, c), at(z // BLOCK * BLOCK + (z + d) % B...]
    unnamed x6 -> x7, local copies, waits for them, and re-layouts: 3.73 us -> 3.74 us
  transfers between devices with their start and end apart: 26 -> 20, of which waited for: 12 -> 8; matrix products, arithmetic and copies ran while one was open for 0% -> 0% of each run, Pallas kernels for 13% -> 11%
where the time goes in v1:
time: 104 us
  starting transfers between devices  49.7 us (48%)
  waiting for transfers between devices  27.8 us (27%)
  Pallas kernels  20.6 us (20%)
  local copies, waits for them, and re-layouts  4.98 us (5%)
    ppermute x3, starting transfers between devices, far(): lax.ppermute(a, 'seq', [(at(z, x, c), at(z + (BLOCK if c == 0 else -BLOCK...  18.4 us
    ppermute x6, starting transfers between devices, turn(): lax.ppermute(a, 'seq', [(at(z, x, c), at(z // BLOCK * BLOCK + (z + d) % B...  16.2 us
    ppermute x11, starting transfers between devices, move(): lax.ppermute(a, 'seq', [(at(z, x, c), at(z + dz, x + dx, c + dc)) for z,...  15.1 us
    pallas_call x4, Pallas kernels, attend(): pl.pallas_call(functools.partial(attend_kernel, len(parts), first, last),...  15.1 us
    ppermute x3, waiting for transfers between devices, far(): lax.ppermute(a, 'seq', [(at(z, x, c), at(z + (BLOCK if c == 0 else -BLOCK...  14.6 us
    ppermute x6, waiting for transfers between devices, turn(): lax.ppermute(a, 'seq', [(at(z, x, c), at(z // BLOCK * BLOCK + (z + d) % B...  8.37 us
    ppermute x11, waiting for transfers between devices, move(): lax.ppermute(a, 'seq', [(at(z, x, c), at(z + dz, x + dx, c + dc)) for z,...  4.82 us
    unnamed x7, local copies, waits for them, and re-layouts  3.74 us
  transfers between devices with their start and end apart: 20, of which 8 were waited for; matrix products, arithmetic and copies ran while one was open for 0% of the time, Pallas kernels for 11%

profile of v1, /device:TPU:40, one launch (start us, length us, event | category | flops | bytes accessed | tf_op | source)
XLA Modules:
  0.0 104.0 jit_solution(6997030915907434583)
XLA Ops:
  0.0 2.1 %prep.1 = bf16[4,392,128]{2,1,0:T(8,128)(2,1)} custom-call(s32[1,64]{1,0:T(1,128)} %bitcast.23, bf16[64,2048]{1,0:T(8,128)(2,1)} %q_hbm.1, bf16[64,512]{1,0:T(8,128)(2,1)} %k_hbm.1, bf16[64,512]{1,0:T(8,128)(2,1)} %v_hbm.1), custom_call_target="tpu_custom_call" | custom-call | flops 25165824 | bytes 800000 | tf_op jit(solution)/shard_map/prep/pallas_call | solution.py:79
  2.2 1.1 %constant_dynamic-slice_fusion = (bf16[1,392,128]{2,1,0:T(8,128)(2,1)S(1)}, bf16[392,128]{1,0:T(8,128)(2,1)S(1)}, bf16[392,128]{1,0:T(8,128)(2,1)S(1)}, bf16[392,128]{1,0:T(8,128)(2,1)S(1)}) fusion(bf16[4,392,128]{2,1,0:T(8,128)(2,1)} %prep.1, s32[]{:T(128)S(6)} %select_n.19, s32[]{:T(128)S(6)} %select_n.22, s32[]{:T(128)S(6)} %select_n.21, s32[]{:T(128)S(6)} %select_n.20), kind=kLoop, calls=%fused_computation.12 | loop fusion | bytes 802832 | tf_op jit(solution)/shard_map/jit(dynamic_index_in_dim)/dynamic_slice | solution.py:309
  3.2 7.3 %collective-permute-start.2 = (bf16[392,128]{1,0:T(8,128)(2,1)S(1)}, bf16[392,128]{1,0:T(8,128)(2,1)S(1)}, u32[]{:S(2)}, u32[]{:S(2)}) collective-permute-start(bf16[392,128]{1,0:T(8,128)(2,1)S(1)} %get-tuple-element.58), channel_id=1, source_target_pairs={{0,24},{1,25},{2,26},{3,27},{4,28},{5,29},{6,30},{7,31},{8,0},{9,1... | collective-permute-start | bytes 301064 | tf_op jit(solution)/shard_map/ppermute | solution.py:300
  10.5 0.0 collective-permute-start.1
  10.6 0.7 collective-permute-start
  11.3 2.5 %collective-permute-done.2 = bf16[392,128]{1,0:T(8,128)(2,1)S(1)} collective-permute-done((bf16[392,128]{1,0:T(8,128)(2,1)S(1)}, bf16[392,128]{1,0:T(8,128)(2,1)S(1)}, u32[]{:S(2)}, u32[]{:S(2)}) %collective-permute-start.2) | collective-permute-done | bytes 100384 | tf_op jit(solution)/shard_map/ppermute | solution.py:300
  13.8 5.8 %collective-permute-done.1 = bf16[392,128]{1,0:T(8,128)(2,1)S(1)} collective-permute-done((bf16[392,128]{1,0:T(8,128)(2,1)S(1)}, bf16[392,128]{1,0:T(8,128)(2,1)S(1)}, u32[]{:S(2)}, u32[]{:S(2)}) %collective-permute-start.1) | collective-permute-done | bytes 100384 | tf_op jit(solution)/shard_map/ppermute | solution.py:300
  19.6 0.0 collective-permute-done
  19.6 0.1 pad_maximum_fusion.refs_1_
  19.7 0.1 collective-permute-start.3
  19.9 10.7 %collective-permute-start.4 = (bf16[4,136,128]{2,1,0:T(8,128)(2,1)S(1)}, bf16[4,136,128]{2,1,0:T(8,128)(2,1)S(1)}, u32[]{:S(2)}, u32[]{:S(2)}) collective-permute-start(bf16[4,136,128]{2,1,0:T(8,128)(2,1)S(1)} %pad_maximum_fusion.1.refs_3_), channel_id=1, source_target_pairs={{0,32},{1,97},{2,34},{3,99},{4,36},{5,101},{6,38},{7,103},{8,40},{... | collective-permute-start | bytes 417800 | tf_op jit(solution)/shard_map/ppermute | solution.py:295
  31.3 3.3 %collective-permute-start.7 = (bf16[4,136,128]{2,1,0:T(8,128)(2,1)S(1)}, bf16[4,136,128]{2,1,0:T(8,128)(2,1)S(1)}, u32[]{:S(2)}, u32[]{:S(2)}) collective-permute-start(bf16[4,136,128]{2,1,0:T(8,128)(2,1)S(1)} %pad_maximum_fusion.1.refs_3_), channel_id=1, source_target_pairs={{0,6},{1,7},{2,0},{3,1},{4,2},{5,3},{6,4},{7,5},{8,14},{9,15},{10,... | collective-permute-start | bytes 417800 | tf_op jit(solution)/shard_map/ppermute | solution.py:292
  34.6 0.0 collective-permute-start.6
  34.6 2.1 %collective-permute-start.5 = (bf16[4,136,128]{2,1,0:T(8,128)(2,1)S(1)}, bf16[4,136,128]{2,1,0:T(8,128)(2,1)S(1)}, u32[]{:S(2)}, u32[]{:S(2)}) collective-permute-start(bf16[4,136,128]{2,1,0:T(8,128)(2,1)S(1)} %pad_maximum_fusion.1.refs_3_), channel_id=1, source_target_pairs={{0,4},{1,5},{2,6},{3,7},{4,0},{5,1},{6,2},{7,3},{8,12},{9,13},{10,... | collective-permute-start | bytes 417800 | tf_op jit(solution)/shard_map/ppermute | solution.py:292
  36.7 5.0 %collective-permute-done.4 = bf16[4,136,128]{2,1,0:T(8,128)(2,1)S(1)} collective-permute-done((bf16[4,136,128]{2,1,0:T(8,128)(2,1)S(1)}, bf16[4,136,128]{2,1,0:T(8,128)(2,1)S(1)}, u32[]{:S(2)}, u32[]{:S(2)}) %collective-permute-start.4) | collective-permute-done | bytes 139296 | tf_op jit(solution)/shard_map/ppermute | solution.py:295
  41.7 0.0 collective-permute-done.3.refs_2_
  41.8 3.0 %collective-permute-start.8 = (bf16[4,136,128]{2,1,0:T(8,128)(2,1)S(1)}, bf16[4,136,128]{2,1,0:T(8,128)(2,1)S(1)}, u32[]{:S(2)}, u32[]{:S(2)}) collective-permute-start(bf16[4,136,128]{2,1,0:T(8,128)(2,1)S(1)} %pad_maximum_fusion.2), channel_id=1, source_target_pairs={{0,32},{1,97},{2,34},{3,99},{4,36},{5,101},{6,38},{7,103},{8,40},{... | collective-permute-start | bytes 417800 | tf_op jit(solution)/shard_map/ppermute | solution.py:295
  44.8 0.0 collective-permute-done.7.refs_6_
  44.8 0.0 collective-permute-done.6.refs_5_
  44.8 2.8 %attend.3 = (f32[4,256,128]{2,1,0:T(8,128)S(1)}, f32[4,256,256]{2,1,0:T(8,128)S(1)}, f32[4,256,128]{2,1,0:T(8,128)S(1)}, f32[4,256,256]{2,1,0:T(8,128)S(1)}) custom-call(s32[1]{0:T(128)S(6)} %copy.30.refs_0_, bf16[4,392,128]{2,1,0:T(8,128)(2,1)S(1)} %pad_maximum_fusion.refs_1_, bf16[4,392,128]{2,1,0:T(8,128)(2,1)S(1)} %collective-permute-done.3.refs_2_, ...), custom_call_target="tpu_custom_call" | custom-call | flops 2415919104 | bytes 4000000 | tf_op jit(solution)/shard_map/attend/pallas_call | solution.py:191
  47.6 4.7 %collective-permute-done.8 = bf16[4,136,128]{2,1,0:T(8,128)(2,1)S(1)} collective-permute-done((bf16[4,136,128]{2,1,0:T(8,128)(2,1)S(1)}, bf16[4,136,128]{2,1,0:T(8,128)(2,1)S(1)}, u32[]{:S(2)}, u32[]{:S(2)}) %collective-permute-start.8) | collective-permute-done | bytes 139296 | tf_op jit(solution)/shard_map/ppermute | solution.py:295
  52.3 3.4 %collective-permute-start.9 = (bf16[8,136,128]{2,1,0:T(8,128)(2,1)S(1)}, bf16[8,136,128]{2,1,0:T(8,128)(2,1)S(1)}, u32[]{:S(2)}, u32[]{:S(2)}) collective-permute-start(bf16[8,136,128]{2,1,0:T(8,128)(2,1)S(1)} %constant_dynamic-update-slice_fusion.refs_3_), channel_id=1, source_target_pairs={{0,4},{1,5},{2,6},{3,7},{4,0},{5,1},{6,2},{7,3},{8,12},{9,13},{10,... | collective-permute-start | bytes 835592 | tf_op jit(solution)/shard_map/ppermute | solution.py:292
  55.7 1.0 collective-permute-start.15
  56.7 1.0 collective-permute-start.14
  57.7 4.7 %collective-permute-start.10 = (bf16[4,136,128]{2,1,0:T(8,128)(2,1)S(1)}, bf16[4,136,128]{2,1,0:T(8,128)(2,1)S(1)}, u32[]{:S(2)}, u32[]{:S(2)}) collective-permute-start(bf16[4,136,128]{2,1,0:T(8,128)(2,1)S(1)} %collective-permute-done.4), channel_id=1, source_target_pairs={{0,32},{1,97},{2,34},{3,99},{4,36},{5,101},{6,38},{7,103},{8,40},{... | collective-permute-start | bytes 417800 | tf_op jit(solution)/shard_map/ppermute | solution.py:295
  62.4 0.2 collective-permute-done.9.refs_4_
  62.6 3.8 %attend.4 = (f32[4,256,128]{2,1,0:T(8,128)S(1)}, f32[4,256,256]{2,1,0:T(8,128)S(1)}, f32[4,256,128]{2,1,0:T(8,128)S(1)}, f32[4,256,256]{2,1,0:T(8,128)S(1)}) custom-call(s32[1]{0:T(128)S(6)} %copy.30.refs_0_, bf16[4,392,128]{2,1,0:T(8,128)(2,1)S(1)} %pad_maximum_fusion.refs_1_, ...), custom_call_target="tpu_custom_call", output_to_operand_aliasing={{0}: (5, {}), {1}: (6, {}), {2}: (7, {}), {3}: (8, {})} | custom-call | flops 2415919104 | bytes 4000000 | tf_op jit(solution)/shard_map/attend/pallas_call | solution.py:191
  66.4 5.0 %collective-permute-done.10.refs_5_ = bf16[4,136,128]{2,1,0:T(8,128)(2,1)S(1)} collective-permute-done((bf16[4,136,128]{2,1,0:T(8,128)(2,1)S(1)}, bf16[4,136,128]{2,1,0:T(8,128)(2,1)S(1)}, u32[]{:S(2)}, u32[]{:S(2)}) %collective-permute-start.10) | collective-permute-done | bytes 139296 | tf_op jit(solution)/shard_map/ppermute | solution.py:295
  71.3 2.7 %collective-permute-start.13 = (bf16[4,136,128]{2,1,0:T(8,128)(2,1)S(1)}, bf16[4,136,128]{2,1,0:T(8,128)(2,1)S(1)}, u32[]{:S(2)}, u32[]{:S(2)}) collective-permute-start(bf16[4,136,128]{2,1,0:T(8,128)(2,1)S(1)} %collective-permute-done.10.refs_5_), channel_id=1, source_target_pairs={{0,6},{1,7},{2,0},{3,1},{4,2},{5,3},{6,4},{7,5},{8,14},{9,15},{10,... | collective-permute-start | bytes 417800 | tf_op jit(solution)/shard_map/ppermute | solution.py:292
  74.0 0.0 collective-permute-start.12
  74.0 1.5 %collective-permute-start.11 = (bf16[4,136,128]{2,1,0:T(8,128)(2,1)S(1)}, bf16[4,136,128]{2,1,0:T(8,128)(2,1)S(1)}, u32[]{:S(2)}, u32[]{:S(2)}) collective-permute-start(bf16[4,136,128]{2,1,0:T(8,128)(2,1)S(1)} %collective-permute-done.10.refs_5_), channel_id=1, source_target_pairs={{0,4},{1,5},{2,6},{3,7},{4,0},{5,1},{6,2},{7,3},{8,12},{9,13},{10,... | collective-permute-start | bytes 417800 | tf_op jit(solution)/shard_map/ppermute | solution.py:292
  75.5 0.0 collective-permute-done.14.refs_3_
  75.5 4.5 %attend.5 = (f32[4,256,128]{2,1,0:T(8,128)S(1)}, f32[4,256,256]{2,1,0:T(8,128)S(1)}, f32[4,256,128]{2,1,0:T(8,128)S(1)}, f32[4,256,256]{2,1,0:T(8,128)S(1)}) custom-call(s32[1]{0:T(128)S(6)} %copy.30.refs_0_, bf16[4,392,128]{2,1,0:T(8,128)(2,1)S(1)} %pad_maximum_fusion.refs_1_, ...), custom_call_target="tpu_custom_call", output_to_operand_aliasing={{0}: (6, {}), {1}: (7, {}), {2}: (8, {}), {3}: (9, {})} | custom-call | flops 3019898880 | bytes 4000000 | tf_op jit(solution)/shard_map/attend/pallas_call | solution.py:191
  80.0 1.8 %collective-permute-done.12.refs_4_ = bf16[4,136,128]{2,1,0:T(8,128)(2,1)S(1)} collective-permute-done((bf16[4,136,128]{2,1,0:T(8,128)(2,1)S(1)}, bf16[4,136,128]{2,1,0:T(8,128)(2,1)S(1)}, u32[]{:S(2)}, u32[]{:S(2)}) %collective-permute-start.12) | collective-permute-done | bytes 139296 | tf_op jit(solution)/shard_map/ppermute | solution.py:292
  81.8 0.0 collective-permute-done.11.refs_3_
  81.8 4.0 %attend_last.1 = (f32[4,256,128]{2,1,0:T(8,128)S(1)}, f32[4,256,256]{2,1,0:T(8,128)S(1)}, f32[4,256,256]{2,1,0:T(8,128)}) custom-call(s32[1]{0:T(128)S(6)} %copy.30.refs_0_, bf16[4,392,128]{2,1,0:T(8,128)(2,1)S(1)} %pad_maximum_fusion.refs_1_, bf16[4,392,128]{2,1,0:T(8,128)(2,1)S(1)} %collective-permute-done.3.refs_2_, ...), custom_call_target="tpu_custom_call", output_to_operand_aliasing={{0}: (6, {}), {1}: (7, {})} | custom-call | flops 1811939328 | bytes 4000000 | tf_op jit(solution)/shard_map/attend_last/pallas_call | solution.py:191
  85.8 0.1 copy.18.pos_ref
  85.9 2.8 %collective-permute-done.16.got_ref = f32[4,256,256]{2,1,0:T(8,128)S(1)} collective-permute-done((f32[4,256,256]{2,1,0:T(8,128)}, f32[4,256,256]{2,1,0:T(8,128)S(1)}, u32[]{:S(2)}, u32[]{:S(2)}) %collective-permute-start.16) | collective-permute-done | bytes 1048608 | tf_op jit(solution)/shard_map/ppermute | solution.py:292
  88.7 0.4 merge.1
  89.1 2.9 %collective-permute-start.19 = (bf16[4,64,128]{2,1,0:T(8,128)(2,1)S(1)}, bf16[4,64,128]{2,1,0:T(8,128)(2,1)S(1)}, u32[]{:S(2)}, u32[]{:S(2)}) collective-permute-start(bf16[4,64,128]{2,1,0:T(8,128)(2,1)S(1)} %get-tuple-element.61), channel_id=1, source_target_pairs={{0,8},{1,9},{2,10},{3,11},{4,12},{5,13},{6,14},{7,15},{8,16},{9,17... | collective-permute-start | bytes 196616 | tf_op jit(solution)/shard_map/ppermute | solution.py:300
  92.0 2.4 %collective-permute-start.18 = (bf16[4,64,128]{2,1,0:T(8,128)(2,1)S(1)}, bf16[4,64,128]{2,1,0:T(8,128)(2,1)S(1)}, u32[]{:S(2)}, u32[]{:S(2)}) collective-permute-start(bf16[4,64,128]{2,1,0:T(8,128)(2,1)S(1)} %get-tuple-element.62), channel_id=1, source_target_pairs={{0,16},{1,17},{2,18},{3,19},{4,20},{5,21},{6,22},{7,23},{8,24},{9,... | collective-permute-start | bytes 196616 | tf_op jit(solution)/shard_map/ppermute | solution.py:300
  94.4 2.8 %collective-permute-start.17 = (bf16[4,64,128]{2,1,0:T(8,128)(2,1)S(1)}, bf16[4,64,128]{2,1,0:T(8,128)(2,1)S(1)}, u32[]{:S(2)}, u32[]{:S(2)}) collective-permute-start(bf16[4,64,128]{2,1,0:T(8,128)(2,1)S(1)} %get-tuple-element.63), channel_id=1, source_target_pairs={{0,24},{1,25},{2,26},{3,27},{4,28},{5,29},{6,30},{7,31},{8,0},{9,1... | collective-permute-start | bytes 196616 | tf_op jit(solution)/shard_map/ppermute | solution.py:300
  97.2 3.4 %copy-done = bf16[2048,2048]{1,0:T(8,128)(2,1)S(1)} copy-done((bf16[2048,2048]{1,0:T(8,128)(2,1)S(1)}, bf16[2048,2048]{1,0:T(8,128)(2,1)}, u32[]{:S(2)}) %copy-start) | copy-done | bytes 8388632
  100.6 0.6 hold.1.refs_4_
  101.2 0.0 collective-permute-done.18.refs_2_
  101.2 0.0 collective-permute-done.17.refs_1_
  101.2 0.3 copy-done.1
  101.6 2.5 %project.1 = bf16[64,2048]{1,0:T(8,128)(2,1)} custom-call(s32[1]{0:T(128)} %bitcast.member_ref, s32[64,1]{1,0:T(8,128)S(1)} %copy.18.pos_ref, bf16[4,64,128]{2,1,0:T(8,128)(2,1)S(1)} %get-tuple-element.64.refs_0_, bf16[4,64,128]{2,1,0:T(8,128)(2,1)S(1)} %collective-permute-done.17.refs_1_, bf16[4,64,128]{2,1,0:T(8,128)(2,1)S(1)} %collective-permute-done.18.refs_2_, ...), custom_call_target="tpu_custom_call" | custom-call | flops 536870912 | bytes 9000000 | tf_op jit(solution)/shard_map/project/pallas_call | solution.py:271
  (18 shorter events, 0.1 us)
Async XLA Ops:
  3.2 10.5 %collective-permute-start.2 = (bf16[392,128]{1,0:T(8,128)(2,1)S(1)}, bf16[392,128]{1,0:T(8,128)(2,1)S(1)}, u32[]{:S(2)}, u32[]{:S(2)}) collective-permute-start(bf16[392,128]{1,0:T(8,128)(2,1)S(1)} %get-tuple-element.58), channel_id=1, source_target_pairs={{0,24},{1,25},{2,26},{3,27},{4,28},{5,29},{6,30},{7,31},{8,0},{9,1... | collective-permute-start | bytes 301064 | tf_op jit(solution)/shard_map/ppermute | solution.py:300
  10.5 9.1 %collective-permute-start.1 = (bf16[392,128]{1,0:T(8,128)(2,1)S(1)}, bf16[392,128]{1,0:T(8,128)(2,1)S(1)}, u32[]{:S(2)}, u32[]{:S(2)}) collective-permute-start(bf16[392,128]{1,0:T(8,128)(2,1)S(1)} %get-tuple-element.59), channel_id=1, source_target_pairs={{0,16},{1,17},{2,18},{3,19},{4,20},{5,21},{6,22},{7,23},{8,24},{9,... | collective-permute-start | bytes 301064 | tf_op jit(solution)/shard_map/ppermute | solution.py:300
  10.6 9.1 %collective-permute-start = (bf16[392,128]{1,0:T(8,128)(2,1)S(1)}, bf16[392,128]{1,0:T(8,128)(2,1)S(1)}, u32[]{:S(2)}, u32[]{:S(2)}) collective-permute-start(bf16[392,128]{1,0:T(8,128)(2,1)S(1)} %get-tuple-element.60), channel_id=1, source_target_pairs={{0,8},{1,9},{2,10},{3,11},{4,12},{5,13},{6,14},{7,15},{8,16},{9,17... | collective-permute-start | bytes 301064 | tf_op jit(solution)/shard_map/ppermute | solution.py:300
  19.7 22.1 %collective-permute-start.3 = (bf16[4,392,128]{2,1,0:T(8,128)(2,1)S(1)}, bf16[4,392,128]{2,1,0:T(8,128)(2,1)S(1)}, u32[]{:S(2)}, u32[]{:S(2)}) collective-permute-start(bf16[4,392,128]{2,1,0:T(8,128)(2,1)S(1)} %pad_maximum_fusion.refs_1_), channel_id=1, source_target_pairs={{0,1},{1,0},{2,3},{3,2},{4,5},{5,4},{6,7},{7,6},{8,9},{9,8},{10,11... | collective-permute-start | bytes 1204232 | tf_op jit(solution)/shard_map/ppermute | solution.py:292
  19.9 21.8 %collective-permute-start.4 = (bf16[4,136,128]{2,1,0:T(8,128)(2,1)S(1)}, bf16[4,136,128]{2,1,0:T(8,128)(2,1)S(1)}, u32[]{:S(2)}, u32[]{:S(2)}) collective-permute-start(bf16[4,136,128]{2,1,0:T(8,128)(2,1)S(1)} %pad_maximum_fusion.1.refs_3_), channel_id=1, source_target_pairs={{0,32},{1,97},{2,34},{3,99},{4,36},{5,101},{6,38},{7,103},{8,40},{... | collective-permute-start | bytes 417800 | tf_op jit(solution)/shard_map/ppermute | solution.py:295
  31.3 13.5 %collective-permute-start.7 = (bf16[4,136,128]{2,1,0:T(8,128)(2,1)S(1)}, bf16[4,136,128]{2,1,0:T(8,128)(2,1)S(1)}, u32[]{:S(2)}, u32[]{:S(2)}) collective-permute-start(bf16[4,136,128]{2,1,0:T(8,128)(2,1)S(1)} %pad_maximum_fusion.1.refs_3_), channel_id=1, source_target_pairs={{0,6},{1,7},{2,0},{3,1},{4,2},{5,3},{6,4},{7,5},{8,14},{9,15},{10,... | collective-permute-start | bytes 417800 | tf_op jit(solution)/shard_map/ppermute | solution.py:292
  34.6 10.2 %collective-permute-start.6 = (bf16[4,136,128]{2,1,0:T(8,128)(2,1)S(1)}, bf16[4,136,128]{2,1,0:T(8,128)(2,1)S(1)}, u32[]{:S(2)}, u32[]{:S(2)}) collective-permute-start(bf16[4,136,128]{2,1,0:T(8,128)(2,1)S(1)} %pad_maximum_fusion.1.refs_3_), channel_id=1, source_target_pairs={{0,2},{1,3},{2,4},{3,5},{4,6},{5,7},{6,0},{7,1},{8,10},{9,11},{10,... | collective-permute-start | bytes 417800 | tf_op jit(solution)/shard_map/ppermute | solution.py:292
  34.6 10.2 %collective-permute-start.5 = (bf16[4,136,128]{2,1,0:T(8,128)(2,1)S(1)}, bf16[4,136,128]{2,1,0:T(8,128)(2,1)S(1)}, u32[]{:S(2)}, u32[]{:S(2)}) collective-permute-start(bf16[4,136,128]{2,1,0:T(8,128)(2,1)S(1)} %pad_maximum_fusion.1.refs_3_), channel_id=1, source_target_pairs={{0,4},{1,5},{2,6},{3,7},{4,0},{5,1},{6,2},{7,3},{8,12},{9,13},{10,... | collective-permute-start | bytes 417800 | tf_op jit(solution)/shard_map/ppermute | solution.py:292
  41.8 10.4 %collective-permute-start.8 = (bf16[4,136,128]{2,1,0:T(8,128)(2,1)S(1)}, bf16[4,136,128]{2,1,0:T(8,128)(2,1)S(1)}, u32[]{:S(2)}, u32[]{:S(2)}) collective-permute-start(bf16[4,136,128]{2,1,0:T(8,128)(2,1)S(1)} %pad_maximum_fusion.2), channel_id=1, source_target_pairs={{0,32},{1,97},{2,34},{3,99},{4,36},{5,101},{6,38},{7,103},{8,40},{... | collective-permute-start | bytes 417800 | tf_op jit(solution)/shard_map/ppermute | solution.py:295
  52.3 10.4 %collective-permute-start.9 = (bf16[8,136,128]{2,1,0:T(8,128)(2,1)S(1)}, bf16[8,136,128]{2,1,0:T(8,128)(2,1)S(1)}, u32[]{:S(2)}, u32[]{:S(2)}) collective-permute-start(bf16[8,136,128]{2,1,0:T(8,128)(2,1)S(1)} %constant_dynamic-update-slice_fusion.refs_3_), channel_id=1, source_target_pairs={{0,4},{1,5},{2,6},{3,7},{4,0},{5,1},{6,2},{7,3},{8,12},{9,13},{10,... | collective-permute-start | bytes 835592 | tf_op jit(solution)/shard_map/ppermute | solution.py:292
  55.7 19.8 %collective-permute-start.15 = (bf16[8,136,128]{2,1,0:T(8,128)(2,1)S(1)}, bf16[8,136,128]{2,1,0:T(8,128)(2,1)S(1)}, u32[]{:S(2)}, u32[]{:S(2)}) collective-permute-start(bf16[8,136,128]{2,1,0:T(8,128)(2,1)S(1)} %constant_dynamic-update-slice_fusion.refs_3_), channel_id=1, source_target_pairs={{0,6},{1,7},{2,0},{3,1},{4,2},{5,3},{6,4},{7,5},{8,14},{9,15},{10,... | collective-permute-start | bytes 835592 | tf_op jit(solution)/shard_map/ppermute | solution.py:292
  56.7 18.8 %collective-permute-start.14 = (bf16[8,136,128]{2,1,0:T(8,128)(2,1)S(1)}, bf16[8,136,128]{2,1,0:T(8,128)(2,1)S(1)}, u32[]{:S(2)}, u32[]{:S(2)}) collective-permute-start(bf16[8,136,128]{2,1,0:T(8,128)(2,1)S(1)} %constant_dynamic-update-slice_fusion.refs_3_), channel_id=1, source_target_pairs={{0,2},{1,3},{2,4},{3,5},{4,6},{5,7},{6,0},{7,1},{8,10},{9,11},{10,... | collective-permute-start | bytes 835592 | tf_op jit(solution)/shard_map/ppermute | solution.py:292
  57.7 13.6 %collective-permute-start.10 = (bf16[4,136,128]{2,1,0:T(8,128)(2,1)S(1)}, bf16[4,136,128]{2,1,0:T(8,128)(2,1)S(1)}, u32[]{:S(2)}, u32[]{:S(2)}) collective-permute-start(bf16[4,136,128]{2,1,0:T(8,128)(2,1)S(1)} %collective-permute-done.4), channel_id=1, source_target_pairs={{0,32},{1,97},{2,34},{3,99},{4,36},{5,101},{6,38},{7,103},{8,40},{... | collective-permute-start | bytes 417800 | tf_op jit(solution)/shard_map/ppermute | solution.py:295
  71.3 14.5 %copy-start.2 = (s32[64]{0:T(128)S(1)}, s32[64]{0:T(128)}, u32[]{:S(2)}) copy-start(s32[64]{0:T(128)} %param.10) | copy-start | bytes 772
  71.3 8.7 %collective-permute-start.13 = (bf16[4,136,128]{2,1,0:T(8,128)(2,1)S(1)}, bf16[4,136,128]{2,1,0:T(8,128)(2,1)S(1)}, u32[]{:S(2)}, u32[]{:S(2)}) collective-permute-start(bf16[4,136,128]{2,1,0:T(8,128)(2,1)S(1)} %collective-permute-done.10.refs_5_), channel_id=1, source_target_pairs={{0,6},{1,7},{2,0},{3,1},{4,2},{5,3},{6,4},{7,5},{8,14},{9,15},{10,... | collective-permute-start | bytes 417800 | tf_op jit(solution)/shard_map/ppermute | solution.py:292
  74.0 7.8 %collective-permute-start.12 = (bf16[4,136,128]{2,1,0:T(8,128)(2,1)S(1)}, bf16[4,136,128]{2,1,0:T(8,128)(2,1)S(1)}, u32[]{:S(2)}, u32[]{:S(2)}) collective-permute-start(bf16[4,136,128]{2,1,0:T(8,128)(2,1)S(1)} %collective-permute-done.10.refs_5_), channel_id=1, source_target_pairs={{0,2},{1,3},{2,4},{3,5},{4,6},{5,7},{6,0},{7,1},{8,10},{9,11},{10,... | collective-permute-start | bytes 417800 | tf_op jit(solution)/shard_map/ppermute | solution.py:292
  74.0 7.8 %collective-permute-start.11 = (bf16[4,136,128]{2,1,0:T(8,128)(2,1)S(1)}, bf16[4,136,128]{2,1,0:T(8,128)(2,1)S(1)}, u32[]{:S(2)}, u32[]{:S(2)}) collective-permute-start(bf16[4,136,128]{2,1,0:T(8,128)(2,1)S(1)} %collective-permute-done.10.refs_5_), channel_id=1, source_target_pairs={{0,4},{1,5},{2,6},{3,7},{4,0},{5,1},{6,2},{7,3},{8,12},{9,13},{10,... | collective-permute-start | bytes 417800 | tf_op jit(solution)/shard_map/ppermute | solution.py:292
  85.8 2.9 %collective-permute-start.16 = (f32[4,256,256]{2,1,0:T(8,128)}, f32[4,256,256]{2,1,0:T(8,128)S(1)}, u32[]{:S(2)}, u32[]{:S(2)}) collective-permute-start(f32[4,256,256]{2,1,0:T(8,128)} %get-tuple-element.55), channel_id=1, source_target_pairs={{0,1},{1,0},{2,3},{3,2},{4,5},{5,4},{6,7},{7,6},{8,9},{9,8},{10,11... | collective-permute-start | bytes 3145736 | tf_op jit(solution)/shard_map/ppermute | solution.py:292
  89.1 12.1 %collective-permute-start.19 = (bf16[4,64,128]{2,1,0:T(8,128)(2,1)S(1)}, bf16[4,64,128]{2,1,0:T(8,128)(2,1)S(1)}, u32[]{:S(2)}, u32[]{:S(2)}) collective-permute-start(bf16[4,64,128]{2,1,0:T(8,128)(2,1)S(1)} %get-tuple-element.61), channel_id=1, source_target_pairs={{0,8},{1,9},{2,10},{3,11},{4,12},{5,13},{6,14},{7,15},{8,16},{9,17... | collective-permute-start | bytes 196616 | tf_op jit(solution)/shard_map/ppermute | solution.py:300
  92.0 9.2 %collective-permute-start.18 = (bf16[4,64,128]{2,1,0:T(8,128)(2,1)S(1)}, bf16[4,64,128]{2,1,0:T(8,128)(2,1)S(1)}, u32[]{:S(2)}, u32[]{:S(2)}) collective-permute-start(bf16[4,64,128]{2,1,0:T(8,128)(2,1)S(1)} %get-tuple-element.62), channel_id=1, source_target_pairs={{0,16},{1,17},{2,18},{3,19},{4,20},{5,21},{6,22},{7,23},{8,24},{9,... | collective-permute-start | bytes 196616 | tf_op jit(solution)/shard_map/ppermute | solution.py:300
  94.4 6.8 %collective-permute-start.17 = (bf16[4,64,128]{2,1,0:T(8,128)(2,1)S(1)}, bf16[4,64,128]{2,1,0:T(8,128)(2,1)S(1)}, u32[]{:S(2)}, u32[]{:S(2)}) collective-permute-start(bf16[4,64,128]{2,1,0:T(8,128)(2,1)S(1)} %get-tuple-element.63), channel_id=1, source_target_pairs={{0,24},{1,25},{2,26},{3,27},{4,28},{5,29},{6,30},{7,31},{8,0},{9,1... | collective-permute-start | bytes 196616 | tf_op jit(solution)/shard_map/ppermute | solution.py:300
  97.2 3.4 %copy-start = (bf16[2048,2048]{1,0:T(8,128)(2,1)S(1)}, bf16[2048,2048]{1,0:T(8,128)(2,1)}, u32[]{:S(2)}) copy-start(bf16[2048,2048]{1,0:T(8,128)(2,1)} %weight_ref) | copy-start | bytes 25165828
  100.6 0.9 copy-start.1

commit v2 on v1

--- a/solution.py
+++ b/solution.py
@@ -19,8 +19,11 @@
 HALF = 32
 KV_ROWS = 2 * TOK + 8
 ALL_ROWS = (2 + GROUP) * TOK + 8
-ROWS = 256
+TOGETHER = 4
+ROWS = TOGETHER * GROUP * HALF
+PAIRS = KV_HEADS // TOGETHER
 SCALE = HEAD_DIM ** -0.5 * math.log2(math.e)
+PART = 32
 NEVER = -1e30
 LOWEST = -1e20
 VMEM = pltpu.VMEM
@@ -75,10 +78,14 @@
         out_ref[h, (2 + GROUP) * TOK:ALL_ROWS, :] = table
 
 
+def in_hbm(a):
+    return pltpu.with_memory_space_constraint(a, pltpu.HBM)
+
+
 def prep(positions, query_rows, key_rows, value_rows):
     return pl.pallas_call(
         prep_kernel,
-        out_shape=jax.ShapeDtypeStruct((KV_HEADS, ALL_ROWS, HEAD_DIM), BF16),
+        out_shape=VMEM((KV_HEADS, ALL_ROWS, HEAD_DIM), BF16),
         in_specs=[pl.BlockSpec(memory_space=pltpu.HBM)] * 4,
         out_specs=pl.BlockSpec(memory_space=VMEM),
         scratch_shapes=[
@@ -88,10 +95,10 @@
             VMEM(value_rows.shape, BF16),
             pltpu.SemaphoreType.DMA((4,)),
         ],
-        compiler_params=pltpu.CompilerParams(vmem_limit_bytes=60 * 1024 * 1024),
+        compiler_params=pltpu.CompilerParams(vmem_limit_bytes=8 * 1024 * 1024),
         cost_estimate=pl.CostEstimate(flops=TOK * TOK * 3072 * 2, bytes_accessed=800_000, transcendentals=0),
         name="prep",
-    )(positions.reshape(1, TOK), query_rows, key_rows, value_rows)
+    )(*(in_hbm(a) for a in (positions.reshape(1, TOK), query_rows, key_rows, value_rows)))
 
 
 def attend_kernel(parts, first, last, *refs):
@@ -137,11 +144,11 @@
     )
     for half, q_ref in enumerate((qa_ref, qb_ref)):
         for i in range(2):
-            for sp in range(2):
-                b = i * 2 + sp
+            for sp in range(PAIRS):
+                b = i * PAIRS + sp
                 q_rows = []
                 q_poss = []
-                for src in (2 * sp, 2 * sp + 1):
+                for src in range(TOGETHER * sp, TOGETHER * (sp + 1)):
                     for g in range(GROUP):
                         at = (2 + g) * TOK + HALF * i
                         q_rows.append(q_ref[src, at:at + HALF, :])
@@ -171,8 +178,13 @@
                     sums = sums + old_refs[2 * half + 1][b] * jnp.concatenate([rescale, rescale], axis=1)
                 if last and half == 1:
                     lane = iota((ROWS, HEAD_DIM), 1)
-                    new_refs[2][b, :, 0:HEAD_DIM] = sums[:, 0:HEAD_DIM]
-                    new_refs[2][b, :, HEAD_DIM:] = jnp.where(lane < HEAD_DIM // 2, new_max, sums[:, HEAD_DIM:])
+                    total = jnp.maximum(sums[:, HEAD_DIM:], 1e-30)
+                    level = new_max + jnp.log2(total)
+                    high = level.astype(BF16).astype(F32)
+                    middle = (level - high).astype(BF16).astype(F32)
+                    parts3 = jnp.where(lane < PART, high, jnp.where(lane < 2 * PART, middle, level - high - middle))
+                    new_refs[2][b, :, 0:HEAD_DIM] = (sums[:, 0:HEAD_DIM] / total).astype(BF16)
+                    new_refs[2][b, :, HEAD_DIM:] = parts3.astype(BF16)
                 else:
                     new_refs[2 * half][b] = new_max
                     new_refs[2 * half + 1][b] = sums
@@ -181,12 +193,12 @@
 def attend(limit, qa, qb, parts, state, last=False):
     shards = sum(part.shape[0] for part in parts) // KV_HEADS
     wide = shards * HEAD_DIM
-    stats = jax.ShapeDtypeStruct((4, ROWS, HEAD_DIM), F32)
-    sums = jax.ShapeDtypeStruct((4, ROWS, 2 * HEAD_DIM), F32)
-    shapes = (stats, sums, sums) if last else (stats, sums, stats, sums)
+    stats = jax.ShapeDtypeStruct((2 * PAIRS, ROWS, HEAD_DIM), F32)
+    sums = jax.ShapeDtypeStruct((2 * PAIRS, ROWS, 2 * HEAD_DIM), F32)
+    shapes = (stats, sums, VMEM(sums.shape, BF16)) if last else (stats, sums, stats, sums)
     first = state is None
     held = [] if first else list(state)
-    score_count = 4 * 2 * ROWS * 3 * wide
+    score_count = 4 * 2 * 256 * 3 * wide
     base = 3 + len(parts)
     return pl.pallas_call(
         functools.partial(attend_kernel, len(parts), first, last),
@@ -212,30 +224,31 @@
 def hold(weight):
     return pl.pallas_call(
         hold_kernel,
-        out_shape=jax.ShapeDtypeStruct(weight.shape, weight.dtype),
-        in_specs=[pl.BlockSpec(memory_space=pl.ANY)],
+        out_shape=VMEM(weight.shape, weight.dtype),
+        in_specs=[pl.BlockSpec(memory_space=pltpu.HBM)],
         out_specs=pl.BlockSpec(memory_space=VMEM),
         scratch_shapes=[pltpu.SemaphoreType.DMA],
         compiler_params=pltpu.CompilerParams(vmem_limit_bytes=10 * 1024 * 1024),
         cost_estimate=pl.CostEstimate(flops=2_000_000_000, bytes_accessed=8_000_000, transcendentals=0),
         name="hold",
-    )(weight)
+    )(in_hbm(weight))
 
 
 def merge_kernel(max_ref, sum_ref, got_ref, out_ref):
     for i in range(2):
-        for sp in range(2):
-            b = i * 2 + sp
+        for sp in range(PAIRS):
+            b = i * PAIRS + sp
             max_a = max_ref[b]
-            max_b = jnp.broadcast_to(got_ref[b, :, HEAD_DIM:HEAD_DIM + 1], (ROWS, HEAD_DIM))
-            total_b = jnp.broadcast_to(got_ref[b, :, 2 * HEAD_DIM - 1:], (ROWS, HEAD_DIM))
+            level = got_ref[b, :, HEAD_DIM:].astype(F32)
+            level = level[:, 0:1] + level[:, PART:PART + 1] + level[:, 2 * PART:2 * PART + 1]
+            max_b = jnp.broadcast_to(level, (ROWS, HEAD_DIM))
             top = jnp.maximum(max_a, max_b)
             part_a = jnp.exp2(max_a - top)
             part_b = jnp.exp2(max_b - top)
-            total = sum_ref[b, :, HEAD_DIM:] * part_a + total_b * part_b
-            value = sum_ref[b, :, 0:HEAD_DIM] * part_a + got_ref[b, :, 0:HEAD_DIM] * part_b
-            value = (value / total).astype(BF16).reshape(2, GROUP, HALF, HEAD_DIM)
-            out_ref[2 * sp:2 * sp + 2, :, HALF * i:HALF * (i + 1), :] = value
+            total = sum_ref[b, :, HEAD_DIM:] * part_a + part_b
+            value = sum_ref[b, :, 0:HEAD_DIM] * part_a + got_ref[b, :, 0:HEAD_DIM].astype(F32) * part_b
+            value = (value / total).astype(BF16).reshape(TOGETHER, GROUP, HALF, HEAD_DIM)
+            out_ref[TOGETHER * sp:TOGETHER * (sp + 1), :, HALF * i:HALF * (i + 1), :] = value
 
 
 def merge(maxima, sums, got):
@@ -302,7 +315,7 @@
         )
 
     def spread(a):
-        return [move(a, dx=2), move(a, dx=1), move(a, dx=-1)]
+        return [move(a, dx=1), move(a, dx=-1), move(a, dx=2)]
 
     member = lax.rem(lax.axis_index("seq") // (X_DEV * CORES), BLOCK)
     message = prep(positions, query_rows, key_rows, value_rows)
@@ -316,17 +329,15 @@
     mine = kv_of(own)
     one = far(mine)
     other = far(kv_of(twin))
-    group = [mine] + spread(mine)
+    own_group = [mine] + spread(mine)
     two = far(one)
-    state = attend(prompt_length, own, twin, group, None)
-    state, other = lax.optimization_barrier((state, other))
-    one = jnp.concatenate([one, other], axis=0)
-    group = [one] + spread(one)
-    state = attend(prompt_length, own, twin, group[:2], state)
-    state, two = lax.optimization_barrier((state, two))
-    last_group = spread(two)
-    state = attend(prompt_length, own, twin, group[2:] + [two], state)
-    state = attend(prompt_length, own, twin, last_group, state, last=True)
+    one_group = [one] + spread(one)
+    other_group = [other] + spread(other)
+    two_group = [two] + spread(two)
+    state = attend(prompt_length, own, twin, own_group, None)
+    state = attend(prompt_length, own, twin, one_group, state)
+    state = attend(prompt_length, own, twin, other_group, state)
+    state = attend(prompt_length, own, twin, two_group, state, last=True)
     got = move(state[2], dc=1)
     done = merge(state[0], state[1], got)
     parts = [done[0]] + [turn(done[d], -d) for d in range(1, BLOCK)]

time: 104 us -> 101 us (0.971)
  local copies, waits for them, and re-layouts: 4.98 us -> 0.19 us
    unnamed x7 -> x4, local copies, waits for them, and re-layouts: 3.74 us -> 0.01 us
    ppermute x11 -> x14, starting transfers between devices: 15.1 us -> 17.9 us  [move(): lax.ppermute(a, 'seq', [(at(z, x, c), at(z + dz, x + dx, c + dc)) for z,...]
    pallas_call x2, Pallas kernels: 2.71 us -> 4.78 us  [the longest x1 3.39 us: hold(): pl.pallas_call(hold_kernel, out_shape=VMEM(weight.shape, weight.dtype), i...]
    ppermute x11 -> x14, waiting for transfers between devices: 4.82 us -> 6.8 us  [move(): lax.ppermute(a, 'seq', [(at(z, x, c), at(z + dz, x + dx, c + dc)) for z,...]
    pallas_call x4, Pallas kernels: 15.1 us -> 13.2 us  [attend(): pl.pallas_call(functools.partial(attend_kernel, len(parts), first, last),...]
    ppermute x3, starting transfers between devices: 18.4 us -> 16.9 us  [far(): lax.ppermute(a, 'seq', [(at(z, x, c), at(z + (BLOCK if c == 0 else -BLOCK...]
    ppermute x3, waiting for transfers between devices: 14.6 us -> 13.2 us  [far(): lax.ppermute(a, 'seq', [(at(z, x, c), at(z + (BLOCK if c == 0 else -BLOCK...]
  transfers between devices with their start and end apart: 20 -> 23, of which waited for: 8 -> 9; matrix products, arithmetic and copies ran while one was open for 0% -> 0% of each run, Pallas kernels for 11% -> 13%
where the time goes in v2:
time: 101 us
  starting transfers between devices  50.3 us (50%)
  waiting for transfers between devices  28.3 us (28%)
  Pallas kernels  20.9 us (21%)
    ppermute x14, starting transfers between devices, move(): lax.ppermute(a, 'seq', [(at(z, x, c), at(z + dz, x + dx, c + dc)) for z,...  17.9 us
    ppermute x3, starting transfers between devices, far(): lax.ppermute(a, 'seq', [(at(z, x, c), at(z + (BLOCK if c == 0 else -BLOCK...  16.9 us
    ppermute x6, starting transfers between devices, turn(): lax.ppermute(a, 'seq', [(at(z, x, c), at(z // BLOCK * BLOCK + (z + d) % B...  15.6 us
    pallas_call x4, Pallas kernels, attend(): pl.pallas_call(functools.partial(attend_kernel, len(parts), first, last),...  13.2 us
    ppermute x3, waiting for transfers between devices, far(): lax.ppermute(a, 'seq', [(at(z, x, c), at(z + (BLOCK if c == 0 else -BLOCK...  13.2 us
    ppermute x6, waiting for transfers between devices, turn(): lax.ppermute(a, 'seq', [(at(z, x, c), at(z // BLOCK * BLOCK + (z + d) % B...  8.37 us
    ppermute x14, waiting for transfers between devices, move(): lax.ppermute(a, 'seq', [(at(z, x, c), at(z + dz, x + dx, c + dc)) for z,...  6.8 us
    pallas_call x1, Pallas kernels, hold(): pl.pallas_call(hold_kernel, out_shape=VMEM(weight.shape, weight.dtype), i...  3.39 us
  transfers between devices with their start and end apart: 23, of which 9 were waited for; matrix products, arithmetic and copies ran while one was open for 0% of the time, Pallas kernels for 13%

profile of v2, /device:TPU:40, one launch (start us, length us, event | category | flops | bytes accessed | tf_op | source)
XLA Modules:
  0.0 100.7 jit_solution(9027973481415238065)
XLA Ops:
  0.0 1.4 %prep.1 = bf16[4,392,128]{2,1,0:T(8,128)(2,1)S(1)} custom-call(s32[1,64]{1,0:T(1,128)} %bitcast.23, bf16[64,2048]{1,0:T(8,128)(2,1)} %q_hbm.1, bf16[64,512]{1,0:T(8,128)(2,1)} %k_hbm.1, bf16[64,512]{1,0:T(8,128)(2,1)} %v_hbm.1), custom_call_target="tpu_custom_call" | custom-call | flops 25165824 | bytes 800000 | tf_op jit(solution)/shard_map/prep/pallas_call | solution.py:86
  1.4 7.3 %collective-permute-start.2 = (bf16[392,128]{1,0:T(8,128)(2,1)S(1)}, bf16[392,128]{1,0:T(8,128)(2,1)S(1)}, u32[]{:S(2)}, u32[]{:S(2)}) collective-permute-start(bf16[392,128]{1,0:T(8,128)(2,1)S(1)} %get-tuple-element.38), channel_id=1, source_target_pairs={{0,24},{1,25},{2,26},{3,27},{4,28},{5,29},{6,30},{7,31},{8,0},{9,1... | collective-permute-start | bytes 301064 | tf_op jit(solution)/shard_map/ppermute | solution.py:313
  8.8 0.7 collective-permute-start
  9.5 2.5 %collective-permute-done.2 = bf16[392,128]{1,0:T(8,128)(2,1)S(1)} collective-permute-done((bf16[392,128]{1,0:T(8,128)(2,1)S(1)}, bf16[392,128]{1,0:T(8,128)(2,1)S(1)}, u32[]{:S(2)}, u32[]{:S(2)}) %collective-permute-start.2) | collective-permute-done | bytes 100384 | tf_op jit(solution)/shard_map/ppermute | solution.py:313
  12.0 5.8 %collective-permute-done.1 = bf16[392,128]{1,0:T(8,128)(2,1)S(1)} collective-permute-done((bf16[392,128]{1,0:T(8,128)(2,1)S(1)}, bf16[392,128]{1,0:T(8,128)(2,1)S(1)}, u32[]{:S(2)}, u32[]{:S(2)}) %collective-permute-start.1) | collective-permute-done | bytes 100384 | tf_op jit(solution)/shard_map/ppermute | solution.py:313
  17.8 0.0 collective-permute-done
  17.8 0.1 pad_maximum_fusion.refs_1_
  17.9 0.1 collective-permute-start.3
  18.1 10.7 %collective-permute-start.4 = (bf16[4,136,128]{2,1,0:T(8,128)(2,1)S(1)}, bf16[4,136,128]{2,1,0:T(8,128)(2,1)S(1)}, u32[]{:S(2)}, u32[]{:S(2)}) collective-permute-start(bf16[4,136,128]{2,1,0:T(8,128)(2,1)S(1)} %pad_maximum_fusion.1.refs_3_), channel_id=1, source_target_pairs={{0,32},{1,97},{2,34},{3,99},{4,36},{5,101},{6,38},{7,103},{8,40},{... | collective-permute-start | bytes 417800 | tf_op jit(solution)/shard_map/ppermute | solution.py:308
  28.8 3.3 %collective-permute-start.18 = (bf16[4,136,128]{2,1,0:T(8,128)(2,1)S(1)}, bf16[4,136,128]{2,1,0:T(8,128)(2,1)S(1)}, u32[]{:S(2)}, u32[]{:S(2)}) collective-permute-start(bf16[4,136,128]{2,1,0:T(8,128)(2,1)S(1)} %pad_maximum_fusion.1.refs_3_), channel_id=1, source_target_pairs={{0,4},{1,5},{2,6},{3,7},{4,0},{5,1},{6,2},{7,3},{8,12},{9,13},{10,... | collective-permute-start | bytes 417800 | tf_op jit(solution)/shard_map/ppermute | solution.py:305
  32.1 1.0 %collective-permute-start.17 = (bf16[4,136,128]{2,1,0:T(8,128)(2,1)S(1)}, bf16[4,136,128]{2,1,0:T(8,128)(2,1)S(1)}, u32[]{:S(2)}, u32[]{:S(2)}) collective-permute-start(bf16[4,136,128]{2,1,0:T(8,128)(2,1)S(1)} %pad_maximum_fusion.1.refs_3_), channel_id=1, source_target_pairs={{0,6},{1,7},{2,0},{3,1},{4,2},{5,3},{6,4},{7,5},{8,14},{9,15},{10,... | collective-permute-start | bytes 417800 | tf_op jit(solution)/shard_map/ppermute | solution.py:305
  33.1 6.8 %collective-permute-done.4.refs_3_ = bf16[4,136,128]{2,1,0:T(8,128)(2,1)S(1)} collective-permute-done((bf16[4,136,128]{2,1,0:T(8,128)(2,1)S(1)}, bf16[4,136,128]{2,1,0:T(8,128)(2,1)S(1)}, u32[]{:S(2)}, u32[]{:S(2)}) %collective-permute-start.4) | collective-permute-done | bytes 139296 | tf_op jit(solution)/shard_map/ppermute | solution.py:308
  39.9 1.4 %collective-permute-start.5 = (bf16[4,136,128]{2,1,0:T(8,128)(2,1)S(1)}, bf16[4,136,128]{2,1,0:T(8,128)(2,1)S(1)}, u32[]{:S(2)}, u32[]{:S(2)}) collective-permute-start(bf16[4,136,128]{2,1,0:T(8,128)(2,1)S(1)} %collective-permute-done.4.refs_3_), channel_id=1, source_target_pairs={{0,32},{1,97},{2,34},{3,99},{4,36},{5,101},{6,38},{7,103},{8,40},{... | collective-permute-start | bytes 417800 | tf_op jit(solution)/shard_map/ppermute | solution.py:308
  41.3 1.6 %collective-permute-start.16 = (bf16[4,136,128]{2,1,0:T(8,128)(2,1)S(1)}, bf16[4,136,128]{2,1,0:T(8,128)(2,1)S(1)}, u32[]{:S(2)}, u32[]{:S(2)}) collective-permute-start(bf16[4,136,128]{2,1,0:T(8,128)(2,1)S(1)} %pad_maximum_fusion.1.refs_3_), channel_id=1, source_target_pairs={{0,2},{1,3},{2,4},{3,5},{4,6},{5,7},{6,0},{7,1},{8,10},{9,11},{10,... | collective-permute-start | bytes 417800 | tf_op jit(solution)/shard_map/ppermute | solution.py:305
  43.6 3.1 %collective-permute-start.15 = (bf16[4,136,128]{2,1,0:T(8,128)(2,1)S(1)}, bf16[4,136,128]{2,1,0:T(8,128)(2,1)S(1)}, u32[]{:S(2)}, u32[]{:S(2)}) collective-permute-start(bf16[4,136,128]{2,1,0:T(8,128)(2,1)S(1)} %collective-permute-done.4.refs_3_), channel_id=1, source_target_pairs={{0,4},{1,5},{2,6},{3,7},{4,0},{5,1},{6,2},{7,3},{8,12},{9,13},{10,... | collective-permute-start | bytes 417800 | tf_op jit(solution)/shard_map/ppermute | solution.py:305
  46.8 1.4 %collective-permute-start.14 = (bf16[4,136,128]{2,1,0:T(8,128)(2,1)S(1)}, bf16[4,136,128]{2,1,0:T(8,128)(2,1)S(1)}, u32[]{:S(2)}, u32[]{:S(2)}) collective-permute-start(bf16[4,136,128]{2,1,0:T(8,128)(2,1)S(1)} %collective-permute-done.4.refs_3_), channel_id=1, source_target_pairs={{0,6},{1,7},{2,0},{3,1},{4,2},{5,3},{6,4},{7,5},{8,14},{9,15},{10,... | collective-permute-start | bytes 417800 | tf_op jit(solution)/shard_map/ppermute | solution.py:305
  48.2 0.0 collective-permute-done.17.refs_5_
  48.2 0.7 collective-permute-start.13
  48.9 1.3 %collective-permute-done.5.refs_3_ = bf16[4,136,128]{2,1,0:T(8,128)(2,1)S(1)} collective-permute-done((bf16[4,136,128]{2,1,0:T(8,128)(2,1)S(1)}, bf16[4,136,128]{2,1,0:T(8,128)(2,1)S(1)}, u32[]{:S(2)}, u32[]{:S(2)}) %collective-permute-start.5) | collective-permute-done | bytes 139296 | tf_op jit(solution)/shard_map/ppermute | solution.py:308
  50.2 3.3 %collective-permute-start.8 = (bf16[4,136,128]{2,1,0:T(8,128)(2,1)S(1)}, bf16[4,136,128]{2,1,0:T(8,128)(2,1)S(1)}, u32[]{:S(2)}, u32[]{:S(2)}) collective-permute-start(bf16[4,136,128]{2,1,0:T(8,128)(2,1)S(1)} %collective-permute-done.5.refs_3_), channel_id=1, source_target_pairs={{0,4},{1,5},{2,6},{3,7},{4,0},{5,1},{6,2},{7,3},{8,12},{9,13},{10,... | collective-permute-start | bytes 417800 | tf_op jit(solution)/shard_map/ppermute | solution.py:305
  53.5 0.0 collective-permute-done.16.refs_4_
  53.5 4.7 %collective-permute-start.9 = (bf16[4,136,128]{2,1,0:T(8,128)(2,1)S(1)}, bf16[4,136,128]{2,1,0:T(8,128)(2,1)S(1)}, u32[]{:S(2)}, u32[]{:S(2)}) collective-permute-start(bf16[4,136,128]{2,1,0:T(8,128)(2,1)S(1)} %pad_maximum_fusion.2), channel_id=1, source_target_pairs={{0,32},{1,97},{2,34},{3,99},{4,36},{5,101},{6,38},{7,103},{8,40},{... | collective-permute-start | bytes 417800 | tf_op jit(solution)/shard_map/ppermute | solution.py:308
  58.2 2.7 %attend.3 = (f32[2,512,128]{2,1,0:T(8,128)S(1)}, f32[2,512,256]{2,1,0:T(8,128)S(1)}, f32[2,512,128]{2,1,0:T(8,128)S(1)}, f32[2,512,256]{2,1,0:T(8,128)S(1)}) custom-call(s32[1]{0:T(128)S(6)} %copy.29.refs_0_, bf16[4,392,128]{2,1,0:T(8,128)(2,1)S(1)} %pad_maximum_fusion.refs_1_, bf16[4,392,128]{2,1,0:T(8,128)(2,1)S(1)} %collective-permute-done.3.refs_2_, ...), custom_call_target="tpu_custom_call" | custom-call | flops 2415919104 | bytes 4000000 | tf_op jit(solution)/shard_map/attend/pallas_call | solution.py:203
  61.0 1.1 %collective-permute-start.7 = (bf16[4,136,128]{2,1,0:T(8,128)(2,1)S(1)}, bf16[4,136,128]{2,1,0:T(8,128)(2,1)S(1)}, u32[]{:S(2)}, u32[]{:S(2)}) collective-permute-start(bf16[4,136,128]{2,1,0:T(8,128)(2,1)S(1)} %collective-permute-done.5.refs_3_), channel_id=1, source_target_pairs={{0,6},{1,7},{2,0},{3,1},{4,2},{5,3},{6,4},{7,5},{8,14},{9,15},{10,... | collective-permute-start | bytes 417800 | tf_op jit(solution)/shard_map/ppermute | solution.py:305
  62.1 5.1 %collective-permute-done.9.refs_3_ = bf16[4,136,128]{2,1,0:T(8,128)(2,1)S(1)} collective-permute-done((bf16[4,136,128]{2,1,0:T(8,128)(2,1)S(1)}, bf16[4,136,128]{2,1,0:T(8,128)(2,1)S(1)}, u32[]{:S(2)}, u32[]{:S(2)}) %collective-permute-start.9) | collective-permute-done | bytes 139296 | tf_op jit(solution)/shard_map/ppermute | solution.py:308
  67.2 0.0 collective-permute-start.12
  67.2 0.0 collective-permute-done.14.refs_5_
  67.2 1.9 %collective-permute-start.11 = (bf16[4,136,128]{2,1,0:T(8,128)(2,1)S(1)}, bf16[4,136,128]{2,1,0:T(8,128)(2,1)S(1)}, u32[]{:S(2)}, u32[]{:S(2)}) collective-permute-start(bf16[4,136,128]{2,1,0:T(8,128)(2,1)S(1)} %collective-permute-done.9.refs_3_), channel_id=1, source_target_pairs={{0,6},{1,7},{2,0},{3,1},{4,2},{5,3},{6,4},{7,5},{8,14},{9,15},{10,... | collective-permute-start | bytes 417800 | tf_op jit(solution)/shard_map/ppermute | solution.py:305
  69.1 0.1 collective-permute-start.10
  69.2 3.6 %attend.4 = (f32[2,512,128]{2,1,0:T(8,128)S(1)}, f32[2,512,256]{2,1,0:T(8,128)S(1)}, f32[2,512,128]{2,1,0:T(8,128)S(1)}, f32[2,512,256]{2,1,0:T(8,128)S(1)}) custom-call(s32[1]{0:T(128)S(6)} %copy.29.refs_0_, bf16[4,392,128]{2,1,0:T(8,128)(2,1)S(1)} %pad_maximum_fusion.refs_1_, ...), custom_call_target="tpu_custom_call", output_to_operand_aliasing={{0}: (7, {}), {1}: (8, {}), {2}: (9, {}), {3}: (10, {})} | custom-call | flops 2415919104 | bytes 4000000 | tf_op jit(solution)/shard_map/attend/pallas_call | solution.py:203
  72.8 2.4 %collective-permute-done.12.refs_6_ = bf16[4,136,128]{2,1,0:T(8,128)(2,1)S(1)} collective-permute-done((bf16[4,136,128]{2,1,0:T(8,128)(2,1)S(1)}, bf16[4,136,128]{2,1,0:T(8,128)(2,1)S(1)}, u32[]{:S(2)}, u32[]{:S(2)}) %collective-permute-start.12) | collective-permute-done | bytes 139296 | tf_op jit(solution)/shard_map/ppermute | solution.py:305
  75.2 0.0 collective-permute-start.6
  75.2 0.0 collective-permute-done.11.refs_5_
  75.2 2.1 %collective-permute-done.10.refs_4_ = bf16[4,136,128]{2,1,0:T(8,128)(2,1)S(1)} collective-permute-done((bf16[4,136,128]{2,1,0:T(8,128)(2,1)S(1)}, bf16[4,136,128]{2,1,0:T(8,128)(2,1)S(1)}, u32[]{:S(2)}, u32[]{:S(2)}) %collective-permute-start.10) | collective-permute-done | bytes 139296 | tf_op jit(solution)/shard_map/ppermute | solution.py:305
  77.4 3.6 %attend.5 = (f32[2,512,128]{2,1,0:T(8,128)S(1)}, f32[2,512,256]{2,1,0:T(8,128)S(1)}, f32[2,512,128]{2,1,0:T(8,128)S(1)}, f32[2,512,256]{2,1,0:T(8,128)S(1)}) custom-call(s32[1]{0:T(128)S(6)} %copy.29.refs_0_, bf16[4,392,128]{2,1,0:T(8,128)(2,1)S(1)} %pad_maximum_fusion.refs_1_, ...), custom_call_target="tpu_custom_call", output_to_operand_aliasing={{0}: (7, {}), {1}: (8, {}), {2}: (9, {}), {3}: (10, {})} | custom-call | flops 2415919104 | bytes 4000000 | tf_op jit(solution)/shard_map/attend/pallas_call | solution.py:203
  81.0 0.0 collective-permute-done.8.refs_6_
  81.0 0.0 collective-permute-done.7.refs_5_
  81.0 0.5 collective-permute-done.6.refs_4_
  81.5 3.2 %attend_last.1 = (f32[2,512,128]{2,1,0:T(8,128)S(1)}, f32[2,512,256]{2,1,0:T(8,128)S(1)}, bf16[2,512,256]{2,1,0:T(8,128)(2,1)S(1)}) custom-call(s32[1]{0:T(128)S(6)} %copy.29.refs_0_, bf16[4,392,128]{2,1,0:T(8,128)(2,1)S(1)} %pad_maximum_fusion.refs_1_, ...), custom_call_target="tpu_custom_call", output_to_operand_aliasing={{0}: (7, {}), {1}: (8, {})} | custom-call | flops 2415919104 | bytes 4000000 | tf_op jit(solution)/shard_map/attend_last/pallas_call | solution.py:203
  84.7 0.1 collective-permute-start.19
  84.9 0.1 copy.18.pos_ref
  85.0 1.8 %collective-permute-done.19.got_ref = bf16[2,512,256]{2,1,0:T(8,128)(2,1)S(1)} collective-permute-done((bf16[2,512,256]{2,1,0:T(8,128)(2,1)S(1)}, bf16[2,512,256]{2,1,0:T(8,128)(2,1)S(1)}, u32[]{:S(2)}, u32[]{:S(2)}) %collective-permute-start.19) | collective-permute-done | bytes 524320 | tf_op jit(solution)/shard_map/ppermute | solution.py:305
  86.7 0.5 merge.1
  87.3 2.3 %collective-permute-start.22 = (bf16[4,64,128]{2,1,0:T(8,128)(2,1)S(1)}, bf16[4,64,128]{2,1,0:T(8,128)(2,1)S(1)}, u32[]{:S(2)}, u32[]{:S(2)}) collective-permute-start(bf16[4,64,128]{2,1,0:T(8,128)(2,1)S(1)} %get-tuple-element.41), channel_id=1, source_target_pairs={{0,8},{1,9},{2,10},{3,11},{4,12},{5,13},{6,14},{7,15},{8,16},{9,17... | collective-permute-start | bytes 196616 | tf_op jit(solution)/shard_map/ppermute | solution.py:313
  89.6 2.4 %collective-permute-start.21 = (bf16[4,64,128]{2,1,0:T(8,128)(2,1)S(1)}, bf16[4,64,128]{2,1,0:T(8,128)(2,1)S(1)}, u32[]{:S(2)}, u32[]{:S(2)}) collective-permute-start(bf16[4,64,128]{2,1,0:T(8,128)(2,1)S(1)} %get-tuple-element.42), channel_id=1, source_target_pairs={{0,16},{1,17},{2,18},{3,19},{4,20},{5,21},{6,22},{7,23},{8,24},{9,... | collective-permute-start | bytes 196616 | tf_op jit(solution)/shard_map/ppermute | solution.py:313
  92.0 2.8 %collective-permute-start.20 = (bf16[4,64,128]{2,1,0:T(8,128)(2,1)S(1)}, bf16[4,64,128]{2,1,0:T(8,128)(2,1)S(1)}, u32[]{:S(2)}, u32[]{:S(2)}) collective-permute-start(bf16[4,64,128]{2,1,0:T(8,128)(2,1)S(1)} %get-tuple-element.43), channel_id=1, source_target_pairs={{0,24},{1,25},{2,26},{3,27},{4,28},{5,29},{6,30},{7,31},{8,0},{9,1... | collective-permute-start | bytes 196616 | tf_op jit(solution)/shard_map/ppermute | solution.py:313
  94.8 3.4 %hold.1.refs_4_ = bf16[2048,2048]{1,0:T(8,128)(2,1)S(1)} custom-call(bf16[2048,2048]{1,0:T(8,128)(2,1)} %weight_ref), custom_call_target="tpu_custom_call" | custom-call | flops 2000000000 | bytes 8000000 | tf_op jit(solution)/shard_map/hold/pallas_call | solution.py:225
  98.2 2.5 %project.1 = bf16[64,2048]{1,0:T(8,128)(2,1)} custom-call(s32[1]{0:T(128)} %bitcast.member_ref, s32[64,1]{1,0:T(8,128)S(1)} %copy.18.pos_ref, bf16[4,64,128]{2,1,0:T(8,128)(2,1)S(1)} %get-tuple-element.44.refs_0_, bf16[4,64,128]{2,1,0:T(8,128)(2,1)S(1)} %collective-permute-done.20.refs_1_, bf16[4,64,128]{2,1,0:T(8,128)(2,1)S(1)} %collective-permute-done.21.refs_2_, ...), custom_call_target="tpu_custom_call" | custom-call | flops 536870912 | bytes 9000000 | tf_op jit(solution)/shard_map/project/pallas_call | solution.py:284
  (20 shorter events, 0.1 us)
Async XLA Ops:
  1.4 10.5 %collective-permute-start.2 = (bf16[392,128]{1,0:T(8,128)(2,1)S(1)}, bf16[392,128]{1,0:T(8,128)(2,1)S(1)}, u32[]{:S(2)}, u32[]{:S(2)}) collective-permute-start(bf16[392,128]{1,0:T(8,128)(2,1)S(1)} %get-tuple-element.38), channel_id=1, source_target_pairs={{0,24},{1,25},{2,26},{3,27},{4,28},{5,29},{6,30},{7,31},{8,0},{9,1... | collective-permute-start | bytes 301064 | tf_op jit(solution)/shard_map/ppermute | solution.py:313
  8.8 9.1 %collective-permute-start.1 = (bf16[392,128]{1,0:T(8,128)(2,1)S(1)}, bf16[392,128]{1,0:T(8,128)(2,1)S(1)}, u32[]{:S(2)}, u32[]{:S(2)}) collective-permute-start(bf16[392,128]{1,0:T(8,128)(2,1)S(1)} %get-tuple-element.39), channel_id=1, source_target_pairs={{0,16},{1,17},{2,18},{3,19},{4,20},{5,21},{6,22},{7,23},{8,24},{9,... | collective-permute-start | bytes 301064 | tf_op jit(solution)/shard_map/ppermute | solution.py:313
  8.8 9.1 %collective-permute-start = (bf16[392,128]{1,0:T(8,128)(2,1)S(1)}, bf16[392,128]{1,0:T(8,128)(2,1)S(1)}, u32[]{:S(2)}, u32[]{:S(2)}) collective-permute-start(bf16[392,128]{1,0:T(8,128)(2,1)S(1)} %get-tuple-element.40), channel_id=1, source_target_pairs={{0,8},{1,9},{2,10},{3,11},{4,12},{5,13},{6,14},{7,15},{8,16},{9,17... | collective-permute-start | bytes 301064 | tf_op jit(solution)/shard_map/ppermute | solution.py:313
  17.9 25.7 %collective-permute-start.3 = (bf16[4,392,128]{2,1,0:T(8,128)(2,1)S(1)}, bf16[4,392,128]{2,1,0:T(8,128)(2,1)S(1)}, u32[]{:S(2)}, u32[]{:S(2)}) collective-permute-start(bf16[4,392,128]{2,1,0:T(8,128)(2,1)S(1)} %pad_maximum_fusion.refs_1_), channel_id=1, source_target_pairs={{0,1},{1,0},{2,3},{3,2},{4,5},{5,4},{6,7},{7,6},{8,9},{9,8},{10,11... | collective-permute-start | bytes 1204232 | tf_op jit(solution)/shard_map/ppermute | solution.py:305
  18.1 21.8 %collective-permute-start.4 = (bf16[4,136,128]{2,1,0:T(8,128)(2,1)S(1)}, bf16[4,136,128]{2,1,0:T(8,128)(2,1)S(1)}, u32[]{:S(2)}, u32[]{:S(2)}) collective-permute-start(bf16[4,136,128]{2,1,0:T(8,128)(2,1)S(1)} %pad_maximum_fusion.1.refs_3_), channel_id=1, source_target_pairs={{0,32},{1,97},{2,34},{3,99},{4,36},{5,101},{6,38},{7,103},{8,40},{... | collective-permute-start | bytes 417800 | tf_op jit(solution)/shard_map/ppermute | solution.py:308
  28.8 18.0 %collective-permute-start.18 = (bf16[4,136,128]{2,1,0:T(8,128)(2,1)S(1)}, bf16[4,136,128]{2,1,0:T(8,128)(2,1)S(1)}, u32[]{:S(2)}, u32[]{:S(2)}) collective-permute-start(bf16[4,136,128]{2,1,0:T(8,128)(2,1)S(1)} %pad_maximum_fusion.1.refs_3_), channel_id=1, source_target_pairs={{0,4},{1,5},{2,6},{3,7},{4,0},{5,1},{6,2},{7,3},{8,12},{9,13},{10,... | collective-permute-start | bytes 417800 | tf_op jit(solution)/shard_map/ppermute | solution.py:305
  32.1 16.1 %collective-permute-start.17 = (bf16[4,136,128]{2,1,0:T(8,128)(2,1)S(1)}, bf16[4,136,128]{2,1,0:T(8,128)(2,1)S(1)}, u32[]{:S(2)}, u32[]{:S(2)}) collective-permute-start(bf16[4,136,128]{2,1,0:T(8,128)(2,1)S(1)} %pad_maximum_fusion.1.refs_3_), channel_id=1, source_target_pairs={{0,6},{1,7},{2,0},{3,1},{4,2},{5,3},{6,4},{7,5},{8,14},{9,15},{10,... | collective-permute-start | bytes 417800 | tf_op jit(solution)/shard_map/ppermute | solution.py:305
  39.9 10.3 %collective-permute-start.5 = (bf16[4,136,128]{2,1,0:T(8,128)(2,1)S(1)}, bf16[4,136,128]{2,1,0:T(8,128)(2,1)S(1)}, u32[]{:S(2)}, u32[]{:S(2)}) collective-permute-start(bf16[4,136,128]{2,1,0:T(8,128)(2,1)S(1)} %collective-permute-done.4.refs_3_), channel_id=1, source_target_pairs={{0,32},{1,97},{2,34},{3,99},{4,36},{5,101},{6,38},{7,103},{8,40},{... | collective-permute-start | bytes 417800 | tf_op jit(solution)/shard_map/ppermute | solution.py:308
  41.3 12.2 %collective-permute-start.16 = (bf16[4,136,128]{2,1,0:T(8,128)(2,1)S(1)}, bf16[4,136,128]{2,1,0:T(8,128)(2,1)S(1)}, u32[]{:S(2)}, u32[]{:S(2)}) collective-permute-start(bf16[4,136,128]{2,1,0:T(8,128)(2,1)S(1)} %pad_maximum_fusion.1.refs_3_), channel_id=1, source_target_pairs={{0,2},{1,3},{2,4},{3,5},{4,6},{5,7},{6,0},{7,1},{8,10},{9,11},{10,... | collective-permute-start | bytes 417800 | tf_op jit(solution)/shard_map/ppermute | solution.py:305
  43.6 17.3 %collective-permute-start.15 = (bf16[4,136,128]{2,1,0:T(8,128)(2,1)S(1)}, bf16[4,136,128]{2,1,0:T(8,128)(2,1)S(1)}, u32[]{:S(2)}, u32[]{:S(2)}) collective-permute-start(bf16[4,136,128]{2,1,0:T(8,128)(2,1)S(1)} %collective-permute-done.4.refs_3_), channel_id=1, source_target_pairs={{0,4},{1,5},{2,6},{3,7},{4,0},{5,1},{6,2},{7,3},{8,12},{9,13},{10,... | collective-permute-start | bytes 417800 | tf_op jit(solution)/shard_map/ppermute | solution.py:305
  46.8 20.4 %collective-permute-start.14 = (bf16[4,136,128]{2,1,0:T(8,128)(2,1)S(1)}, bf16[4,136,128]{2,1,0:T(8,128)(2,1)S(1)}, u32[]{:S(2)}, u32[]{:S(2)}) collective-permute-start(bf16[4,136,128]{2,1,0:T(8,128)(2,1)S(1)} %collective-permute-done.4.refs_3_), channel_id=1, source_target_pairs={{0,6},{1,7},{2,0},{3,1},{4,2},{5,3},{6,4},{7,5},{8,14},{9,15},{10,... | collective-permute-start | bytes 417800 | tf_op jit(solution)/shard_map/ppermute | solution.py:305
  48.2 20.9 %collective-permute-start.13 = (bf16[4,136,128]{2,1,0:T(8,128)(2,1)S(1)}, bf16[4,136,128]{2,1,0:T(8,128)(2,1)S(1)}, u32[]{:S(2)}, u32[]{:S(2)}) collective-permute-start(bf16[4,136,128]{2,1,0:T(8,128)(2,1)S(1)} %collective-permute-done.4.refs_3_), channel_id=1, source_target_pairs={{0,2},{1,3},{2,4},{3,5},{4,6},{5,7},{6,0},{7,1},{8,10},{9,11},{10,... | collective-permute-start | bytes 417800 | tf_op jit(solution)/shard_map/ppermute | solution.py:305
  50.2 30.8 %collective-permute-start.8 = (bf16[4,136,128]{2,1,0:T(8,128)(2,1)S(1)}, bf16[4,136,128]{2,1,0:T(8,128)(2,1)S(1)}, u32[]{:S(2)}, u32[]{:S(2)}) collective-permute-start(bf16[4,136,128]{2,1,0:T(8,128)(2,1)S(1)} %collective-permute-done.5.refs_3_), channel_id=1, source_target_pairs={{0,4},{1,5},{2,6},{3,7},{4,0},{5,1},{6,2},{7,3},{8,12},{9,13},{10,... | collective-permute-start | bytes 417800 | tf_op jit(solution)/shard_map/ppermute | solution.py:305
  53.5 13.6 %collective-permute-start.9 = (bf16[4,136,128]{2,1,0:T(8,128)(2,1)S(1)}, bf16[4,136,128]{2,1,0:T(8,128)(2,1)S(1)}, u32[]{:S(2)}, u32[]{:S(2)}) collective-permute-start(bf16[4,136,128]{2,1,0:T(8,128)(2,1)S(1)} %pad_maximum_fusion.2), channel_id=1, source_target_pairs={{0,32},{1,97},{2,34},{3,99},{4,36},{5,101},{6,38},{7,103},{8,40},{... | collective-permute-start | bytes 417800 | tf_op jit(solution)/shard_map/ppermute | solution.py:308
  61.0 20.0 %collective-permute-start.7 = (bf16[4,136,128]{2,1,0:T(8,128)(2,1)S(1)}, bf16[4,136,128]{2,1,0:T(8,128)(2,1)S(1)}, u32[]{:S(2)}, u32[]{:S(2)}) collective-permute-start(bf16[4,136,128]{2,1,0:T(8,128)(2,1)S(1)} %collective-permute-done.5.refs_3_), channel_id=1, source_target_pairs={{0,6},{1,7},{2,0},{3,1},{4,2},{5,3},{6,4},{7,5},{8,14},{9,15},{10,... | collective-permute-start | bytes 417800 | tf_op jit(solution)/shard_map/ppermute | solution.py:305
  67.2 8.0 %collective-permute-start.12 = (bf16[4,136,128]{2,1,0:T(8,128)(2,1)S(1)}, bf16[4,136,128]{2,1,0:T(8,128)(2,1)S(1)}, u32[]{:S(2)}, u32[]{:S(2)}) collective-permute-start(bf16[4,136,128]{2,1,0:T(8,128)(2,1)S(1)} %collective-permute-done.9.refs_3_), channel_id=1, source_target_pairs={{0,4},{1,5},{2,6},{3,7},{4,0},{5,1},{6,2},{7,3},{8,12},{9,13},{10,... | collective-permute-start | bytes 417800 | tf_op jit(solution)/shard_map/ppermute | solution.py:305
  67.2 8.0 %collective-permute-start.11 = (bf16[4,136,128]{2,1,0:T(8,128)(2,1)S(1)}, bf16[4,136,128]{2,1,0:T(8,128)(2,1)S(1)}, u32[]{:S(2)}, u32[]{:S(2)}) collective-permute-start(bf16[4,136,128]{2,1,0:T(8,128)(2,1)S(1)} %collective-permute-done.9.refs_3_), channel_id=1, source_target_pairs={{0,6},{1,7},{2,0},{3,1},{4,2},{5,3},{6,4},{7,5},{8,14},{9,15},{10,... | collective-permute-start | bytes 417800 | tf_op jit(solution)/shard_map/ppermute | solution.py:305
  69.1 8.3 %collective-permute-start.10 = (bf16[4,136,128]{2,1,0:T(8,128)(2,1)S(1)}, bf16[4,136,128]{2,1,0:T(8,128)(2,1)S(1)}, u32[]{:S(2)}, u32[]{:S(2)}) collective-permute-start(bf16[4,136,128]{2,1,0:T(8,128)(2,1)S(1)} %collective-permute-done.9.refs_3_), channel_id=1, source_target_pairs={{0,2},{1,3},{2,4},{3,5},{4,6},{5,7},{6,0},{7,1},{8,10},{9,11},{10,... | collective-permute-start | bytes 417800 | tf_op jit(solution)/shard_map/ppermute | solution.py:305
  75.2 6.3 %collective-permute-start.6 = (bf16[4,136,128]{2,1,0:T(8,128)(2,1)S(1)}, bf16[4,136,128]{2,1,0:T(8,128)(2,1)S(1)}, u32[]{:S(2)}, u32[]{:S(2)}) collective-permute-start(bf16[4,136,128]{2,1,0:T(8,128)(2,1)S(1)} %collective-permute-done.5.refs_3_), channel_id=1, source_target_pairs={{0,2},{1,3},{2,4},{3,5},{4,6},{5,7},{6,0},{7,1},{8,10},{9,11},{10,... | collective-permute-start | bytes 417800 | tf_op jit(solution)/shard_map/ppermute | solution.py:305
  77.4 7.5 %copy-start.1 = (s32[64]{0:T(128)S(1)}, s32[64]{0:T(128)}, u32[]{:S(2)}) copy-start(s32[64]{0:T(128)} %param.10) | copy-start | bytes 772
  84.7 2.0 %collective-permute-start.19 = (bf16[2,512,256]{2,1,0:T(8,128)(2,1)S(1)}, bf16[2,512,256]{2,1,0:T(8,128)(2,1)S(1)}, u32[]{:S(2)}, u32[]{:S(2)}) collective-permute-start(bf16[2,512,256]{2,1,0:T(8,128)(2,1)S(1)} %get-tuple-element.35), channel_id=1, source_target_pairs={{0,1},{1,0},{2,3},{3,2},{4,5},{5,4},{6,7},{7,6},{8,9},{9,8},{10,11... | collective-permute-start | bytes 1572872 | tf_op jit(solution)/shard_map/ppermute | solution.py:305
  87.3 10.9 %collective-permute-start.22 = (bf16[4,64,128]{2,1,0:T(8,128)(2,1)S(1)}, bf16[4,64,128]{2,1,0:T(8,128)(2,1)S(1)}, u32[]{:S(2)}, u32[]{:S(2)}) collective-permute-start(bf16[4,64,128]{2,1,0:T(8,128)(2,1)S(1)} %get-tuple-element.41), channel_id=1, source_target_pairs={{0,8},{1,9},{2,10},{3,11},{4,12},{5,13},{6,14},{7,15},{8,16},{9,17... | collective-permute-start | bytes 196616 | tf_op jit(solution)/shard_map/ppermute | solution.py:313
  89.6 8.6 %collective-permute-start.21 = (bf16[4,64,128]{2,1,0:T(8,128)(2,1)S(1)}, bf16[4,64,128]{2,1,0:T(8,128)(2,1)S(1)}, u32[]{:S(2)}, u32[]{:S(2)}) collective-permute-start(bf16[4,64,128]{2,1,0:T(8,128)(2,1)S(1)} %get-tuple-element.42), channel_id=1, source_target_pairs={{0,16},{1,17},{2,18},{3,19},{4,20},{5,21},{6,22},{7,23},{8,24},{9,... | collective-permute-start | bytes 196616 | tf_op jit(solution)/shard_map/ppermute | solution.py:313
  92.0 6.2 %copy-start = (bf16[64,2048]{1,0:T(8,128)(2,1)S(1)}, bf16[64,2048]{1,0:T(8,128)(2,1)}, u32[]{:S(2)}) copy-start(bf16[64,2048]{1,0:T(8,128)(2,1)} %refs_5_.1) | copy-start | bytes 786436
  92.0 6.2 %collective-permute-start.20 = (bf16[4,64,128]{2,1,0:T(8,128)(2,1)S(1)}, bf16[4,64,128]{2,1,0:T(8,128)(2,1)S(1)}, u32[]{:S(2)}, u32[]{:S(2)}) collective-permute-start(bf16[4,64,128]{2,1,0:T(8,128)(2,1)S(1)} %get-tuple-element.43), channel_id=1, source_target_pairs={{0,24},{1,25},{2,26},{3,27},{4,28},{5,29},{6,30},{7,31},{8,0},{9,1... | collective-permute-start | bytes 196616 | tf_op jit(solution)/shard_map/ppermute | solution.py:313

commit v3 on v2

--- a/solution.py
+++ b/solution.py
@@ -19,7 +19,7 @@
 HALF = 32
 KV_ROWS = 2 * TOK + 8
 ALL_ROWS = (2 + GROUP) * TOK + 8
-TOGETHER = 4
+TOGETHER = 2
 ROWS = TOGETHER * GROUP * HALF
 PAIRS = KV_HEADS // TOGETHER
 SCALE = HEAD_DIM ** -0.5 * math.log2(math.e)
@@ -108,7 +108,7 @@
     if first:
         old_refs = None
     else:
-        old_refs, refs = refs[:4], refs[4:]
+        offsets, old_refs, refs = refs[0], refs[1:5], refs[5:]
     new_refs, (keys, vals) = refs[:-2], refs[-2:]
     limit = limit_ref[0]
     sources = KV_HEADS
@@ -132,74 +132,88 @@
         chunk = (iota((8, HEAD_DIM), 0) * (HALF * RUN)).astype(F32)
         tables.append(jnp.where(table + chunk >= limit.astype(F32), 1e9, table))
     ramp = (iota((HALF, HEAD_DIM), 0) * RUN).astype(F32)
-    diagonal = iota((HALF, HEAD_DIM), 0) == iota((HALF, HEAD_DIM), 1)
-    spread = [
-        jnp.where(diagonal, q_ref[src, ALL_ROWS - 8 + i:ALL_ROWS - 7 + i, :].astype(F32), 0.0).astype(BF16)
-        for q_ref in (qa_ref, qb_ref)
-        for i in range(2)
-        for src in range(sources)
-    ]
-    offsets = jnp.dot(
-        jnp.concatenate(spread, axis=0), jnp.ones((HEAD_DIM, HEAD_DIM), BF16), preferred_element_type=F32
-    )
-    for half, q_ref in enumerate((qa_ref, qb_ref)):
-        for i in range(2):
-            for sp in range(PAIRS):
-                b = i * PAIRS + sp
-                q_rows = []
-                q_poss = []
-                for src in range(TOGETHER * sp, TOGETHER * (sp + 1)):
-                    for g in range(GROUP):
-                        at = (2 + g) * TOK + HALF * i
-                        q_rows.append(q_ref[src, at:at + HALF, :])
-                    at = ((half * 2 + i) * sources + src) * HALF
-                    q_poss += [offsets[at:at + HALF, :] + ramp] * GROUP
-                q = jnp.concatenate(q_rows, axis=0)
-                q_pos = jnp.concatenate(q_poss, axis=0)
-                count = (i + 1) * wide
-                s = lax.dot_general(
-                    q, keys[0:count, :], (((1,), (1,)), ((), ())), preferred_element_type=F32
-                ) * SCALE
-                pieces = [s[:, c * HEAD_DIM:(c + 1) * HEAD_DIM] for c in range(count // HEAD_DIM)]
-                for n in range(shards):
-                    c = i * shards + n
-                    pieces[c] = jnp.where(tables[n][i:i + 1, :] <= q_pos, pieces[c], NEVER)
-                top = functools.reduce(jnp.maximum, pieces)
-                top = jnp.max(top, axis=1, keepdims=True)
-                if first:
-                    new_max = jnp.broadcast_to(jnp.maximum(top, LOWEST), (ROWS, HEAD_DIM))
-                else:
-                    old_max = old_refs[2 * half][b]
-                    new_max = jnp.maximum(old_max, top)
-                weights = jnp.concatenate([jnp.exp2(piece - new_max).astype(BF16) for piece in pieces], axis=1)
-                sums = jnp.dot(weights, vals[0:count, :], preferred_element_type=F32)
-                if not first:
-                    rescale = jnp.exp2(old_max - new_max)
-                    sums = sums + old_refs[2 * half + 1][b] * jnp.concatenate([rescale, rescale], axis=1)
-                if last and half == 1:
-                    lane = iota((ROWS, HEAD_DIM), 1)
-                    total = jnp.maximum(sums[:, HEAD_DIM:], 1e-30)
-                    level = new_max + jnp.log2(total)
-                    high = level.astype(BF16).astype(F32)
-                    middle = (level - high).astype(BF16).astype(F32)
-                    parts3 = jnp.where(lane < PART, high, jnp.where(lane < 2 * PART, middle, level - high - middle))
-                    new_refs[2][b, :, 0:HEAD_DIM] = (sums[:, 0:HEAD_DIM] / total).astype(BF16)
-                    new_refs[2][b, :, HEAD_DIM:] = parts3.astype(BF16)
-                else:
-                    new_refs[2 * half][b] = new_max
-                    new_refs[2 * half + 1][b] = sums
-
-
-def attend(limit, qa, qb, parts, state, last=False):
+    if first:
+        diagonal = iota((HALF, HEAD_DIM), 0) == iota((HALF, HEAD_DIM), 1)
+        spread = [
+            jnp.where(diagonal, q_ref[src, ALL_ROWS - 8 + i:ALL_ROWS - 7 + i, :].astype(F32), 0.0).astype(BF16)
+            for q_ref in (qa_ref, qb_ref)
+            for i in range(2)
+            for src in range(sources)
+        ]
+        offsets = new_refs[4]
+        offsets[...] = jnp.dot(
+            jnp.concatenate(spread, axis=0), jnp.ones((HEAD_DIM, HEAD_DIM), BF16), preferred_element_type=F32
+        )
+    blocks = [(half, i, sp) for half in range(2) for i in range(2) for sp in range(PAIRS)]
+
+    def score(half, i, sp):
+        q_ref = (qa_ref, qb_ref)[half]
+        q_rows = []
+        for src in range(TOGETHER * sp, TOGETHER * (sp + 1)):
+            for g in range(GROUP):
+                at = (2 + g) * TOK + HALF * i
+                q_rows.append(q_ref[src, at:at + HALF, :])
+        return lax.dot_general(
+            jnp.concatenate(q_rows, axis=0),
+            keys[0:(i + 1) * wide, :],
+            (((1,), (1,)), ((), ())),
+            preferred_element_type=F32,
+        )
+
+    ready = score(*blocks[0])
+    for at_block, (half, i, sp) in enumerate(blocks):
+        s = ready * SCALE
+        if at_block + 1 < len(blocks):
+            ready = score(*blocks[at_block + 1])
+        b = i * PAIRS + sp
+        q_poss = []
+        for src in range(TOGETHER * sp, TOGETHER * (sp + 1)):
+            at = ((half * 2 + i) * sources + src) * HALF
+            q_poss += [offsets[at:at + HALF, :] + ramp] * GROUP
+        q_pos = jnp.concatenate(q_poss, axis=0)
+        count = (i + 1) * wide
+        pieces = [s[:, c * HEAD_DIM:(c + 1) * HEAD_DIM] for c in range(count // HEAD_DIM)]
+        for n in range(shards):
+            c = i * shards + n
+            pieces[c] = jnp.where(tables[n][i:i + 1, :] <= q_pos, pieces[c], NEVER)
+        top = functools.reduce(jnp.maximum, pieces)
+        top = jnp.max(top, axis=1, keepdims=True)
+        if first:
+            new_max = jnp.broadcast_to(jnp.maximum(top, LOWEST), (ROWS, HEAD_DIM))
+        else:
+            old_max = old_refs[2 * half][b]
+            new_max = jnp.maximum(old_max, top)
+        weights = jnp.concatenate([jnp.exp2(piece - new_max).astype(BF16) for piece in pieces], axis=1)
+        sums = jnp.dot(weights, vals[0:count, :], preferred_element_type=F32)
+        if not first:
+            rescale = jnp.exp2(old_max - new_max)
+            sums = sums + old_refs[2 * half + 1][b] * jnp.concatenate([rescale, rescale], axis=1)
+        if last and half == 1:
+            lane = iota((ROWS, HEAD_DIM), 1)
+            total = jnp.maximum(sums[:, HEAD_DIM:], 1e-30)
+            level = new_max + jnp.log2(total)
+            high = level.astype(BF16).astype(F32)
+            middle = (level - high).astype(BF16).astype(F32)
+            parts3 = jnp.where(lane < PART, high, jnp.where(lane < 2 * PART, middle, level - high - middle))
+            new_refs[2][b, :, 0:HEAD_DIM] = (sums[:, 0:HEAD_DIM] / total).astype(BF16)
+            new_refs[2][b, :, HEAD_DIM:] = parts3.astype(BF16)
+        else:
+            new_refs[2 * half][b] = new_max
+            new_refs[2 * half + 1][b] = sums
+
+
+def attend(limit, qa, qb, parts, state, offsets=None, last=False):
     shards = sum(part.shape[0] for part in parts) // KV_HEADS
     wide = shards * HEAD_DIM
     stats = jax.ShapeDtypeStruct((2 * PAIRS, ROWS, HEAD_DIM), F32)
     sums = jax.ShapeDtypeStruct((2 * PAIRS, ROWS, 2 * HEAD_DIM), F32)
     shapes = (stats, sums, VMEM(sums.shape, BF16)) if last else (stats, sums, stats, sums)
     first = state is None
-    held = [] if first else list(state)
+    held = [] if first else [offsets] + list(state)
+    if first:
+        shapes += (jax.ShapeDtypeStruct((4 * KV_HEADS * HALF, HEAD_DIM), F32),)
     score_count = 4 * 2 * 256 * 3 * wide
-    base = 3 + len(parts)
+    base = 4 + len(parts)
     return pl.pallas_call(
         functools.partial(attend_kernel, len(parts), first, last),
         out_shape=shapes,
@@ -334,10 +348,10 @@
     one_group = [one] + spread(one)
     other_group = [other] + spread(other)
     two_group = [two] + spread(two)
-    state = attend(prompt_length, own, twin, own_group, None)
-    state = attend(prompt_length, own, twin, one_group, state)
-    state = attend(prompt_length, own, twin, other_group, state)
-    state = attend(prompt_length, own, twin, two_group, state, last=True)
+    *state, offsets = attend(prompt_length, own, twin, own_group, None)
+    state = attend(prompt_length, own, twin, one_group, state, offsets)
+    state = attend(prompt_length, own, twin, other_group, state, offsets)
+    state = attend(prompt_length, own, twin, two_group, state, offsets, last=True)
     got = move(state[2], dc=1)
     done = merge(state[0], state[1], got)
     parts = [done[0]] + [turn(done[d], -d) for d in range(1, BLOCK)]

time: 101 us -> 101 us (level)
  starting transfers between devices: 50.3 us -> 55.8 us
  waiting for transfers between devices: 28.3 us -> 23.3 us
  Pallas kernels: 20.9 us -> 19.6 us
    ppermute x14, starting transfers between devices: 17.9 us -> 22 us  [move(): lax.ppermute(a, 'seq', [(at(z, x, c), at(z + dz, x + dx, c + dc)) for z,...]
    ppermute x14, waiting for transfers between devices: 6.8 us -> 3.65 us  [move(): lax.ppermute(a, 'seq', [(at(z, x, c), at(z + dz, x + dx, c + dc)) for z,...]
    ppermute x3, waiting for transfers between devices: 13.2 us -> 10.5 us  [far(): lax.ppermute(a, 'seq', [(at(z, x, c), at(z + (BLOCK if c == 0 else -BLOCK...]
    pallas_call x4, Pallas kernels: 13.2 us -> 11.7 us  [attend(): pl.pallas_call(functools.partial(attend_kernel, len(parts), first, last),...]
  transfers between devices with their start and end apart: 23 -> 23, of which waited for: 9 -> 9; matrix products, arithmetic and copies ran while one was open for 0% -> 0% of each run, Pallas kernels for 13% -> 12%
where the time goes in v3:
time: 101 us; the launch traced here: 99.8 us
  starting transfers between devices  55.8 us (55%)
  waiting for transfers between devices  23.3 us (23%)
  Pallas kernels  19.6 us (19%)
    ppermute x14, starting transfers between devices, move(): lax.ppermute(a, 'seq', [(at(z, x, c), at(z + dz, x + dx, c + dc)) for z,...  22 us
    ppermute x3, starting transfers between devices, far(): lax.ppermute(a, 'seq', [(at(z, x, c), at(z + (BLOCK if c == 0 else -BLOCK...  17.6 us
    ppermute x6, starting transfers between devices, turn(): lax.ppermute(a, 'seq', [(at(z, x, c), at(z // BLOCK * BLOCK + (z + d) % B...  16.2 us
    pallas_call x4, Pallas kernels, attend(): pl.pallas_call(functools.partial(attend_kernel, len(parts), first, last),...  11.7 us
    ppermute x3, waiting for transfers between devices, far(): lax.ppermute(a, 'seq', [(at(z, x, c), at(z + (BLOCK if c == 0 else -BLOCK...  10.5 us
    ppermute x6, waiting for transfers between devices, turn(): lax.ppermute(a, 'seq', [(at(z, x, c), at(z // BLOCK * BLOCK + (z + d) % B...  9.15 us
    ppermute x14, waiting for transfers between devices, move(): lax.ppermute(a, 'seq', [(at(z, x, c), at(z + dz, x + dx, c + dc)) for z,...  3.65 us
    pallas_call x1, Pallas kernels, hold(): pl.pallas_call(hold_kernel, out_shape=VMEM(weight.shape, weight.dtype), i...  3.39 us
  transfers between devices with their start and end apart: 23, of which 9 were waited for; matrix products, arithmetic and copies ran while one was open for 0% of the time, Pallas kernels for 12%

profile of v3, /device:TPU:40, one launch (start us, length us, event | category | flops | bytes accessed | tf_op | source)
XLA Modules:
  0.0 99.8 jit_solution(6529656889288947288)
XLA Ops:
  0.0 1.4 %prep.1 = bf16[4,392,128]{2,1,0:T(8,128)(2,1)S(1)} custom-call(s32[1,64]{1,0:T(1,128)} %bitcast.23, bf16[64,2048]{1,0:T(8,128)(2,1)} %q_hbm.1, bf16[64,512]{1,0:T(8,128)(2,1)} %k_hbm.1, bf16[64,512]{1,0:T(8,128)(2,1)} %v_hbm.1), custom_call_target="tpu_custom_call" | custom-call | flops 25165824 | bytes 800000 | tf_op jit(solution)/shard_map/prep/pallas_call | solution.py:86
  1.4 2.9 %collective-permute-start = (bf16[392,128]{1,0:T(8,128)(2,1)S(1)}, bf16[392,128]{1,0:T(8,128)(2,1)S(1)}, u32[]{:S(2)}, u32[]{:S(2)}) collective-permute-start(bf16[392,128]{1,0:T(8,128)(2,1)S(1)} %get-tuple-element.42), channel_id=1, source_target_pairs={{0,8},{1,9},{2,10},{3,11},{4,12},{5,13},{6,14},{7,15},{8,16},{9,17... | collective-permute-start | bytes 301064 | tf_op jit(solution)/shard_map/ppermute | solution.py:327
  4.3 5.0 %collective-permute-start.1 = (bf16[392,128]{1,0:T(8,128)(2,1)S(1)}, bf16[392,128]{1,0:T(8,128)(2,1)S(1)}, u32[]{:S(2)}, u32[]{:S(2)}) collective-permute-start(bf16[392,128]{1,0:T(8,128)(2,1)S(1)} %get-tuple-element.41), channel_id=1, source_target_pairs={{0,16},{1,17},{2,18},{3,19},{4,20},{5,21},{6,22},{7,23},{8,24},{9,... | collective-permute-start | bytes 301064 | tf_op jit(solution)/shard_map/ppermute | solution.py:327
  9.3 0.2 collective-permute-start.2
  9.5 3.1 %collective-permute-done = bf16[392,128]{1,0:T(8,128)(2,1)S(1)} collective-permute-done((bf16[392,128]{1,0:T(8,128)(2,1)S(1)}, bf16[392,128]{1,0:T(8,128)(2,1)S(1)}, u32[]{:S(2)}, u32[]{:S(2)}) %collective-permute-start) | collective-permute-done | bytes 100384 | tf_op jit(solution)/shard_map/ppermute | solution.py:327
  12.6 3.6 %collective-permute-done.1 = bf16[392,128]{1,0:T(8,128)(2,1)S(1)} collective-permute-done((bf16[392,128]{1,0:T(8,128)(2,1)S(1)}, bf16[392,128]{1,0:T(8,128)(2,1)S(1)}, u32[]{:S(2)}, u32[]{:S(2)}) %collective-permute-start.1) | collective-permute-done | bytes 100384 | tf_op jit(solution)/shard_map/ppermute | solution.py:327
  16.1 0.1 pad_maximum_fusion.refs_1_
  16.2 0.1 collective-permute-start.3
  16.4 10.7 %collective-permute-start.4 = (bf16[4,136,128]{2,1,0:T(8,128)(2,1)S(1)}, bf16[4,136,128]{2,1,0:T(8,128)(2,1)S(1)}, u32[]{:S(2)}, u32[]{:S(2)}) collective-permute-start(bf16[4,136,128]{2,1,0:T(8,128)(2,1)S(1)} %pad_maximum_fusion.1.refs_3_), channel_id=1, source_target_pairs={{0,32},{1,97},{2,34},{3,99},{4,36},{5,101},{6,38},{7,103},{8,40},{... | collective-permute-start | bytes 417800 | tf_op jit(solution)/shard_map/ppermute | solution.py:322
  27.1 3.2 %collective-permute-start.10 = (bf16[4,136,128]{2,1,0:T(8,128)(2,1)S(1)}, bf16[4,136,128]{2,1,0:T(8,128)(2,1)S(1)}, u32[]{:S(2)}, u32[]{:S(2)}) collective-permute-start(bf16[4,136,128]{2,1,0:T(8,128)(2,1)S(1)} %pad_maximum_fusion.1.refs_3_), channel_id=1, source_target_pairs={{0,6},{1,7},{2,0},{3,1},{4,2},{5,3},{6,4},{7,5},{8,14},{9,15},{10,... | collective-permute-start | bytes 417800 | tf_op jit(solution)/shard_map/ppermute | solution.py:319
  30.3 0.5 collective-permute-start.11
  30.8 7.4 %collective-permute-done.4.refs_3_ = bf16[4,136,128]{2,1,0:T(8,128)(2,1)S(1)} collective-permute-done((bf16[4,136,128]{2,1,0:T(8,128)(2,1)S(1)}, bf16[4,136,128]{2,1,0:T(8,128)(2,1)S(1)}, u32[]{:S(2)}, u32[]{:S(2)}) %collective-permute-start.4) | collective-permute-done | bytes 139296 | tf_op jit(solution)/shard_map/ppermute | solution.py:322
  38.2 2.1 %collective-permute-start.5 = (bf16[4,136,128]{2,1,0:T(8,128)(2,1)S(1)}, bf16[4,136,128]{2,1,0:T(8,128)(2,1)S(1)}, u32[]{:S(2)}, u32[]{:S(2)}) collective-permute-start(bf16[4,136,128]{2,1,0:T(8,128)(2,1)S(1)} %collective-permute-done.4.refs_3_), channel_id=1, source_target_pairs={{0,32},{1,97},{2,34},{3,99},{4,36},{5,101},{6,38},{7,103},{8,40},{... | collective-permute-start | bytes 417800 | tf_op jit(solution)/shard_map/ppermute | solution.py:322
  40.3 1.6 %collective-permute-start.9 = (bf16[4,136,128]{2,1,0:T(8,128)(2,1)S(1)}, bf16[4,136,128]{2,1,0:T(8,128)(2,1)S(1)}, u32[]{:S(2)}, u32[]{:S(2)}) collective-permute-start(bf16[4,136,128]{2,1,0:T(8,128)(2,1)S(1)} %pad_maximum_fusion.1.refs_3_), channel_id=1, source_target_pairs={{0,2},{1,3},{2,4},{3,5},{4,6},{5,7},{6,0},{7,1},{8,10},{9,11},{10,... | collective-permute-start | bytes 417800 | tf_op jit(solution)/shard_map/ppermute | solution.py:319
  42.6 0.0 collective-permute-done.3.refs_2_
  42.6 1.7 %collective-permute-start.16 = (bf16[4,136,128]{2,1,0:T(8,128)(2,1)S(1)}, bf16[4,136,128]{2,1,0:T(8,128)(2,1)S(1)}, u32[]{:S(2)}, u32[]{:S(2)}) collective-permute-start(bf16[4,136,128]{2,1,0:T(8,128)(2,1)S(1)} %collective-permute-done.4.refs_3_), channel_id=1, source_target_pairs={{0,2},{1,3},{2,4},{3,5},{4,6},{5,7},{6,0},{7,1},{8,10},{9,11},{10,... | collective-permute-start | bytes 417800 | tf_op jit(solution)/shard_map/ppermute | solution.py:319
  44.4 1.7 %collective-permute-start.17 = (bf16[4,136,128]{2,1,0:T(8,128)(2,1)S(1)}, bf16[4,136,128]{2,1,0:T(8,128)(2,1)S(1)}, u32[]{:S(2)}, u32[]{:S(2)}) collective-permute-start(bf16[4,136,128]{2,1,0:T(8,128)(2,1)S(1)} %collective-permute-done.4.refs_3_), channel_id=1, source_target_pairs={{0,6},{1,7},{2,0},{3,1},{4,2},{5,3},{6,4},{7,5},{8,14},{9,15},{10,... | collective-permute-start | bytes 417800 | tf_op jit(solution)/shard_map/ppermute | solution.py:319
  46.1 0.0 collective-permute-done.11.refs_6_
  46.1 1.8 %collective-permute-start.18 = (bf16[4,136,128]{2,1,0:T(8,128)(2,1)S(1)}, bf16[4,136,128]{2,1,0:T(8,128)(2,1)S(1)}, u32[]{:S(2)}, u32[]{:S(2)}) collective-permute-start(bf16[4,136,128]{2,1,0:T(8,128)(2,1)S(1)} %collective-permute-done.4.refs_3_), channel_id=1, source_target_pairs={{0,4},{1,5},{2,6},{3,7},{4,0},{5,1},{6,2},{7,3},{8,12},{9,13},{10,... | collective-permute-start | bytes 417800 | tf_op jit(solution)/shard_map/ppermute | solution.py:319
  47.9 1.0 %collective-permute-done.5.refs_3_ = bf16[4,136,128]{2,1,0:T(8,128)(2,1)S(1)} collective-permute-done((bf16[4,136,128]{2,1,0:T(8,128)(2,1)S(1)}, bf16[4,136,128]{2,1,0:T(8,128)(2,1)S(1)}, u32[]{:S(2)}, u32[]{:S(2)}) %collective-permute-start.5) | collective-permute-done | bytes 139296 | tf_op jit(solution)/shard_map/ppermute | solution.py:322
  49.0 1.6 %collective-permute-start.6 = (bf16[4,136,128]{2,1,0:T(8,128)(2,1)S(1)}, bf16[4,136,128]{2,1,0:T(8,128)(2,1)S(1)}, u32[]{:S(2)}, u32[]{:S(2)}) collective-permute-start(bf16[4,136,128]{2,1,0:T(8,128)(2,1)S(1)} %collective-permute-done.5.refs_3_), channel_id=1, source_target_pairs={{0,2},{1,3},{2,4},{3,5},{4,6},{5,7},{6,0},{7,1},{8,10},{9,11},{10,... | collective-permute-start | bytes 417800 | tf_op jit(solution)/shard_map/ppermute | solution.py:319
  50.6 0.0 collective-permute-done.9.refs_4_
  50.6 4.8 %collective-permute-start.12 = (bf16[4,136,128]{2,1,0:T(8,128)(2,1)S(1)}, bf16[4,136,128]{2,1,0:T(8,128)(2,1)S(1)}, u32[]{:S(2)}, u32[]{:S(2)}) collective-permute-start(bf16[4,136,128]{2,1,0:T(8,128)(2,1)S(1)} %pad_maximum_fusion.2), channel_id=1, source_target_pairs={{0,32},{1,97},{2,34},{3,99},{4,36},{5,101},{6,38},{7,103},{8,40},{... | collective-permute-start | bytes 417800 | tf_op jit(solution)/shard_map/ppermute | solution.py:322
  55.4 2.5 %attend.3 = (f32[4,256,128]{2,1,0:T(8,128)S(1)}, f32[4,256,256]{2,1,0:T(8,128)S(1)}, f32[4,256,128]{2,1,0:T(8,128)S(1)}, f32[4,256,256]{2,1,0:T(8,128)S(1)}, f32[512,128]{1,0:T(8,128)S(1)}) custom-call(s32[1]{0:T(128)S(6)} %copy.29.refs_0_, bf16[4,392,128]{2,1,0:T(8,128)(2,1)S(1)} %pad_maximum_fusion.refs_1_, ...), custom_call_target="tpu_custom_call" | custom-call | flops 2415919104 | bytes 4000000 | tf_op jit(solution)/shard_map/attend/pallas_call | solution.py:217
  57.9 0.0 collective-permute-done.16.refs_4_
  57.9 2.4 %collective-permute-start.7 = (bf16[4,136,128]{2,1,0:T(8,128)(2,1)S(1)}, bf16[4,136,128]{2,1,0:T(8,128)(2,1)S(1)}, u32[]{:S(2)}, u32[]{:S(2)}) collective-permute-start(bf16[4,136,128]{2,1,0:T(8,128)(2,1)S(1)} %collective-permute-done.5.refs_3_), channel_id=1, source_target_pairs={{0,6},{1,7},{2,0},{3,1},{4,2},{5,3},{6,4},{7,5},{8,14},{9,15},{10,... | collective-permute-start | bytes 417800 | tf_op jit(solution)/shard_map/ppermute | solution.py:319
  60.3 2.1 %collective-permute-done.12.refs_3_ = bf16[4,136,128]{2,1,0:T(8,128)(2,1)S(1)} collective-permute-done((bf16[4,136,128]{2,1,0:T(8,128)(2,1)S(1)}, bf16[4,136,128]{2,1,0:T(8,128)(2,1)S(1)}, u32[]{:S(2)}, u32[]{:S(2)}) %collective-permute-start.12) | collective-permute-done | bytes 139296 | tf_op jit(solution)/shard_map/ppermute | solution.py:322
  62.3 1.6 %collective-permute-start.13 = (bf16[4,136,128]{2,1,0:T(8,128)(2,1)S(1)}, bf16[4,136,128]{2,1,0:T(8,128)(2,1)S(1)}, u32[]{:S(2)}, u32[]{:S(2)}) collective-permute-start(bf16[4,136,128]{2,1,0:T(8,128)(2,1)S(1)} %collective-permute-done.12.refs_3_), channel_id=1, source_target_pairs={{0,2},{1,3},{2,4},{3,5},{4,6},{5,7},{6,0},{7,1},{8,10},{9,11},{10,... | collective-permute-start | bytes 417800 | tf_op jit(solution)/shard_map/ppermute | solution.py:319
  64.0 1.6 %collective-permute-start.14 = (bf16[4,136,128]{2,1,0:T(8,128)(2,1)S(1)}, bf16[4,136,128]{2,1,0:T(8,128)(2,1)S(1)}, u32[]{:S(2)}, u32[]{:S(2)}) collective-permute-start(bf16[4,136,128]{2,1,0:T(8,128)(2,1)S(1)} %collective-permute-done.12.refs_3_), channel_id=1, source_target_pairs={{0,6},{1,7},{2,0},{3,1},{4,2},{5,3},{6,4},{7,5},{8,14},{9,15},{10,... | collective-permute-start | bytes 417800 | tf_op jit(solution)/shard_map/ppermute | solution.py:319
  65.6 1.8 %collective-permute-start.15 = (bf16[4,136,128]{2,1,0:T(8,128)(2,1)S(1)}, bf16[4,136,128]{2,1,0:T(8,128)(2,1)S(1)}, u32[]{:S(2)}, u32[]{:S(2)}) collective-permute-start(bf16[4,136,128]{2,1,0:T(8,128)(2,1)S(1)} %collective-permute-done.12.refs_3_), channel_id=1, source_target_pairs={{0,4},{1,5},{2,6},{3,7},{4,0},{5,1},{6,2},{7,3},{8,12},{9,13},{10,... | collective-permute-start | bytes 417800 | tf_op jit(solution)/shard_map/ppermute | solution.py:319
  67.4 3.2 %attend.4 = (f32[4,256,128]{2,1,0:T(8,128)S(1)}, f32[4,256,256]{2,1,0:T(8,128)S(1)}, f32[4,256,128]{2,1,0:T(8,128)S(1)}, f32[4,256,256]{2,1,0:T(8,128)S(1)}) custom-call(s32[1]{0:T(128)S(6)} %copy.29.refs_0_, bf16[4,392,128]{2,1,0:T(8,128)(2,1)S(1)} %pad_maximum_fusion.refs_1_, ...), custom_call_target="tpu_custom_call", output_to_operand_aliasing={{0}: (8, {}), {1}: (9, {}), {2}: (10, {}), {3}: (11, {})} | custom-call | flops 2415919104 | bytes 4000000 | tf_op jit(solution)/shard_map/attend/pallas_call | solution.py:217
  70.6 0.0 collective-permute-done.13.refs_4_
  70.6 2.1 %collective-permute-start.8 = (bf16[4,136,128]{2,1,0:T(8,128)(2,1)S(1)}, bf16[4,136,128]{2,1,0:T(8,128)(2,1)S(1)}, u32[]{:S(2)}, u32[]{:S(2)}) collective-permute-start(bf16[4,136,128]{2,1,0:T(8,128)(2,1)S(1)} %collective-permute-done.5.refs_3_), channel_id=1, source_target_pairs={{0,4},{1,5},{2,6},{3,7},{4,0},{5,1},{6,2},{7,3},{8,12},{9,13},{10,... | collective-permute-start | bytes 417800 | tf_op jit(solution)/shard_map/ppermute | solution.py:319
  72.7 0.0 collective-permute-done.14.refs_5_
  72.7 0.6 collective-permute-done.15.refs_6_
  73.3 3.2 %attend.5 = (f32[4,256,128]{2,1,0:T(8,128)S(1)}, f32[4,256,256]{2,1,0:T(8,128)S(1)}, f32[4,256,128]{2,1,0:T(8,128)S(1)}, f32[4,256,256]{2,1,0:T(8,128)S(1)}) custom-call(s32[1]{0:T(128)S(6)} %copy.29.refs_0_, bf16[4,392,128]{2,1,0:T(8,128)(2,1)S(1)} %pad_maximum_fusion.refs_1_, ...), custom_call_target="tpu_custom_call", output_to_operand_aliasing={{0}: (8, {}), {1}: (9, {}), {2}: (10, {}), {3}: (11, {})} | custom-call | flops 2415919104 | bytes 4000000 | tf_op jit(solution)/shard_map/attend/pallas_call | solution.py:217
  76.5 0.0 collective-permute-done.6.refs_4_
  76.5 1.2 %collective-permute-done.8.refs_6_ = bf16[4,136,128]{2,1,0:T(8,128)(2,1)S(1)} collective-permute-done((bf16[4,136,128]{2,1,0:T(8,128)(2,1)S(1)}, bf16[4,136,128]{2,1,0:T(8,128)(2,1)S(1)}, u32[]{:S(2)}, u32[]{:S(2)}) %collective-permute-start.8) | collective-permute-done | bytes 139296 | tf_op jit(solution)/shard_map/ppermute | solution.py:319
  77.8 2.8 %attend_last.1 = (f32[4,256,128]{2,1,0:T(8,128)S(1)}, f32[4,256,256]{2,1,0:T(8,128)S(1)}, bf16[4,256,256]{2,1,0:T(8,128)(2,1)S(1)}) custom-call(s32[1]{0:T(128)S(6)} %copy.29.refs_0_, bf16[4,392,128]{2,1,0:T(8,128)(2,1)S(1)} %pad_maximum_fusion.refs_1_, ...), custom_call_target="tpu_custom_call", output_to_operand_aliasing={{0}: (8, {}), {1}: (9, {})} | custom-call | flops 2415919104 | bytes 4000000 | tf_op jit(solution)/shard_map/attend_last/pallas_call | solution.py:217
  80.5 0.1 collective-permute-start.19
  80.7 0.1 copy.18.pos_ref
  80.8 1.8 %collective-permute-done.19.got_ref = bf16[4,256,256]{2,1,0:T(8,128)(2,1)S(1)} collective-permute-done((bf16[4,256,256]{2,1,0:T(8,128)(2,1)S(1)}, bf16[4,256,256]{2,1,0:T(8,128)(2,1)S(1)}, u32[]{:S(2)}, u32[]{:S(2)}) %collective-permute-start.19) | collective-permute-done | bytes 524320 | tf_op jit(solution)/shard_map/ppermute | solution.py:319
  82.6 0.6 merge.1
  83.2 7.4 %collective-permute-start.20 = (bf16[4,64,128]{2,1,0:T(8,128)(2,1)S(1)}, bf16[4,64,128]{2,1,0:T(8,128)(2,1)S(1)}, u32[]{:S(2)}, u32[]{:S(2)}) collective-permute-start(bf16[4,64,128]{2,1,0:T(8,128)(2,1)S(1)} %get-tuple-element.45), channel_id=1, source_target_pairs={{0,24},{1,25},{2,26},{3,27},{4,28},{5,29},{6,30},{7,31},{8,0},{9,1... | collective-permute-start | bytes 196616 | tf_op jit(solution)/shard_map/ppermute | solution.py:327
  90.7 0.7 collective-permute-start.22
  91.4 3.4 %hold.1.refs_4_ = bf16[2048,2048]{1,0:T(8,128)(2,1)S(1)} custom-call(bf16[2048,2048]{1,0:T(8,128)(2,1)} %weight_ref), custom_call_target="tpu_custom_call" | custom-call | flops 2000000000 | bytes 8000000 | tf_op jit(solution)/shard_map/hold/pallas_call | solution.py:239
  94.8 2.5 %collective-permute-done.21.refs_2_ = bf16[4,64,128]{2,1,0:T(8,128)(2,1)S(1)} collective-permute-done((bf16[4,64,128]{2,1,0:T(8,128)(2,1)S(1)}, bf16[4,64,128]{2,1,0:T(8,128)(2,1)S(1)}, u32[]{:S(2)}, u32[]{:S(2)}) %collective-permute-start.21) | collective-permute-done | bytes 65568 | tf_op jit(solution)/shard_map/ppermute | solution.py:327
  97.3 2.5 %project.1 = bf16[64,2048]{1,0:T(8,128)(2,1)} custom-call(s32[1]{0:T(128)} %bitcast.member_ref, s32[64,1]{1,0:T(8,128)S(1)} %copy.18.pos_ref, bf16[4,64,128]{2,1,0:T(8,128)(2,1)S(1)} %get-tuple-element.46.refs_0_, bf16[4,64,128]{2,1,0:T(8,128)(2,1)S(1)} %collective-permute-done.20.refs_1_, bf16[4,64,128]{2,1,0:T(8,128)(2,1)S(1)} %collective-permute-done.21.refs_2_, ...), custom_call_target="tpu_custom_call" | custom-call | flops 536870912 | bytes 9000000 | tf_op jit(solution)/shard_map/project/pallas_call | solution.py:298
  (20 shorter events, 0.1 us)
Async XLA Ops:
  1.4 11.1 %collective-permute-start = (bf16[392,128]{1,0:T(8,128)(2,1)S(1)}, bf16[392,128]{1,0:T(8,128)(2,1)S(1)}, u32[]{:S(2)}, u32[]{:S(2)}) collective-permute-start(bf16[392,128]{1,0:T(8,128)(2,1)S(1)} %get-tuple-element.42), channel_id=1, source_target_pairs={{0,8},{1,9},{2,10},{3,11},{4,12},{5,13},{6,14},{7,15},{8,16},{9,17... | collective-permute-start | bytes 301064 | tf_op jit(solution)/shard_map/ppermute | solution.py:327
  4.3 11.8 %collective-permute-start.1 = (bf16[392,128]{1,0:T(8,128)(2,1)S(1)}, bf16[392,128]{1,0:T(8,128)(2,1)S(1)}, u32[]{:S(2)}, u32[]{:S(2)}) collective-permute-start(bf16[392,128]{1,0:T(8,128)(2,1)S(1)} %get-tuple-element.41), channel_id=1, source_target_pairs={{0,16},{1,17},{2,18},{3,19},{4,20},{5,21},{6,22},{7,23},{8,24},{9,... | collective-permute-start | bytes 301064 | tf_op jit(solution)/shard_map/ppermute | solution.py:327
  9.3 6.8 %collective-permute-start.2 = (bf16[392,128]{1,0:T(8,128)(2,1)S(1)}, bf16[392,128]{1,0:T(8,128)(2,1)S(1)}, u32[]{:S(2)}, u32[]{:S(2)}) collective-permute-start(bf16[392,128]{1,0:T(8,128)(2,1)S(1)} %get-tuple-element.40), channel_id=1, source_target_pairs={{0,24},{1,25},{2,26},{3,27},{4,28},{5,29},{6,30},{7,31},{8,0},{9,1... | collective-permute-start | bytes 301064 | tf_op jit(solution)/shard_map/ppermute | solution.py:327
  16.2 26.4 %collective-permute-start.3 = (bf16[4,392,128]{2,1,0:T(8,128)(2,1)S(1)}, bf16[4,392,128]{2,1,0:T(8,128)(2,1)S(1)}, u32[]{:S(2)}, u32[]{:S(2)}) collective-permute-start(bf16[4,392,128]{2,1,0:T(8,128)(2,1)S(1)} %pad_maximum_fusion.refs_1_), channel_id=1, source_target_pairs={{0,1},{1,0},{2,3},{3,2},{4,5},{5,4},{6,7},{7,6},{8,9},{9,8},{10,11... | collective-permute-start | bytes 1204232 | tf_op jit(solution)/shard_map/ppermute | solution.py:319
  16.4 21.8 %collective-permute-start.4 = (bf16[4,136,128]{2,1,0:T(8,128)(2,1)S(1)}, bf16[4,136,128]{2,1,0:T(8,128)(2,1)S(1)}, u32[]{:S(2)}, u32[]{:S(2)}) collective-permute-start(bf16[4,136,128]{2,1,0:T(8,128)(2,1)S(1)} %pad_maximum_fusion.1.refs_3_), channel_id=1, source_target_pairs={{0,32},{1,97},{2,34},{3,99},{4,36},{5,101},{6,38},{7,103},{8,40},{... | collective-permute-start | bytes 417800 | tf_op jit(solution)/shard_map/ppermute | solution.py:322
  27.1 17.3 %collective-permute-start.10 = (bf16[4,136,128]{2,1,0:T(8,128)(2,1)S(1)}, bf16[4,136,128]{2,1,0:T(8,128)(2,1)S(1)}, u32[]{:S(2)}, u32[]{:S(2)}) collective-permute-start(bf16[4,136,128]{2,1,0:T(8,128)(2,1)S(1)} %pad_maximum_fusion.1.refs_3_), channel_id=1, source_target_pairs={{0,6},{1,7},{2,0},{3,1},{4,2},{5,3},{6,4},{7,5},{8,14},{9,15},{10,... | collective-permute-start | bytes 417800 | tf_op jit(solution)/shard_map/ppermute | solution.py:319
  30.3 15.8 %collective-permute-start.11 = (bf16[4,136,128]{2,1,0:T(8,128)(2,1)S(1)}, bf16[4,136,128]{2,1,0:T(8,128)(2,1)S(1)}, u32[]{:S(2)}, u32[]{:S(2)}) collective-permute-start(bf16[4,136,128]{2,1,0:T(8,128)(2,1)S(1)} %pad_maximum_fusion.1.refs_3_), channel_id=1, source_target_pairs={{0,4},{1,5},{2,6},{3,7},{4,0},{5,1},{6,2},{7,3},{8,12},{9,13},{10,... | collective-permute-start | bytes 417800 | tf_op jit(solution)/shard_map/ppermute | solution.py:319
  38.2 10.7 %collective-permute-start.5 = (bf16[4,136,128]{2,1,0:T(8,128)(2,1)S(1)}, bf16[4,136,128]{2,1,0:T(8,128)(2,1)S(1)}, u32[]{:S(2)}, u32[]{:S(2)}) collective-permute-start(bf16[4,136,128]{2,1,0:T(8,128)(2,1)S(1)} %collective-permute-done.4.refs_3_), channel_id=1, source_target_pairs={{0,32},{1,97},{2,34},{3,99},{4,36},{5,101},{6,38},{7,103},{8,40},{... | collective-permute-start | bytes 417800 | tf_op jit(solution)/shard_map/ppermute | solution.py:322
  40.3 10.3 %collective-permute-start.9 = (bf16[4,136,128]{2,1,0:T(8,128)(2,1)S(1)}, bf16[4,136,128]{2,1,0:T(8,128)(2,1)S(1)}, u32[]{:S(2)}, u32[]{:S(2)}) collective-permute-start(bf16[4,136,128]{2,1,0:T(8,128)(2,1)S(1)} %pad_maximum_fusion.1.refs_3_), channel_id=1, source_target_pairs={{0,2},{1,3},{2,4},{3,5},{4,6},{5,7},{6,0},{7,1},{8,10},{9,11},{10,... | collective-permute-start | bytes 417800 | tf_op jit(solution)/shard_map/ppermute | solution.py:319
  42.6 15.3 %collective-permute-start.16 = (bf16[4,136,128]{2,1,0:T(8,128)(2,1)S(1)}, bf16[4,136,128]{2,1,0:T(8,128)(2,1)S(1)}, u32[]{:S(2)}, u32[]{:S(2)}) collective-permute-start(bf16[4,136,128]{2,1,0:T(8,128)(2,1)S(1)} %collective-permute-done.4.refs_3_), channel_id=1, source_target_pairs={{0,2},{1,3},{2,4},{3,5},{4,6},{5,7},{6,0},{7,1},{8,10},{9,11},{10,... | collective-permute-start | bytes 417800 | tf_op jit(solution)/shard_map/ppermute | solution.py:319
  44.4 19.6 %collective-permute-start.17 = (bf16[4,136,128]{2,1,0:T(8,128)(2,1)S(1)}, bf16[4,136,128]{2,1,0:T(8,128)(2,1)S(1)}, u32[]{:S(2)}, u32[]{:S(2)}) collective-permute-start(bf16[4,136,128]{2,1,0:T(8,128)(2,1)S(1)} %collective-permute-done.4.refs_3_), channel_id=1, source_target_pairs={{0,6},{1,7},{2,0},{3,1},{4,2},{5,3},{6,4},{7,5},{8,14},{9,15},{10,... | collective-permute-start | bytes 417800 | tf_op jit(solution)/shard_map/ppermute | solution.py:319
  46.1 19.5 %collective-permute-start.18 = (bf16[4,136,128]{2,1,0:T(8,128)(2,1)S(1)}, bf16[4,136,128]{2,1,0:T(8,128)(2,1)S(1)}, u32[]{:S(2)}, u32[]{:S(2)}) collective-permute-start(bf16[4,136,128]{2,1,0:T(8,128)(2,1)S(1)} %collective-permute-done.4.refs_3_), channel_id=1, source_target_pairs={{0,4},{1,5},{2,6},{3,7},{4,0},{5,1},{6,2},{7,3},{8,12},{9,13},{10,... | collective-permute-start | bytes 417800 | tf_op jit(solution)/shard_map/ppermute | solution.py:319
  49.0 27.6 %collective-permute-start.6 = (bf16[4,136,128]{2,1,0:T(8,128)(2,1)S(1)}, bf16[4,136,128]{2,1,0:T(8,128)(2,1)S(1)}, u32[]{:S(2)}, u32[]{:S(2)}) collective-permute-start(bf16[4,136,128]{2,1,0:T(8,128)(2,1)S(1)} %collective-permute-done.5.refs_3_), channel_id=1, source_target_pairs={{0,2},{1,3},{2,4},{3,5},{4,6},{5,7},{6,0},{7,1},{8,10},{9,11},{10,... | collective-permute-start | bytes 417800 | tf_op jit(solution)/shard_map/ppermute | solution.py:319
  50.6 11.8 %collective-permute-start.12 = (bf16[4,136,128]{2,1,0:T(8,128)(2,1)S(1)}, bf16[4,136,128]{2,1,0:T(8,128)(2,1)S(1)}, u32[]{:S(2)}, u32[]{:S(2)}) collective-permute-start(bf16[4,136,128]{2,1,0:T(8,128)(2,1)S(1)} %pad_maximum_fusion.2), channel_id=1, source_target_pairs={{0,32},{1,97},{2,34},{3,99},{4,36},{5,101},{6,38},{7,103},{8,40},{... | collective-permute-start | bytes 417800 | tf_op jit(solution)/shard_map/ppermute | solution.py:322
  57.9 18.6 %collective-permute-start.7 = (bf16[4,136,128]{2,1,0:T(8,128)(2,1)S(1)}, bf16[4,136,128]{2,1,0:T(8,128)(2,1)S(1)}, u32[]{:S(2)}, u32[]{:S(2)}) collective-permute-start(bf16[4,136,128]{2,1,0:T(8,128)(2,1)S(1)} %collective-permute-done.5.refs_3_), channel_id=1, source_target_pairs={{0,6},{1,7},{2,0},{3,1},{4,2},{5,3},{6,4},{7,5},{8,14},{9,15},{10,... | collective-permute-start | bytes 417800 | tf_op jit(solution)/shard_map/ppermute | solution.py:319
  62.3 8.2 %collective-permute-start.13 = (bf16[4,136,128]{2,1,0:T(8,128)(2,1)S(1)}, bf16[4,136,128]{2,1,0:T(8,128)(2,1)S(1)}, u32[]{:S(2)}, u32[]{:S(2)}) collective-permute-start(bf16[4,136,128]{2,1,0:T(8,128)(2,1)S(1)} %collective-permute-done.12.refs_3_), channel_id=1, source_target_pairs={{0,2},{1,3},{2,4},{3,5},{4,6},{5,7},{6,0},{7,1},{8,10},{9,11},{10,... | collective-permute-start | bytes 417800 | tf_op jit(solution)/shard_map/ppermute | solution.py:319
  64.0 8.7 %collective-permute-start.14 = (bf16[4,136,128]{2,1,0:T(8,128)(2,1)S(1)}, bf16[4,136,128]{2,1,0:T(8,128)(2,1)S(1)}, u32[]{:S(2)}, u32[]{:S(2)}) collective-permute-start(bf16[4,136,128]{2,1,0:T(8,128)(2,1)S(1)} %collective-permute-done.12.refs_3_), channel_id=1, source_target_pairs={{0,6},{1,7},{2,0},{3,1},{4,2},{5,3},{6,4},{7,5},{8,14},{9,15},{10,... | collective-permute-start | bytes 417800 | tf_op jit(solution)/shard_map/ppermute | solution.py:319
  65.6 7.7 %collective-permute-start.15 = (bf16[4,136,128]{2,1,0:T(8,128)(2,1)S(1)}, bf16[4,136,128]{2,1,0:T(8,128)(2,1)S(1)}, u32[]{:S(2)}, u32[]{:S(2)}) collective-permute-start(bf16[4,136,128]{2,1,0:T(8,128)(2,1)S(1)} %collective-permute-done.12.refs_3_), channel_id=1, source_target_pairs={{0,4},{1,5},{2,6},{3,7},{4,0},{5,1},{6,2},{7,3},{8,12},{9,13},{10,... | collective-permute-start | bytes 417800 | tf_op jit(solution)/shard_map/ppermute | solution.py:319
  70.6 7.2 %collective-permute-start.8 = (bf16[4,136,128]{2,1,0:T(8,128)(2,1)S(1)}, bf16[4,136,128]{2,1,0:T(8,128)(2,1)S(1)}, u32[]{:S(2)}, u32[]{:S(2)}) collective-permute-start(bf16[4,136,128]{2,1,0:T(8,128)(2,1)S(1)} %collective-permute-done.5.refs_3_), channel_id=1, source_target_pairs={{0,4},{1,5},{2,6},{3,7},{4,0},{5,1},{6,2},{7,3},{8,12},{9,13},{10,... | collective-permute-start | bytes 417800 | tf_op jit(solution)/shard_map/ppermute | solution.py:319
  73.3 7.4 %copy-start.1 = (s32[64]{0:T(128)S(1)}, s32[64]{0:T(128)}, u32[]{:S(2)}) copy-start(s32[64]{0:T(128)} %param.10) | copy-start | bytes 772
  80.5 2.0 %collective-permute-start.19 = (bf16[4,256,256]{2,1,0:T(8,128)(2,1)S(1)}, bf16[4,256,256]{2,1,0:T(8,128)(2,1)S(1)}, u32[]{:S(2)}, u32[]{:S(2)}) collective-permute-start(bf16[4,256,256]{2,1,0:T(8,128)(2,1)S(1)} %get-tuple-element.37), channel_id=1, source_target_pairs={{0,1},{1,0},{2,3},{3,2},{4,5},{5,4},{6,7},{7,6},{8,9},{9,8},{10,11... | collective-permute-start | bytes 1572872 | tf_op jit(solution)/shard_map/ppermute | solution.py:319
  83.2 11.6 %collective-permute-start.20 = (bf16[4,64,128]{2,1,0:T(8,128)(2,1)S(1)}, bf16[4,64,128]{2,1,0:T(8,128)(2,1)S(1)}, u32[]{:S(2)}, u32[]{:S(2)}) collective-permute-start(bf16[4,64,128]{2,1,0:T(8,128)(2,1)S(1)} %get-tuple-element.45), channel_id=1, source_target_pairs={{0,24},{1,25},{2,26},{3,27},{4,28},{5,29},{6,30},{7,31},{8,0},{9,1... | collective-permute-start | bytes 196616 | tf_op jit(solution)/shard_map/ppermute | solution.py:327
  90.7 6.6 %collective-permute-start.21 = (bf16[4,64,128]{2,1,0:T(8,128)(2,1)S(1)}, bf16[4,64,128]{2,1,0:T(8,128)(2,1)S(1)}, u32[]{:S(2)}, u32[]{:S(2)}) collective-permute-start(bf16[4,64,128]{2,1,0:T(8,128)(2,1)S(1)} %get-tuple-element.44), channel_id=1, source_target_pairs={{0,16},{1,17},{2,18},{3,19},{4,20},{5,21},{6,22},{7,23},{8,24},{9,... | collective-permute-start | bytes 196616 | tf_op jit(solution)/shard_map/ppermute | solution.py:327
  90.7 6.6 %copy-start = (bf16[64,2048]{1,0:T(8,128)(2,1)S(1)}, bf16[64,2048]{1,0:T(8,128)(2,1)}, u32[]{:S(2)}) copy-start(bf16[64,2048]{1,0:T(8,128)(2,1)} %refs_5_.1) | copy-start | bytes 786436
  90.7 6.6 %collective-permute-start.22 = (bf16[4,64,128]{2,1,0:T(8,128)(2,1)S(1)}, bf16[4,64,128]{2,1,0:T(8,128)(2,1)S(1)}, u32[]{:S(2)}, u32[]{:S(2)}) collective-permute-start(bf16[4,64,128]{2,1,0:T(8,128)(2,1)S(1)} %get-tuple-element.43), channel_id=1, source_target_pairs={{0,8},{1,9},{2,10},{3,11},{4,12},{5,13},{6,14},{7,15},{8,16},{9,17... | collective-permute-start | bytes 196616 | tf_op jit(solution)/shard_map/ppermute | solution.py:327
